TPU v7x, 1024 devices: a whole 8x8x8 slice. The times are simulated.
1024 devices in a mesh: face: 8 (over y), tx: 32 (over z, x_hi), ty: 4 (over x_lo, core).
Axes of the slice: x: 8 (x_hi: 4, x_lo: 2; x = x_hi * 2 + x_lo), y: 8, z: 8, core: 2. Of those that a mesh axis runs over, the one named last changes fastest.
Arguments:
- probes: float32 [2, 4, 8, 6, 256, 256], P(None, None, 'face', None, 'tx', 'ty'), may hold values from -6 to 6
- background_wind: float32 [2, 8, 6, 256, 256], P(None, 'face', None, 'tx', 'ty'), may hold values from -6 to 6
- layer_mass: float32 [8, 6, 256, 256], P('face', None, 'tx', 'ty'), may hold values from 0.5 to 2
- trajectory_heat_factor: float32 [8, 6, 256, 256], P('face', None, 'tx', 'ty'), may hold values from 0.3 to 3
- spread: float32 [4, 8, 6, 256, 256], P(None, 'face', None, 'tx', 'ty'), may hold values from 0.5 to 2
- inverse_misfit_variance: float32 [4, 8, 6, 256, 256], P(None, 'face', None, 'tx', 'ty'), may hold values from 0.25 to 4
- face_links: int32 [6, 4, 7], replicated, may hold values from -1 to 5, as said below
Outputs:
- applied: float32 [2, 4, 8, 6, 256, 256], P(None, None, 'face', None, 'tx', 'ty')
Inputs may be any that keep to these rules, and one draw needn't show every extreme that they name: `face_links`: the table describes the six panels of a cube, each with a right-handed frame: for panel f and edge e, the panel across it, the edge of that panel which touches f, whether the index along the shared edge runs the other way, and the matrix of entries -1, 0, 1 that carries vector components from that panel's frame into the frame of f.
All inputs are finite; a program needn't handle non-finite values.
Results may differ from a plain program's by a relative error of at most 0.00002.
Values sent between devices are 32-bit elements; how exact they have to be, the bound alone decides.
No kernel may reach another device: no remote copies, remote signals or barrier semaphores. Data moves between devices by JAX's collectives and lax.ppermute only.
A program may use at most 64 MiB of HBM per device.

v0:
```python
import functools

import jax
import jax.numpy as jnp
import numpy as np
from jax import lax
from jax.experimental import pallas as pl
from jax.experimental.pallas import tpu as pltpu
from jax.sharding import PartitionSpec as P

dt = 0.3
PROBES = 2
FORWARD = ("zonal", "meridional", "flux_x", "flux_y", "temp", "geo")
FORWARD_X = {
    "geo": {"geo": (0, 0)},
    "zonal": {"zonal": (1, 0), "meridional": (2, 0)},
    "meridional": {"zonal": (3, 0), "meridional": (4, 0)},
    "flux_x": {"flux_x": (1, 0), "flux_y": (2, 0)},
    "temp": {"temp": (0, 0)},
}
FORWARD_Y = {
    "geo": {"geo": (0, 0)},
    "zonal": {"zonal": (1, 0), "meridional": (2, 0)},
    "meridional": {"zonal": (3, 0), "meridional": (4, 0)},
    "flux_y": {"flux_x": (3, 0), "flux_y": (4, 0)},
    "temp": {"temp": (0, 0)},
}
ADJOINT = ("ez", "em", "nz", "nm", "z", "m", "t", "eh", "nh")
ADJOINT_X = {
    "ez": {"ez": (1, 1), "em": (1, 2), "nz": (2, 1), "nm": (2, 2)},
    "em": {"ez": (1, 3), "em": (1, 4), "nz": (2, 3), "nm": (2, 4)},
    "z": {"z": (1, 0), "m": (2, 0)},
    "t": {"t": (0, 0)},
    "eh": {"eh": (1, 0), "nh": (2, 0)},
}
ADJOINT_Y = {
    "nz": {"ez": (3, 1), "em": (3, 2), "nz": (4, 1), "nm": (4, 2)},
    "nm": {"ez": (3, 3), "em": (3, 4), "nz": (4, 3), "nm": (4, 4)},
    "m": {"z": (3, 0), "m": (4, 0)},
    "t": {"t": (0, 0)},
    "nh": {"eh": (3, 0), "nh": (4, 0)},
}
ROWS = 56
STRIP = 16 + ROWS


def source_index(unit, panel):
    return (panel % 2) * 64 + unit * 3 + panel // 2


def target_index(unit, panel):
    return (panel % 2) * 32 + unit * 3 + panel // 2


def codes_of(sources, x_targets, y_targets):
    codes = np.full((5, 128, 64), -1.0, np.float32)
    for d, targets in enumerate((x_targets, y_targets)):
        for t, (_, terms) in enumerate(targets.items()):
            for name, (i, j) in terms.items():
                s = sources.index(name)
                for probe in range(PROBES):
                    for n in range(6):
                        for f in range(6):
                            r = source_index(s * PROBES + probe, n)
                            c = target_index(t * PROBES + probe, f)
                            codes[2 * d, r, c] = i
                            codes[2 * d + 1, r, c] = j
    for u in range(len(sources) * PROBES):
        for n in range(6):
            codes[4, source_index(u, n), :] = n
    return codes


def picks_of(sources, y_targets):
    picks = np.zeros((128, 64), np.float32)
    for t, name in enumerate(y_targets):
        for probe in range(PROBES):
            for f in range(6):
                picks[
                    source_index(sources.index(name) * PROBES + probe, f),
                    target_index(t * PROBES + probe, f),
                ] = 1.0
    return picks


TABLES = {
    "forward": (FORWARD, FORWARD_X, FORWARD_Y),
    "adjoint": (ADJOINT, ADJOINT_X, ADJOINT_Y),
}


def dot(a, b, contract=(1, 0)):
    return lax.dot_general(
        a,
        b,
        (((contract[0],), (contract[1],)), ((), ())),
        precision=lax.Precision.HIGHEST,
        preferred_element_type=jnp.float32,
    )


def reversal(size):
    row = lax.broadcasted_iota(jnp.int32, (size, size), 0)
    column = lax.broadcasted_iota(jnp.int32, (size, size), 1)
    return (row + column == size - 1).astype(jnp.float32)


def identity(size):
    row = lax.broadcasted_iota(jnp.int32, (size, size), 0)
    column = lax.broadcasted_iota(jnp.int32, (size, size), 1)
    return (row == column).astype(jnp.float32)


def lanes(shape):
    return lax.broadcasted_iota(jnp.int32, shape, len(shape) - 1)


def joined(even, odd):
    return jnp.concatenate([even, odd], axis=1)


def pair(ref, index, pp):
    return joined(ref[(*index, 2 * pp)], ref[(*index, 2 * pp + 1)])


def link_lanes(links, edge, item):
    lane = lanes((1, 64))
    within = jnp.where(lane >= 32, lane - 32, lane)
    third = within - 3 * ((within * 43) // 128)
    out = jnp.zeros((1, 64), jnp.float32)
    for f in range(6):
        value = links[f * 28 + edge * 7 + item].astype(jnp.float32)
        here = (third == f // 2) & ((lane >= 32) == (f % 2 == 1))
        out = jnp.where(here, value, out)
    return out


def coefficients(links, edge, code_a, code_b, panel):
    one = jnp.ones((1, 64), jnp.float32)
    entries = [one] + [link_lanes(links, edge, 3 + k) for k in range(4)]
    a = jnp.zeros(code_a.shape, jnp.float32)
    b = jnp.zeros(code_a.shape, jnp.float32)
    for k in range(5):
        a = jnp.where(code_a == k, entries[k], a)
        b = jnp.where(code_b == k, entries[k], b)
    return jnp.where(panel == link_lanes(links, edge, 0), a * b, 0.0)


def put_strips(planes, out_ref, tile_row):
    lane = lanes((8, 128))
    south = jnp.zeros((8, 128), jnp.float32)
    north = jnp.zeros((8, 128), jnp.float32)
    rows = []
    for a, plane in enumerate(planes):
        here = (lane == a) | (lane == a + 64)
        south = jnp.where(here, plane if a == 0 else pltpu.roll(plane, a, 1), south)
        shift = (a - 63) % 128
        north = jnp.where(here, plane if shift == 0 else pltpu.roll(plane, shift, 1), north)
        rows.append(jnp.where(tile_row == 0, plane[0:1], plane[7:8]))
    out_ref[0:8] = south
    out_ref[8:16] = north
    rows.append(jnp.zeros((ROWS - len(rows), 128), jnp.float32))
    out_ref[16:STRIP] = jnp.concatenate(rows, axis=0)


def put_outer_rows(planes, top_ref, bottom_ref):
    spare = [jnp.zeros((32 - len(planes), 128), jnp.float32)]
    top_ref[...] = jnp.concatenate([p[0:1] for p in planes] + spare, axis=0)
    bottom_ref[...] = jnp.concatenate([p[7:8] for p in planes] + spare, axis=0)


def slopes_x(plane, b, west, east):
    row = lax.broadcasted_iota(jnp.int32, (8, 128), 0)
    after = jnp.where(row == 7, east[b : b + 1], pltpu.roll(plane, 7, 0))
    before = jnp.where(row == 0, west[b : b + 1], pltpu.roll(plane, 1, 0))
    return 0.5 * (after - before)


def slopes_y(plane, b, south, north):
    lane = lanes((8, 128))
    low = (lane == 0) | (lane == 64)
    high = (lane == 63) | (lane == 127)
    from_south = south if b == 0 else pltpu.roll(south, 128 - b, 1)
    after = jnp.where(high, pltpu.roll(north, 63 - b, 1), pltpu.roll(plane, 127, 1))
    before = jnp.where(low, from_south, pltpu.roll(plane, 1, 1))
    return 0.5 * (after - before)


def thickness_kernel(slots, probes, spread, out):
    for probe in range(PROBES):
        for pp in range(3):
            value = pair(spread, (2, 0), pp) * pair(probes, (probe, 2, 0), pp)
            for k in range(slots):
                out[k, (probe * 3 + pp) * 8 : (probe * 3 + pp) * 8 + 8] = value


def fields_kernel(
    level_count, place, probes, spread, wind, mass, heat, totals, fields, strips, top, bottom
):
    level = place[0]
    planes = {}
    for pp in range(3):
        east = pair(wind, (0, 0), pp)
        north = pair(wind, (1, 0), pp)
        mass_here = pair(mass, (0,), pp)
        heat_here = pair(heat, (0,), pp)
        for probe in range(PROBES):
            scaled = [
                pair(spread, (c, 0), pp) * pair(probes, (probe, c, 0), pp) for c in range(4)
            ]
            zonal, meridional, thickness, temp = scaled
            at = (probe * 3 + pp) * 8
            pressure = thickness
            for k in range(level_count - 1):
                pressure = pressure + jnp.where(k < level, totals[k, at : at + 8], 0.0)
            planes["zonal", probe, pp] = zonal
            planes["meridional", probe, pp] = meridional
            planes["flux_x", probe, pp] = east * thickness + mass_here * zonal
            planes["flux_y", probe, pp] = north * thickness + mass_here * meridional
            planes["temp", probe, pp] = temp
            planes["geo", probe, pp] = temp + heat_here * pressure
    ordered = [planes[n, pr, pp] for n in FORWARD for pr in range(PROBES) for pp in range(3)]
    for a, plane in enumerate(ordered):
        fields[a] = plane
    put_strips(ordered, strips, place[1])
    put_outer_rows(
        [planes[n, pr, pp] for n in FORWARD_X for pr in range(PROBES) for pp in range(3)],
        top,
        bottom,
    )


def route_kernel(
    nt, nq, place, links, gathered, top, bottom, codes, picks, slots, swap_a, swap_b, local, halos
):
    tile_row, tile_column = place[1], place[2]
    is_first, is_last = tile_row == 0, tile_row == nt - 1
    line = jnp.where(is_first, 0, 1)
    line_f = line.astype(jnp.float32)
    column_edge = jnp.where(tile_column == 0, 2, 3)
    panel = codes[4]
    c0 = coefficients(links, 0, codes[0], codes[1], panel)
    c1 = coefficients(links, 1, codes[0], codes[1], panel)
    cc = coefficients(links, column_edge, codes[2], codes[3], panel)

    def masks(edge, source):
        far = link_lanes(links, edge, 1)
        flip = link_lanes(links, edge, 2)
        here = far == source
        return (
            jnp.where(here & (flip != 1.0), 1.0, 0.0),
            jnp.where(here & (flip == 1.0), 1.0, 0.0),
        )

    back64 = reversal(64)
    empty = jnp.zeros((64 - ROWS, 64), jnp.float32)

    def segment(q):
        packed = gathered[q, 16:STRIP]
        return jnp.concatenate([packed[:, 0:64], empty, packed[:, 64:128], empty], axis=0)

    on_boundary = jnp.where(is_first | is_last, 1.0, 0.0)
    plain_c, turned_c = masks(column_edge, line_f)
    across = [dot(segment(q), cc, (0, 0)) for q in range(nq)]
    pieces = []
    for q in range(nq):
        pieces.append(
            on_boundary
            * (across[q] * plain_c + dot(back64, across[nq - 1 - q] * turned_c))
        )
    low_column, high_column = gathered[0, 0:8], gathered[nq - 1, 8:16]
    low_plain, low_turned = masks(column_edge, 2.0)
    high_plain, high_turned = masks(column_edge, 3.0)
    low_c, high_c = dot(low_column, cc), dot(high_column, cc)
    straight = low_c * low_plain + high_c * high_plain
    flipped = dot(reversal(8), low_c * low_turned + high_c * high_turned)
    to_rows = []
    for edge, c in ((0, c0), (1, c1)):
        far = link_lanes(links, edge, 1)
        to_rows.append(
            dot(low_column, c) * jnp.where(far == 2.0, 1.0, 0.0)
            + dot(high_column, c) * jnp.where(far == 3.0, 1.0, 0.0)
        )
    for t in range(nt):
        q, at = t // 8, (t % 8) * 8
        left = pieces[q][at : at + 8]
        left = left + jnp.where(tile_row == t, straight, 0.0)
        left = left + jnp.where(tile_row == nt - 1 - t, flipped, 0.0)
        slots[t] = joined(left, to_rows[1] if t == nt - 1 else to_rows[0])

    mine, mirrored = gathered[tile_column, 16:STRIP], gathered[nq - 1 - tile_column, 16:STRIP]
    mine = jnp.concatenate([mine[:, 0:64], empty, mine[:, 64:128], empty], axis=0)
    mirrored = jnp.concatenate([mirrored[:, 0:64], empty, mirrored[:, 64:128], empty], axis=0)
    by_row = []
    for edge, c in ((0, c0), (1, c1)):
        plain, turned = masks(edge, line_f)
        by_row.append(
            dot(c * plain, mine, (0, 0)) + dot(dot(c * turned, mirrored, (0, 0)), back64)
        )
    by_row = [joined(z[0:32], z[32:64]) for z in by_row]
    local[...] = jnp.where(is_first, by_row[0], by_row[1])
    to_lower = jnp.where(is_first, by_row[1], top[...])
    to_upper = jnp.where(is_last, by_row[0], bottom[...])
    even = lax.rem(tile_row, 2) == 0
    swap_a[...] = jnp.where(even, to_upper, to_lower)
    swap_b[...] = jnp.where(even, to_lower, to_upper)

    below = gathered[jnp.maximum(tile_column - 1, 0), 8:16]
    above = gathered[jnp.minimum(tile_column + 1, nq - 1), 0:8]
    halos[0:8] = jnp.where(tile_column > 0, dot(below, picks[...]), 0.0)
    halos[8:16] = jnp.where(tile_column < nq - 1, dot(above, picks[...]), 0.0)


def outer_values(nt, nq, place, links, arrived, swapped_a, swapped_b, local, halos):
    tile_row, tile_column = place[1], place[2]
    is_first, is_last = tile_row == 0, tile_row == nt - 1
    column = arrived[0]
    for t in range(1, nt):
        column = column + arrived[t]
    column = column[:, 0:64]
    south = halos[0:8] + jnp.where(tile_column == 0, column, 0.0)
    north = halos[8:16] + jnp.where(tile_column == nq - 1, column, 0.0)
    lane = lanes((8, 128))

    def spread_out(narrow):
        wide = joined(narrow, narrow)
        return jnp.where(lane < 32, wide, pltpu.roll(wide, 32, 1))

    mine = arrived[pl.ds(tile_column * 8, 8)].reshape(64, 128)[:, 64:128]
    mirrored = arrived[pl.ds((nq - 1 - tile_column) * 8, 8)].reshape(64, 128)[:, 64:128]
    flip = link_lanes(links, jnp.where(is_first, 0, 1), 2)
    row = dot(jnp.where(flip != 1.0, mine, 0.0), identity(64), (0, 0)) + dot(
        jnp.where(flip == 1.0, mirrored, 0.0), reversal(64), (0, 0)
    )
    row = joined(row[0:32], row[32:64]) + local[...]
    even = lax.rem(tile_row, 2) == 0
    west = jnp.where(even, swapped_b[...], swapped_a[...]) + jnp.where(is_first, row, 0.0)
    east = jnp.where(even, swapped_a[...], swapped_b[...]) + jnp.where(is_last, row, 0.0)
    return west, east, spread_out(south), spread_out(north)


def image_kernel(
    nt,
    nq,
    place,
    links,
    arrived,
    swapped_a,
    swapped_b,
    local,
    halos,
    fields,
    probes,
    spread,
    wind,
    misfit,
    costs,
    strips,
    top,
    bottom,
):
    west, east, south, north = outer_values(
        nt, nq, place, links, arrived, swapped_a, swapped_b, local, halos
    )
    planes = {}
    for pp in range(3):
        u = pair(wind, (0, 0), pp)
        v = pair(wind, (1, 0), pp)
        for probe in range(PROBES):
            field = lambda n: fields[(FORWARD.index(n) * PROBES + probe) * 3 + pp]
            at = lambda n, t: (list(t).index(n) * PROBES + probe) * 3 + pp
            dx = {n: slopes_x(field(n), at(n, FORWARD_X), west, east) for n in FORWARD_X}
            dy = {n: slopes_y(field(n), at(n, FORWARD_Y), south, north) for n in FORWARD_Y}
            thickness = pair(spread, (2, 0), pp) * pair(probes, (probe, 2, 0), pp)
            z = field("zonal") - dt * (dx["geo"] + u * dx["zonal"] + v * dy["zonal"])
            m = field("meridional") - dt * (
                dy["geo"] + u * dx["meridional"] + v * dy["meridional"]
            )
            t = thickness - dt * (dx["flux_x"] + dy["flux_y"])
            h = field("temp") - dt * (u * dx["temp"] + v * dy["temp"])
            z, m, t, h = (pair(misfit, (c, 0), pp) * w for c, w in enumerate((z, m, t, h)))
            for c, w in enumerate((z, m, t, h)):
                costs[(c * PROBES + probe) * 3 + pp] = w
            made = (u * z, u * m, v * z, v * m, z, m, t, u * h, v * h)
            for n, w in zip(ADJOINT, made):
                planes[n, probe, pp] = w
    put_strips(
        [planes[n, pr, pp] for n in ADJOINT for pr in range(PROBES) for pp in range(3)],
        strips,
        place[1],
    )
    put_outer_rows(
        [planes[n, pr, pp] for n in ADJOINT_X for pr in range(PROBES) for pp in range(3)],
        top,
        bottom,
    )


def adjoint_kernel(
    nt,
    nq,
    levels,
    place,
    links,
    arrived,
    swapped_a,
    swapped_b,
    local,
    halos,
    costs,
    wind,
    mass,
    heat,
    backs,
    loads,
):
    west, east, south, north = outer_values(
        nt, nq, place, links, arrived, swapped_a, swapped_b, local, halos
    )
    for pp in range(3):
        u = pair(wind, (0, 0), pp)
        v = pair(wind, (1, 0), pp)
        mass_here = pair(mass, (0,), pp)
        heat_here = pair(heat, (0,), pp)
        for probe in range(PROBES):
            z, m, t, h = (costs[(c * PROBES + probe) * 3 + pp] for c in range(4))
            field = dict(
                zip(ADJOINT, (u * z, u * m, v * z, v * m, z, m, t, u * h, v * h))
            )
            at = lambda n, k: (list(k).index(n) * PROBES + probe) * 3 + pp
            dx = {n: slopes_x(field[n], at(n, ADJOINT_X), west, east) for n in ADJOINT_X}
            dy = {n: slopes_y(field[n], at(n, ADJOINT_Y), south, north) for n in ADJOINT_Y}
            geo_back = dt * (dx["z"] + dy["m"])
            flux_x_back = dt * dx["t"]
            flux_y_back = dt * dy["t"]
            out = (
                z + dt * (dx["ez"] + dy["nz"]) + mass_here * flux_x_back,
                m + dt * (dx["em"] + dy["nm"]) + mass_here * flux_y_back,
                t + u * flux_x_back + v * flux_y_back,
                h + dt * (dx["eh"] + dy["nh"]) + geo_back,
            )
            for c, w in enumerate(out):
                backs[(c * PROBES + probe) * 3 + pp] = w
            load = heat_here * geo_back
            for k in range(levels):
                loads[k, (probe * 3 + pp) * 8 : (probe * 3 + pp) * 8 + 8] = load


def final_kernel(level_count, place, probes, spread, backs, loads, out):
    level = place[0]
    for probe in range(PROBES):
        for pp in range(3):
            at = (probe * 3 + pp) * 8
            load = jnp.zeros((8, 128), jnp.float32)
            for k in range(level_count):
                load = load + jnp.where(k >= level, loads[k, at : at + 8], 0.0)
            for c in range(4):
                back = backs[(c * PROBES + probe) * 3 + pp]
                if c == 2:
                    back = back + load
                for side in range(2):
                    part = back[:, 64 * side : 64 * side + 64]
                    p = 2 * pp + side
                    out[probe, c, 0, p] = probes[probe, c, 0, p] + spread[c, 0, p] * part


SMEM = pl.BlockSpec(memory_space=pltpu.SMEM)
VMEM = pl.BlockSpec(memory_space=pltpu.VMEM)
INTERPRET = False


def call(kernel, name, small, operands, shapes):
    shapes = [jax.ShapeDtypeStruct(s, jnp.float32) for s in shapes]
    return pl.pallas_call(
        kernel,
        name=name,
        out_shape=shapes,
        in_specs=[SMEM] * len(small) + [VMEM] * len(operands),
        out_specs=[VMEM] * len(shapes),
        interpret=INTERPRET,
    )(*small, *operands)


def exchange(kind, nt, nq, place, links, strips, top, bottom):
    sources, x_targets, y_targets = TABLES[kind]
    codes = jnp.asarray(codes_of(sources, x_targets, y_targets))
    picks = jnp.asarray(picks_of(sources, y_targets))
    gathered = lax.all_gather(strips, "ty", axis=0)
    slots, swap_a, swap_b, local, halos = call(
        functools.partial(route_kernel, nt, nq),
        "route_" + kind,
        (place, links),
        (gathered, top, bottom, codes, picks),
        ((nt, 8, 128), (32, 128), (32, 128), (32, 128), (16, 64)),
    )
    near = [(i, i ^ 1) for i in range(nt)]
    wrapped = [(i, (i + 1 if i % 2 else i - 1) % nt) for i in range(nt)]
    swapped_a = lax.ppermute(swap_a, "tx", near)
    swapped_b = lax.ppermute(swap_b, "tx", wrapped)
    arrived = lax.all_to_all(slots, "tx", 0, 0, tiled=True)
    return arrived, swapped_a, swapped_b, local, halos


def body(probes, wind, mass, heat, spread, misfit, face_links):
    nf, nt, nq = (lax.axis_size(a) for a in ("face", "tx", "ty"))
    links = face_links.reshape(-1)
    index = lax.broadcasted_iota(jnp.int32, (3,), 0)
    place = jnp.where(
        index == 0,
        lax.axis_index("face"),
        jnp.where(index == 1, lax.axis_index("tx"), lax.axis_index("ty")),
    )
    (sent,) = call(
        functools.partial(thickness_kernel, nf),
        "thickness",
        (),
        (probes, spread),
        ((nf, 48, 128),),
    )
    totals = lax.all_to_all(sent, "face", 0, 0, tiled=True)
    fields, strips, top, bottom = call(
        functools.partial(fields_kernel, nf),
        "fields",
        (place,),
        (probes, spread, wind, mass, heat, totals),
        ((36, 8, 128), (STRIP, 128), (32, 128), (32, 128)),
    )
    outer = exchange("forward", nt, nq, place, links, strips, top, bottom)
    costs, strips, top, bottom = call(
        functools.partial(image_kernel, nt, nq),
        "image",
        (place, links),
        (*outer, fields, probes, spread, wind, misfit),
        ((24, 8, 128), (STRIP, 128), (32, 128), (32, 128)),
    )
    outer = exchange("adjoint", nt, nq, place, links, strips, top, bottom)
    backs, loads = call(
        functools.partial(adjoint_kernel, nt, nq, nf),
        "adjoint",
        (place, links),
        (*outer, costs, wind, mass, heat),
        ((24, 8, 128), (nf, 48, 128)),
    )
    loads = lax.all_to_all(loads, "face", 0, 0, tiled=True)
    (applied,) = call(
        functools.partial(final_kernel, nf),
        "final",
        (place,),
        (probes, spread, backs, loads),
        (probes.shape,),
    )
    return applied


def solution(mesh):
    return jax.shard_map(
        body,
        mesh=mesh,
        in_specs=(
            P(None, None, "face", None, "tx", "ty"),
            P(None, "face", None, "tx", "ty"),
            P("face", None, "tx", "ty"),
            P("face", None, "tx", "ty"),
            P(None, "face", None, "tx", "ty"),
            P(None, "face", None, "tx", "ty"),
            P(),
        ),
        out_specs=P(None, None, "face", None, "tx", "ty"),
        check_vma=False,
    )
```

profile of v0, /device:TPU:2, one launch (start us, length us, event | category | flops | bytes accessed | tf_op | source)
XLA Modules:
  0.0 123.1 jit_solution(4662201363598574010)
XLA Ops:
  0.0 1.8 %thickness.1 = f32[8,48,128]{2,1,0:T(8,128)} custom-call(f32[2,4,1,6,8,64]{5,4,3,2,1,0:T(8,128)} %probes.7, f32[4,1,6,8,64]{4,3,2,1,0:T(8,128)} %spread.7), custom_call_target="tpu_custom_call" | custom-call | tf_op jit(solution)/shard_map/thickness/pallas_call | solution.py:474
  1.8 7.6 %all-to-all-start = ((f32[8,48,128]{2,1,0:T(8,128)}), f32[8,48,128]{2,1,0:T(8,128)S(1)}, u32[]{:S(2)}, u32[]{:S(2)}) async-start(f32[8,48,128]{2,1,0:T(8,128)} %thickness.1), calls=%async_computation | async-start | bytes 393216 | tf_op jit(solution)/shard_map/all_to_all | solution.py:520
  9.3 0.0 copy-start.7
  9.3 0.7 copy-done.7
  10.0 0.7 reshape.3.links
  10.7 0.5 compare_select_fusion.1.place
  11.2 8.6 %all-to-all-done.totals = f32[8,48,128]{2,1,0:T(8,128)S(1)} async-done(((f32[8,48,128]{2,1,0:T(8,128)}), f32[8,48,128]{2,1,0:T(8,128)S(1)}, u32[]{:S(2)}, u32[]{:S(2)}) %all-to-all-start) | async-done | bytes 196640 | tf_op jit(solution)/shard_map/all_to_all | solution.py:520
  19.8 0.0 copy-start
  19.8 0.7 copy-done
  20.5 2.0 %fields.1 = (f32[36,8,128]{2,1,0:T(8,128)}, f32[72,128]{1,0:T(8,128)}, f32[32,128]{1,0:T(8,128)}, f32[32,128]{1,0:T(8,128)}) custom-call(s32[3]{0:T(128)} %compare_select_fusion.1.place, f32[2,4,1,6,8,64]{5,4,3,2,1,0:T(8,128)} %probes.7, f32[4,1,6,8,64]{4,3,2,1,0:T(8,128)} %spread.7, f32[2,1,6,8,64]{4,3,2,1,0:T(8,128)} %wind.5, f32[1,6,8,64]{3,2,1,0:T(8,128)} %mass.3, ...), custom_call_target="tpu_custom_call" | custom-call | tf_op jit(solution)/shard_map/fields/pallas_call | solution.py:474
  22.5 13.7 %all-gather = f32[288,128]{1,0:T(8,128)} all-gather(f32[72,128]{1,0:T(8,128)} %get-tuple-element.25), channel_id=2, replica_groups=mesh['face'=8,'tx'=32,'ty'=4] {'ty'}, dimensions={0}, use_global_device_ids=true | all-gather | bytes 184320 | tf_op jit(solution)/shard_map/all_gather | solution.py:488
  36.1 3.3 %route_forward.1 = (f32[32,8,128]{2,1,0:T(8,128)}, f32[32,128]{1,0:T(8,128)}, f32[32,128]{1,0:T(8,128)}, f32[32,128]{1,0:T(8,128)}, f32[16,64]{1,0:T(8,128)}) custom-call(s32[3]{0:T(128)} %compare_select_fusion.1.place, s32[168]{0:T(256)} %reshape.3.links, f32[4,72,128]{2,1,0:T(8,128)} %bitcast.2, f32[32,128]{1,0:T(8,128)} %get-tuple-element.26.top, ...), custom_call_target="tpu_custom_call" | custom-call | tf_op jit(solution)/shard_map/route_forward/pallas_call | solution.py:474
  39.5 0.0 copy-start.10
  39.5 0.0 copy-start.8
  39.5 14.5 %all-to-all-start.1 = ((f32[32,8,128]{2,1,0:T(8,128)}), f32[32,8,128]{2,1,0:T(8,128)S(1)}, u32[]{:S(2)}, u32[]{:S(2)}) async-start(f32[32,8,128]{2,1,0:T(8,128)} %get-tuple-element.28), calls=%async_computation.1 | async-start | bytes 262144 | tf_op jit(solution)/shard_map/all_to_all | solution.py:500
  53.9 0.0 copy-done.10
  53.9 4.6 %collective-permute-start = (f32[32,128]{1,0:T(8,128)S(1)}, f32[32,128]{1,0:T(8,128)S(1)}, u32[]{:S(2)}, u32[]{:S(2)}) collective-permute-start(f32[32,128]{1,0:T(8,128)S(1)} %copy-done.10), channel_id=1, source_target_pairs={{0,4},{4,0},{8,12},{12,8},{16,20},{20,16},{24,28},{28,24},{32,36},... | collective-permute-start | bytes 49160 | tf_op jit(solution)/shard_map/ppermute | solution.py:498
  58.6 0.0 copy-done.8
  58.6 7.7 %collective-permute-start.1 = (f32[32,128]{1,0:T(8,128)S(1)}, f32[32,128]{1,0:T(8,128)S(1)}, u32[]{:S(2)}, u32[]{:S(2)}) collective-permute-start(f32[32,128]{1,0:T(8,128)S(1)} %copy-done.8), channel_id=1, source_target_pairs={{0,124},{4,8},{8,4},{12,16},{16,12},{20,24},{24,20},{28,32},{32,28... | collective-permute-start | bytes 49160 | tf_op jit(solution)/shard_map/ppermute | solution.py:499
  66.2 0.0 collective-permute-done.swapped_a
  66.3 0.0 copy-start.3
  66.3 2.2 %collective-permute-done.1.swapped_b = f32[32,128]{1,0:T(8,128)S(1)} collective-permute-done((f32[32,128]{1,0:T(8,128)S(1)}, f32[32,128]{1,0:T(8,128)S(1)}, u32[]{:S(2)}, u32[]{:S(2)}) %collective-permute-start.1) | collective-permute-done | bytes 16416 | tf_op jit(solution)/shard_map/ppermute | solution.py:499
  68.4 0.0 copy-start.5
  68.4 0.0 all-to-all-done.1.arrived
  68.4 0.0 copy-start.2
  68.4 0.0 copy-done.3
  68.4 0.6 copy-done.5
  69.0 0.1 copy-done.2
  69.1 2.5 %image.1 = (f32[24,8,128]{2,1,0:T(8,128)}, f32[72,128]{1,0:T(8,128)}, f32[32,128]{1,0:T(8,128)}, f32[32,128]{1,0:T(8,128)}) custom-call(s32[3]{0:T(128)} %compare_select_fusion.1.place, s32[168]{0:T(256)} %reshape.3.links, f32[32,8,128]{2,1,0:T(8,128)} %copy-done.2, f32[32,128]{1,0:T(8,128)} %copy-done.3, f32[32,128]{1,0:T(8,128)} %copy-done.5, ...), custom_call_target="tpu_custom_call" | custom-call | tf_op jit(solution)/shard_map/image/pallas_call | solution.py:474
  71.6 6.2 %all-gather.1 = f32[288,128]{1,0:T(8,128)} all-gather(f32[72,128]{1,0:T(8,128)} %get-tuple-element.34), channel_id=3, replica_groups=mesh['face'=8,'tx'=32,'ty'=4] {'ty'}, dimensions={0}, use_global_device_ids=true | all-gather | bytes 184320 | tf_op jit(solution)/shard_map/all_gather | solution.py:488
  77.8 3.3 %route_adjoint.1 = (f32[32,8,128]{2,1,0:T(8,128)}, f32[32,128]{1,0:T(8,128)}, f32[32,128]{1,0:T(8,128)}, f32[32,128]{1,0:T(8,128)}, f32[16,64]{1,0:T(8,128)}) custom-call(s32[3]{0:T(128)} %compare_select_fusion.1.place, s32[168]{0:T(256)} %reshape.3.links, f32[4,72,128]{2,1,0:T(8,128)} %bitcast.3, f32[32,128]{1,0:T(8,128)} %get-tuple-element.35.top, ...), custom_call_target="tpu_custom_call" | custom-call | tf_op jit(solution)/shard_map/route_adjoint/pallas_call | solution.py:474
  81.1 0.0 copy-start.11
  81.1 0.0 copy-start.9
  81.1 8.9 %all-to-all-start.2 = ((f32[32,8,128]{2,1,0:T(8,128)}), f32[32,8,128]{2,1,0:T(8,128)S(1)}, u32[]{:S(2)}, u32[]{:S(2)}) async-start(f32[32,8,128]{2,1,0:T(8,128)} %get-tuple-element.37), calls=%async_computation.2 | async-start | bytes 262144 | tf_op jit(solution)/shard_map/all_to_all | solution.py:500
  90.0 0.0 copy-done.11
  90.0 4.6 %collective-permute-start.2 = (f32[32,128]{1,0:T(8,128)S(1)}, f32[32,128]{1,0:T(8,128)S(1)}, u32[]{:S(2)}, u32[]{:S(2)}) collective-permute-start(f32[32,128]{1,0:T(8,128)S(1)} %copy-done.11), channel_id=1, source_target_pairs={{0,4},{4,0},{8,12},{12,8},{16,20},{20,16},{24,28},{28,24},{32,36},... | collective-permute-start | bytes 49160 | tf_op jit(solution)/shard_map/ppermute | solution.py:498
  94.6 0.0 copy-done.9
  94.6 7.7 %collective-permute-start.3 = (f32[32,128]{1,0:T(8,128)S(1)}, f32[32,128]{1,0:T(8,128)S(1)}, u32[]{:S(2)}, u32[]{:S(2)}) collective-permute-start(f32[32,128]{1,0:T(8,128)S(1)} %copy-done.9), channel_id=1, source_target_pairs={{0,124},{4,8},{8,4},{12,16},{16,12},{20,24},{24,20},{28,32},{32,28... | collective-permute-start | bytes 49160 | tf_op jit(solution)/shard_map/ppermute | solution.py:499
  102.3 0.0 collective-permute-done.2.swapped_a
  102.3 0.0 copy-start.4
  102.4 2.1 %collective-permute-done.3.swapped_b = f32[32,128]{1,0:T(8,128)S(1)} collective-permute-done((f32[32,128]{1,0:T(8,128)S(1)}, f32[32,128]{1,0:T(8,128)S(1)}, u32[]{:S(2)}, u32[]{:S(2)}) %collective-permute-start.3) | collective-permute-done | bytes 16416 | tf_op jit(solution)/shard_map/ppermute | solution.py:499
  104.5 0.0 copy-start.6
  104.5 0.0 all-to-all-done.2.arrived
  104.5 0.0 copy-start.1
  104.5 0.0 copy-done.4
  104.5 0.6 copy-done.6
  105.1 0.1 copy-done.1
  105.2 2.3 %adjoint.1 = (f32[24,8,128]{2,1,0:T(8,128)}, f32[8,48,128]{2,1,0:T(8,128)}) custom-call(s32[3]{0:T(128)} %compare_select_fusion.1.place, s32[168]{0:T(256)} %reshape.3.links, f32[32,8,128]{2,1,0:T(8,128)} %copy-done.1, f32[32,128]{1,0:T(8,128)} %copy-done.4, f32[32,128]{1,0:T(8,128)} %copy-done.6, f32[32,128]{1,0:T(8,128)} %get-tuple-element.40.local, ...), custom_call_target="tpu_custom_call" | custom-call | tf_op jit(solution)/shard_map/adjoint/pallas_call | solution.py:474
  107.4 13.8 %all_to_all.20.loads = f32[8,48,128]{2,1,0:T(8,128)} all-to-all(f32[8,48,128]{2,1,0:T(8,128)} %get-tuple-element.44), channel_id=1, replica_groups=mesh['face'=8,'tx'=32,'ty'=4] {'face'}, dimensions={0} | all-to-all | bytes 393216 | tf_op jit(solution)/shard_map/all_to_all | solution.py:544
  121.2 1.9 %final.1 = f32[2,4,1,6,8,64]{5,4,3,2,1,0:T(8,128)} custom-call(s32[3]{0:T(128)} %compare_select_fusion.1.place, f32[2,4,1,6,8,64]{5,4,3,2,1,0:T(8,128)} %probes.7, f32[4,1,6,8,64]{4,3,2,1,0:T(8,128)} %spread.7, f32[24,8,128]{2,1,0:T(8,128)} %get-tuple-element.43.backs, f32[8,48,128]{2,1,0:T(8,128)} %all_to_all.20.loads), custom_call_target="tpu_custom_call" | custom-call | tf_op jit(solution)/shard_map/final/pallas_call | solution.py:474
Async XLA Ops:
  1.8 18.0 %all-to-all-start = ((f32[8,48,128]{2,1,0:T(8,128)}), f32[8,48,128]{2,1,0:T(8,128)S(1)}, u32[]{:S(2)}, u32[]{:S(2)}) async-start(f32[8,48,128]{2,1,0:T(8,128)} %thickness.1), calls=%async_computation | async-start | bytes 393216 | tf_op jit(solution)/shard_map/all_to_all | solution.py:520
  9.3 0.7 copy-start.7
  19.8 0.7 copy-start
  39.5 14.5 %copy-start.10 = (f32[32,128]{1,0:T(8,128)S(1)}, f32[32,128]{1,0:T(8,128)}, u32[]{:S(2)}) copy-start(f32[32,128]{1,0:T(8,128)} %get-tuple-element.29) | copy-start | bytes 49156
  39.5 19.1 %copy-start.8 = (f32[32,128]{1,0:T(8,128)S(1)}, f32[32,128]{1,0:T(8,128)}, u32[]{:S(2)}) copy-start(f32[32,128]{1,0:T(8,128)} %get-tuple-element.30) | copy-start | bytes 49156
  39.5 29.0 %all-to-all-start.1 = ((f32[32,8,128]{2,1,0:T(8,128)}), f32[32,8,128]{2,1,0:T(8,128)S(1)}, u32[]{:S(2)}, u32[]{:S(2)}) async-start(f32[32,8,128]{2,1,0:T(8,128)} %get-tuple-element.28), calls=%async_computation.1 | async-start | bytes 262144 | tf_op jit(solution)/shard_map/all_to_all | solution.py:500
  53.9 12.3 %collective-permute-start = (f32[32,128]{1,0:T(8,128)S(1)}, f32[32,128]{1,0:T(8,128)S(1)}, u32[]{:S(2)}, u32[]{:S(2)}) collective-permute-start(f32[32,128]{1,0:T(8,128)S(1)} %copy-done.10), channel_id=1, source_target_pairs={{0,4},{4,0},{8,12},{12,8},{16,20},{20,16},{24,28},{28,24},{32,36},... | collective-permute-start | bytes 49160 | tf_op jit(solution)/shard_map/ppermute | solution.py:498
  58.6 9.9 %collective-permute-start.1 = (f32[32,128]{1,0:T(8,128)S(1)}, f32[32,128]{1,0:T(8,128)S(1)}, u32[]{:S(2)}, u32[]{:S(2)}) collective-permute-start(f32[32,128]{1,0:T(8,128)S(1)} %copy-done.8), channel_id=1, source_target_pairs={{0,124},{4,8},{8,4},{12,16},{16,12},{20,24},{24,20},{28,32},{32,28... | collective-permute-start | bytes 49160 | tf_op jit(solution)/shard_map/ppermute | solution.py:499
  66.3 2.2 %copy-start.3 = (f32[32,128]{1,0:T(8,128)}, f32[32,128]{1,0:T(8,128)S(1)}, u32[]{:S(2)}) copy-start(f32[32,128]{1,0:T(8,128)S(1)} %collective-permute-done.swapped_a) | copy-start | bytes 49156
  68.4 0.6 copy-start.5
  68.4 0.7 copy-start.2
  81.1 8.9 %copy-start.11 = (f32[32,128]{1,0:T(8,128)S(1)}, f32[32,128]{1,0:T(8,128)}, u32[]{:S(2)}) copy-start(f32[32,128]{1,0:T(8,128)} %get-tuple-element.38) | copy-start | bytes 49156
  81.1 13.5 %copy-start.9 = (f32[32,128]{1,0:T(8,128)S(1)}, f32[32,128]{1,0:T(8,128)}, u32[]{:S(2)}) copy-start(f32[32,128]{1,0:T(8,128)} %get-tuple-element.39) | copy-start | bytes 49156
  81.1 23.4 %all-to-all-start.2 = ((f32[32,8,128]{2,1,0:T(8,128)}), f32[32,8,128]{2,1,0:T(8,128)S(1)}, u32[]{:S(2)}, u32[]{:S(2)}) async-start(f32[32,8,128]{2,1,0:T(8,128)} %get-tuple-element.37), calls=%async_computation.2 | async-start | bytes 262144 | tf_op jit(solution)/shard_map/all_to_all | solution.py:500
  90.0 12.3 %collective-permute-start.2 = (f32[32,128]{1,0:T(8,128)S(1)}, f32[32,128]{1,0:T(8,128)S(1)}, u32[]{:S(2)}, u32[]{:S(2)}) collective-permute-start(f32[32,128]{1,0:T(8,128)S(1)} %copy-done.11), channel_id=1, source_target_pairs={{0,4},{4,0},{8,12},{12,8},{16,20},{20,16},{24,28},{28,24},{32,36},... | collective-permute-start | bytes 49160 | tf_op jit(solution)/shard_map/ppermute | solution.py:498
  94.6 9.9 %collective-permute-start.3 = (f32[32,128]{1,0:T(8,128)S(1)}, f32[32,128]{1,0:T(8,128)S(1)}, u32[]{:S(2)}, u32[]{:S(2)}) collective-permute-start(f32[32,128]{1,0:T(8,128)S(1)} %copy-done.9), channel_id=1, source_target_pairs={{0,124},{4,8},{8,4},{12,16},{16,12},{20,24},{24,20},{28,32},{32,28... | collective-permute-start | bytes 49160 | tf_op jit(solution)/shard_map/ppermute | solution.py:499
  102.3 2.2 %copy-start.4 = (f32[32,128]{1,0:T(8,128)}, f32[32,128]{1,0:T(8,128)S(1)}, u32[]{:S(2)}) copy-start(f32[32,128]{1,0:T(8,128)S(1)} %collective-permute-done.2.swapped_a) | copy-start | bytes 49156
  104.5 0.6 copy-start.6
  104.5 0.7 copy-start.1
where the time goes:
time: 124 us; the launch traced here: 123 us
  starting transfers between devices  55.5 us (45%)
  blocking collectives  33.6 us (27%)
  Pallas kernels  17.1 us (14%)
  waiting for transfers between devices  12.9 us (10%)
  local copies, waits for them, and re-layouts  3.37 us (3%)
    all_to_all x2, starting transfers between devices, exchange(): arrived = lax.all_to_all(slots, 'tx', 0, 0, tiled=True)  23.4 us
    all_gather x2, blocking collectives, exchange(): gathered = lax.all_gather(strips, 'ty', axis=0)  19.8 us
    pallas_call x7, Pallas kernels, call(): pl.pallas_call(kernel, name=name, out_shape=shapes, in_specs=[SMEM] * len...  17.1 us
    ppermute x2, starting transfers between devices, exchange(): swapped_b = lax.ppermute(swap_b, 'tx', wrapped)  15.4 us
    all_to_all x1, blocking collectives, body(): loads = lax.all_to_all(loads, 'face', 0, 0, tiled=True)  13.8 us
    ppermute x2, starting transfers between devices, exchange(): swapped_a = lax.ppermute(swap_a, 'tx', near)  9.19 us
    all_to_all x1, waiting for transfers between devices, body(): totals = lax.all_to_all(sent, 'face', 0, 0, tiled=True)  8.55 us
    all_to_all x1, starting transfers between devices, body(): totals = lax.all_to_all(sent, 'face', 0, 0, tiled=True)  7.56 us
  transfers between devices with their start and end apart: 7, of which 3 were waited for; matrix products, arithmetic and copies ran while one was open for 1% of the time, Pallas kernels for 0%

commit v1 on v0

--- a/solution.py
+++ b/solution.py
@@ -467,16 +467,17 @@
 SMEM = pl.BlockSpec(memory_space=pltpu.SMEM)
 VMEM = pl.BlockSpec(memory_space=pltpu.VMEM)
 INTERPRET = False
-
-
-def call(kernel, name, small, operands, shapes):
+GRANT = 8 << 20
+
+
+def call(kernel, small, operands, shapes):
     shapes = [jax.ShapeDtypeStruct(s, jnp.float32) for s in shapes]
     return pl.pallas_call(
         kernel,
-        name=name,
         out_shape=shapes,
         in_specs=[SMEM] * len(small) + [VMEM] * len(operands),
         out_specs=[VMEM] * len(shapes),
+        compiler_params=pltpu.CompilerParams(vmem_limit_bytes=GRANT),
         interpret=INTERPRET,
     )(*small, *operands)
 
@@ -488,7 +489,6 @@
     gathered = lax.all_gather(strips, "ty", axis=0)
     slots, swap_a, swap_b, local, halos = call(
         functools.partial(route_kernel, nt, nq),
-        "route_" + kind,
         (place, links),
         (gathered, top, bottom, codes, picks),
         ((nt, 8, 128), (32, 128), (32, 128), (32, 128), (16, 64)),
@@ -510,17 +510,10 @@
         lax.axis_index("face"),
         jnp.where(index == 1, lax.axis_index("tx"), lax.axis_index("ty")),
     )
-    (sent,) = call(
-        functools.partial(thickness_kernel, nf),
-        "thickness",
-        (),
-        (probes, spread),
-        ((nf, 48, 128),),
-    )
+    (sent,) = call(functools.partial(thickness_kernel, nf), (), (probes, spread), ((nf, 48, 128),))
     totals = lax.all_to_all(sent, "face", 0, 0, tiled=True)
     fields, strips, top, bottom = call(
         functools.partial(fields_kernel, nf),
-        "fields",
         (place,),
         (probes, spread, wind, mass, heat, totals),
         ((36, 8, 128), (STRIP, 128), (32, 128), (32, 128)),
@@ -528,7 +521,6 @@
     outer = exchange("forward", nt, nq, place, links, strips, top, bottom)
     costs, strips, top, bottom = call(
         functools.partial(image_kernel, nt, nq),
-        "image",
         (place, links),
         (*outer, fields, probes, spread, wind, misfit),
         ((24, 8, 128), (STRIP, 128), (32, 128), (32, 128)),
@@ -536,7 +528,6 @@
     outer = exchange("adjoint", nt, nq, place, links, strips, top, bottom)
     backs, loads = call(
         functools.partial(adjoint_kernel, nt, nq, nf),
-        "adjoint",
         (place, links),
         (*outer, costs, wind, mass, heat),
         ((24, 8, 128), (nf, 48, 128)),
@@ -544,7 +535,6 @@
     loads = lax.all_to_all(loads, "face", 0, 0, tiled=True)
     (applied,) = call(
         functools.partial(final_kernel, nf),
-        "final",
         (place,),
         (probes, spread, backs, loads),
         (probes.shape,),

time: 124 us -> 114 us (0.919)
  Pallas kernels: 17.1 us -> 10.8 us
  blocking collectives: 33.6 us -> 29.7 us
  waiting for transfers between devices: 12.9 us -> 14.6 us
  local copies, waits for them, and re-layouts: 3.37 us -> 1.97 us
    pallas_call x7, Pallas kernels: 17.1 us -> 10.8 us  [call(): pl.pallas_call(kernel, out_shape=shapes, in_specs=[SMEM] * len(small) + [...]
    all_gather x2, blocking collectives: 19.8 us -> 17.6 us  [exchange(): gathered = lax.all_gather(strips, 'ty', axis=0)]
    all_to_all x1, waiting for transfers between devices: 8.55 us -> 10.3 us  [body(): totals = lax.all_to_all(sent, 'face', 0, 0, tiled=True)]
    all_to_all x1, blocking collectives: 13.8 us -> 12.2 us  [body(): loads = lax.all_to_all(loads, 'face', 0, 0, tiled=True)]
    unnamed x24 -> x26, local copies, waits for them, and re-layouts: 2.7 us -> 1.87 us
  transfers between devices with their start and end apart: 7 -> 7, of which waited for: 3 -> 3; matrix products, arithmetic and copies ran while one was open for 1% -> 0% of each run, Pallas kernels for 0% -> 0%
where the time goes in v1:
time: 114 us
  starting transfers between devices  56.2 us (49%)
  blocking collectives  29.7 us (26%)
  waiting for transfers between devices  14.6 us (13%)
  Pallas kernels  10.8 us (9%)
  local copies, waits for them, and re-layouts  1.97 us (2%)
    all_to_all x2, starting transfers between devices, exchange(): arrived = lax.all_to_all(slots, 'tx', 0, 0, tiled=True)  23.9 us
    all_gather x2, blocking collectives, exchange(): gathered = lax.all_gather(strips, 'ty', axis=0)  17.6 us
    ppermute x2, starting transfers between devices, exchange(): swapped_b = lax.ppermute(swap_b, 'tx', wrapped)  15.4 us
    all_to_all x1, blocking collectives, body(): loads = lax.all_to_all(loads, 'face', 0, 0, tiled=True)  12.2 us
    pallas_call x7, Pallas kernels, call(): pl.pallas_call(kernel, out_shape=shapes, in_specs=[SMEM] * len(small) + [...  10.8 us
    all_to_all x1, waiting for transfers between devices, body(): totals = lax.all_to_all(sent, 'face', 0, 0, tiled=True)  10.3 us
    ppermute x2, starting transfers between devices, exchange(): swapped_a = lax.ppermute(swap_a, 'tx', near)  9.19 us
    all_to_all x1, starting transfers between devices, body(): totals = lax.all_to_all(sent, 'face', 0, 0, tiled=True)  7.7 us
  transfers between devices with their start and end apart: 7, of which 3 were waited for; matrix products, arithmetic and copies ran while one was open for 0% of the time, Pallas kernels for 0%

profile of v1, /device:TPU:2, one launch (start us, length us, event | category | flops | bytes accessed | tf_op | source)
XLA Modules:
  0.0 113.5 jit_solution(8669568432225612823)
XLA Ops:
  0.0 0.0 copy-start
  0.0 0.9 copy-done
  0.9 0.0 copy-start.2
  0.9 0.9 copy-done.2
  1.8 0.8 shard_map.109
  2.6 0.0 copy-start.12
  2.6 0.0 copy-start.1
  2.6 0.0 copy-start.3
  2.6 0.0 copy-start.4
  2.6 0.0 copy-start.9
  2.6 7.7 %all-to-all-start = ((f32[8,48,128]{2,1,0:T(8,128)}), f32[8,48,128]{2,1,0:T(8,128)S(1)}, u32[]{:S(2)}, u32[]{:S(2)}) async-start(f32[8,48,128]{2,1,0:T(8,128)} %shard_map.109), calls=%async_computation | async-start | bytes 393216 | tf_op jit(solution)/shard_map/all_to_all | solution.py:514
  10.3 0.0 copy-start.8
  10.3 0.0 copy-done.12
  10.3 0.1 reshape.3.links
  10.4 0.0 copy-start.6
  10.5 10.3 %all-to-all-done.totals = f32[8,48,128]{2,1,0:T(8,128)S(1)} async-done(((f32[8,48,128]{2,1,0:T(8,128)}), f32[8,48,128]{2,1,0:T(8,128)S(1)}, u32[]{:S(2)}, u32[]{:S(2)}) %all-to-all-start) | async-done | bytes 196640 | tf_op jit(solution)/shard_map/all_to_all | solution.py:514
  20.8 0.0 copy-done.1
  20.8 0.0 copy-done.3
  20.8 0.0 copy-done.4
  20.8 0.0 copy-done.9
  20.8 0.0 copy-done.8
  20.8 0.8 shard_map.110
  21.6 0.0 copy-start.11
  21.6 12.0 %all-gather = f32[288,128]{1,0:T(8,128)S(1)} all-gather(f32[72,128]{1,0:T(8,128)S(1)} %get-tuple-element.25), channel_id=2, replica_groups=mesh['face'=8,'tx'=32,'ty'=4] {'ty'}, dimensions={0}, use_global_device_ids=true | all-gather | bytes 184320 | tf_op jit(solution)/shard_map/all_gather | solution.py:489
  33.6 0.0 copy-done.6
  33.6 0.0 copy-done.11
  33.6 2.8 %shard_map.111 = (f32[32,8,128]{2,1,0:T(8,128)}, f32[32,128]{1,0:T(8,128)S(1)}, f32[32,128]{1,0:T(8,128)S(1)}, f32[32,128]{1,0:T(8,128)S(1)}, f32[16,64]{1,0:T(8,128)S(1)}) custom-call(s32[3]{0:T(128)S(1)} %compare_select_fusion.1.place, s32[168]{0:T(256)S(1)} %reshape.3.links, f32[4,72,128]{2,1,0:T(8,128)S(1)} %bitcast.2, ...), custom_call_target="tpu_custom_call" | custom-call | tf_op jit(solution)/shard_map/pallas_call | solution.py:475
  36.4 0.0 copy-start.7
  36.4 15.0 %all-to-all-start.1 = ((f32[32,8,128]{2,1,0:T(8,128)}), f32[32,8,128]{2,1,0:T(8,128)S(1)}, u32[]{:S(2)}, u32[]{:S(2)}) async-start(f32[32,8,128]{2,1,0:T(8,128)} %get-tuple-element.28), calls=%async_computation.1 | async-start | bytes 262144 | tf_op jit(solution)/shard_map/all_to_all | solution.py:500
  51.4 4.6 %collective-permute-start = (f32[32,128]{1,0:T(8,128)S(1)}, f32[32,128]{1,0:T(8,128)S(1)}, u32[]{:S(2)}, u32[]{:S(2)}) collective-permute-start(f32[32,128]{1,0:T(8,128)S(1)} %get-tuple-element.29), channel_id=1, source_target_pairs={{0,4},{4,0},{8,12},{12,8},{16,20},{20,16},{24,28},{28,24},{32,36},... | collective-permute-start | bytes 49160 | tf_op jit(solution)/shard_map/ppermute | solution.py:498
  56.0 7.7 %collective-permute-start.1 = (f32[32,128]{1,0:T(8,128)S(1)}, f32[32,128]{1,0:T(8,128)S(1)}, u32[]{:S(2)}, u32[]{:S(2)}) collective-permute-start(f32[32,128]{1,0:T(8,128)S(1)} %get-tuple-element.30), channel_id=1, source_target_pairs={{0,124},{4,8},{8,4},{12,16},{16,12},{20,24},{24,20},{28,32},{32,28... | collective-permute-start | bytes 49160 | tf_op jit(solution)/shard_map/ppermute | solution.py:499
  63.7 0.0 collective-permute-done.swapped_a
  63.7 2.2 %collective-permute-done.1.swapped_b = f32[32,128]{1,0:T(8,128)S(1)} collective-permute-done((f32[32,128]{1,0:T(8,128)S(1)}, f32[32,128]{1,0:T(8,128)S(1)}, u32[]{:S(2)}, u32[]{:S(2)}) %collective-permute-start.1) | collective-permute-done | bytes 16416 | tf_op jit(solution)/shard_map/ppermute | solution.py:499
  65.9 0.0 all-to-all-done.1.arrived
  65.9 0.0 copy-done.7
  65.9 0.0 copy-start.5
  65.9 1.2 %shard_map.112 = (f32[24,8,128]{2,1,0:T(8,128)S(1)}, f32[72,128]{1,0:T(8,128)S(1)}, f32[32,128]{1,0:T(8,128)S(1)}, f32[32,128]{1,0:T(8,128)S(1)}) custom-call(s32[3]{0:T(128)S(1)} %compare_select_fusion.1.place, s32[168]{0:T(256)S(1)} %reshape.3.links, f32[32,8,128]{2,1,0:T(8,128)S(1)} %all-to-all-done.1.arrived, ...), custom_call_target="tpu_custom_call" | custom-call | tf_op jit(solution)/shard_map/pallas_call | solution.py:475
  67.1 0.0 copy-start.10
  67.1 5.6 %all-gather.1 = f32[288,128]{1,0:T(8,128)S(1)} all-gather(f32[72,128]{1,0:T(8,128)S(1)} %get-tuple-element.34), channel_id=3, replica_groups=mesh['face'=8,'tx'=32,'ty'=4] {'ty'}, dimensions={0}, use_global_device_ids=true | all-gather | bytes 184320 | tf_op jit(solution)/shard_map/all_gather | solution.py:489
  72.7 0.0 copy-done.5
  72.7 0.0 copy-done.10
  72.7 2.8 %shard_map.113 = (f32[32,8,128]{2,1,0:T(8,128)}, f32[32,128]{1,0:T(8,128)S(1)}, f32[32,128]{1,0:T(8,128)S(1)}, f32[32,128]{1,0:T(8,128)S(1)}, f32[16,64]{1,0:T(8,128)S(1)}) custom-call(s32[3]{0:T(128)S(1)} %compare_select_fusion.1.place, s32[168]{0:T(256)S(1)} %reshape.3.links, f32[4,72,128]{2,1,0:T(8,128)S(1)} %bitcast.3, ...), custom_call_target="tpu_custom_call" | custom-call | tf_op jit(solution)/shard_map/pallas_call | solution.py:475
  75.5 8.9 %all-to-all-start.2 = ((f32[32,8,128]{2,1,0:T(8,128)}), f32[32,8,128]{2,1,0:T(8,128)S(1)}, u32[]{:S(2)}, u32[]{:S(2)}) async-start(f32[32,8,128]{2,1,0:T(8,128)} %get-tuple-element.37), calls=%async_computation.2 | async-start | bytes 262144 | tf_op jit(solution)/shard_map/all_to_all | solution.py:500
  84.5 4.6 %collective-permute-start.2 = (f32[32,128]{1,0:T(8,128)S(1)}, f32[32,128]{1,0:T(8,128)S(1)}, u32[]{:S(2)}, u32[]{:S(2)}) collective-permute-start(f32[32,128]{1,0:T(8,128)S(1)} %get-tuple-element.38), channel_id=1, source_target_pairs={{0,4},{4,0},{8,12},{12,8},{16,20},{20,16},{24,28},{28,24},{32,36},... | collective-permute-start | bytes 49160 | tf_op jit(solution)/shard_map/ppermute | solution.py:498
  89.1 7.7 %collective-permute-start.3 = (f32[32,128]{1,0:T(8,128)S(1)}, f32[32,128]{1,0:T(8,128)S(1)}, u32[]{:S(2)}, u32[]{:S(2)}) collective-permute-start(f32[32,128]{1,0:T(8,128)S(1)} %get-tuple-element.39), channel_id=1, source_target_pairs={{0,124},{4,8},{8,4},{12,16},{16,12},{20,24},{24,20},{28,32},{32,28... | collective-permute-start | bytes 49160 | tf_op jit(solution)/shard_map/ppermute | solution.py:499
  96.8 0.0 collective-permute-done.2.swapped_a
  96.8 2.2 %collective-permute-done.3.swapped_b = f32[32,128]{1,0:T(8,128)S(1)} collective-permute-done((f32[32,128]{1,0:T(8,128)S(1)}, f32[32,128]{1,0:T(8,128)S(1)}, u32[]{:S(2)}, u32[]{:S(2)}) %collective-permute-start.3) | collective-permute-done | bytes 16416 | tf_op jit(solution)/shard_map/ppermute | solution.py:499
  98.9 0.0 all-to-all-done.2.arrived
  98.9 1.1 shard_map.114
  100.0 12.2 %all_to_all.20.loads = f32[8,48,128]{2,1,0:T(8,128)S(1)} all-to-all(f32[8,48,128]{2,1,0:T(8,128)S(1)} %get-tuple-element.44), channel_id=1, replica_groups=mesh['face'=8,'tx'=32,'ty'=4] {'face'}, dimensions={0} | all-to-all | bytes 393216 | tf_op jit(solution)/shard_map/all_to_all | solution.py:535
  112.2 1.3 %shard_map.115 = f32[2,4,1,6,8,64]{5,4,3,2,1,0:T(8,128)} custom-call(s32[3]{0:T(128)S(1)} %compare_select_fusion.1.place, f32[2,4,1,6,8,64]{5,4,3,2,1,0:T(8,128)S(1)} %copy-done.1, f32[4,1,6,8,64]{4,3,2,1,0:T(8,128)S(1)} %copy-done.3, f32[24,8,128]{2,1,0:T(8,128)S(1)} %get-tuple-element.43.backs, f32[8,48,128]{2,1,0:T(8,128)S(1)} %all_to_all.20.loads), custom_call_target="tpu_custom_call" | custom-call | tf_op jit(solution)/shard_map/pallas_call | solution.py:475
  (1 shorter events, 0.0 us)
Async XLA Ops:
  0.0 0.9 copy-start
  0.9 0.9 copy-start.2
  2.6 7.7 %copy-start.12 = (s32[6,4,7]{2,1,0:T(4,128)S(1)}, s32[6,4,7]{2,1,0:T(4,128)}, u32[]{:S(2)}) copy-start(s32[6,4,7]{2,1,0:T(4,128)} %param.17) | copy-start | bytes 2020
  2.6 18.2 %copy-start.1 = (f32[2,4,1,6,8,64]{5,4,3,2,1,0:T(8,128)S(1)}, f32[2,4,1,6,8,64]{5,4,3,2,1,0:T(8,128)}, u32[]{:S(2)}) copy-start(f32[2,4,1,6,8,64]{5,4,3,2,1,0:T(8,128)} %probes.7) | copy-start | bytes 294916
  2.6 18.2 %copy-start.3 = (f32[4,1,6,8,64]{4,3,2,1,0:T(8,128)S(1)}, f32[4,1,6,8,64]{4,3,2,1,0:T(8,128)}, u32[]{:S(2)}) copy-start(f32[4,1,6,8,64]{4,3,2,1,0:T(8,128)} %spread.7) | copy-start | bytes 147460
  2.6 18.2 %copy-start.4 = (f32[2,1,6,8,64]{4,3,2,1,0:T(8,128)S(1)}, f32[2,1,6,8,64]{4,3,2,1,0:T(8,128)}, u32[]{:S(2)}) copy-start(f32[2,1,6,8,64]{4,3,2,1,0:T(8,128)} %wind.5) | copy-start | bytes 73732
  2.6 18.2 %copy-start.9 = (f32[1,6,8,64]{3,2,1,0:T(8,128)S(1)}, f32[1,6,8,64]{3,2,1,0:T(8,128)}, u32[]{:S(2)}) copy-start(f32[1,6,8,64]{3,2,1,0:T(8,128)} %heat.3) | copy-start | bytes 36868
  2.6 18.2 %all-to-all-start = ((f32[8,48,128]{2,1,0:T(8,128)}), f32[8,48,128]{2,1,0:T(8,128)S(1)}, u32[]{:S(2)}, u32[]{:S(2)}) async-start(f32[8,48,128]{2,1,0:T(8,128)} %shard_map.109), calls=%async_computation | async-start | bytes 393216 | tf_op jit(solution)/shard_map/all_to_all | solution.py:514
  10.3 10.5 %copy-start.8 = (f32[1,6,8,64]{3,2,1,0:T(8,128)S(1)}, f32[1,6,8,64]{3,2,1,0:T(8,128)}, u32[]{:S(2)}) copy-start(f32[1,6,8,64]{3,2,1,0:T(8,128)} %mass.3) | copy-start | bytes 36868
  10.4 23.2 %copy-start.6 = (f32[5,128,64]{2,1,0:T(8,128)S(1)}, f32[5,128,64]{2,1,0:T(8,128)}, u32[]{:S(2)}) copy-start(f32[5,128,64]{2,1,0:T(8,128)} %constant.26.clone.codes) | copy-start | bytes 491524
  21.6 12.0 %copy-start.11 = (f32[128,64]{1,0:T(8,128)S(1)}, f32[128,64]{1,0:T(8,128)}, u32[]{:S(2)}) copy-start(f32[128,64]{1,0:T(8,128)} %constant.27.clone.picks) | copy-start | bytes 98308
  36.4 29.5 %copy-start.7 = (f32[4,1,6,8,64]{4,3,2,1,0:T(8,128)S(1)}, f32[4,1,6,8,64]{4,3,2,1,0:T(8,128)}, u32[]{:S(2)}) copy-start(f32[4,1,6,8,64]{4,3,2,1,0:T(8,128)} %misfit.1) | copy-start | bytes 147460
  36.4 29.5 %all-to-all-start.1 = ((f32[32,8,128]{2,1,0:T(8,128)}), f32[32,8,128]{2,1,0:T(8,128)S(1)}, u32[]{:S(2)}, u32[]{:S(2)}) async-start(f32[32,8,128]{2,1,0:T(8,128)} %get-tuple-element.28), calls=%async_computation.1 | async-start | bytes 262144 | tf_op jit(solution)/shard_map/all_to_all | solution.py:500
  51.4 12.3 %collective-permute-start = (f32[32,128]{1,0:T(8,128)S(1)}, f32[32,128]{1,0:T(8,128)S(1)}, u32[]{:S(2)}, u32[]{:S(2)}) collective-permute-start(f32[32,128]{1,0:T(8,128)S(1)} %get-tuple-element.29), channel_id=1, source_target_pairs={{0,4},{4,0},{8,12},{12,8},{16,20},{20,16},{24,28},{28,24},{32,36},... | collective-permute-start | bytes 49160 | tf_op jit(solution)/shard_map/ppermute | solution.py:498
  56.0 9.9 %collective-permute-start.1 = (f32[32,128]{1,0:T(8,128)S(1)}, f32[32,128]{1,0:T(8,128)S(1)}, u32[]{:S(2)}, u32[]{:S(2)}) collective-permute-start(f32[32,128]{1,0:T(8,128)S(1)} %get-tuple-element.30), channel_id=1, source_target_pairs={{0,124},{4,8},{8,4},{12,16},{16,12},{20,24},{24,20},{28,32},{32,28... | collective-permute-start | bytes 49160 | tf_op jit(solution)/shard_map/ppermute | solution.py:499
  65.9 6.8 %copy-start.5 = (f32[5,128,64]{2,1,0:T(8,128)S(1)}, f32[5,128,64]{2,1,0:T(8,128)}, u32[]{:S(2)}) copy-start(f32[5,128,64]{2,1,0:T(8,128)} %constant.28.clone.codes) | copy-start | bytes 491524
  67.1 5.6 %copy-start.10 = (f32[128,64]{1,0:T(8,128)S(1)}, f32[128,64]{1,0:T(8,128)}, u32[]{:S(2)}) copy-start(f32[128,64]{1,0:T(8,128)} %constant.29.clone.picks) | copy-start | bytes 98308
  75.5 23.4 %all-to-all-start.2 = ((f32[32,8,128]{2,1,0:T(8,128)}), f32[32,8,128]{2,1,0:T(8,128)S(1)}, u32[]{:S(2)}, u32[]{:S(2)}) async-start(f32[32,8,128]{2,1,0:T(8,128)} %get-tuple-element.37), calls=%async_computation.2 | async-start | bytes 262144 | tf_op jit(solution)/shard_map/all_to_all | solution.py:500
  84.5 12.3 %collective-permute-start.2 = (f32[32,128]{1,0:T(8,128)S(1)}, f32[32,128]{1,0:T(8,128)S(1)}, u32[]{:S(2)}, u32[]{:S(2)}) collective-permute-start(f32[32,128]{1,0:T(8,128)S(1)} %get-tuple-element.38), channel_id=1, source_target_pairs={{0,4},{4,0},{8,12},{12,8},{16,20},{20,16},{24,28},{28,24},{32,36},... | collective-permute-start | bytes 49160 | tf_op jit(solution)/shard_map/ppermute | solution.py:498
  89.1 9.9 %collective-permute-start.3 = (f32[32,128]{1,0:T(8,128)S(1)}, f32[32,128]{1,0:T(8,128)S(1)}, u32[]{:S(2)}, u32[]{:S(2)}) collective-permute-start(f32[32,128]{1,0:T(8,128)S(1)} %get-tuple-element.39), channel_id=1, source_target_pairs={{0,124},{4,8},{8,4},{12,16},{16,12},{20,24},{24,20},{28,32},{32,28... | collective-permute-start | bytes 49160 | tf_op jit(solution)/shard_map/ppermute | solution.py:499

commit v2 on v1

--- a/solution.py
+++ b/solution.py
@@ -89,26 +89,43 @@
 }
 
 
-def dot(a, b, contract=(1, 0)):
+def parts(data):
+    high = data.astype(jnp.bfloat16)
+    rest = data - high.astype(jnp.float32)
+    middle = rest.astype(jnp.bfloat16)
+    low = (rest - middle.astype(jnp.float32)).astype(jnp.bfloat16)
+    return high, middle, low
+
+
+def product(a, b, contract):
     return lax.dot_general(
         a,
         b,
         (((contract[0],), (contract[1],)), ((), ())),
-        precision=lax.Precision.HIGHEST,
         preferred_element_type=jnp.float32,
     )
+
+
+def moved(data, choice, contract=(1, 0)):
+    high, middle, low = (product(d, choice, contract) for d in data)
+    return (high + middle) + low
+
+
+def chosen(choice, data, contract=(1, 0)):
+    high, middle, low = (product(choice, d, contract) for d in data)
+    return (high + middle) + low
 
 
 def reversal(size):
     row = lax.broadcasted_iota(jnp.int32, (size, size), 0)
     column = lax.broadcasted_iota(jnp.int32, (size, size), 1)
-    return (row + column == size - 1).astype(jnp.float32)
+    return (row + column == size - 1).astype(jnp.float32).astype(jnp.bfloat16)
 
 
 def identity(size):
     row = lax.broadcasted_iota(jnp.int32, (size, size), 0)
     column = lax.broadcasted_iota(jnp.int32, (size, size), 1)
-    return (row == column).astype(jnp.float32)
+    return (row == column).astype(jnp.float32).astype(jnp.bfloat16)
 
 
 def lanes(shape):
@@ -117,6 +134,10 @@
 
 def joined(even, odd):
     return jnp.concatenate([even, odd], axis=1)
+
+
+def joined_all(pieces):
+    return jnp.concatenate(pieces, axis=1)
 
 
 def pair(ref, index, pp):
@@ -129,7 +150,7 @@
     third = within - 3 * ((within * 43) // 128)
     out = jnp.zeros((1, 64), jnp.float32)
     for f in range(6):
-        value = links[f * 28 + edge * 7 + item].astype(jnp.float32)
+        value = links[f, edge, item].astype(jnp.float32)
         here = (third == f // 2) & ((lane >= 32) == (f % 2 == 1))
         out = jnp.where(here, value, out)
     return out
@@ -189,15 +210,15 @@
 def thickness_kernel(slots, probes, spread, out):
     for probe in range(PROBES):
         for pp in range(3):
-            value = pair(spread, (2, 0), pp) * pair(probes, (probe, 2, 0), pp)
+            value = pair(spread, (0, 0), pp) * pair(probes, (probe, 0, 0), pp)
             for k in range(slots):
                 out[k, (probe * 3 + pp) * 8 : (probe * 3 + pp) * 8 + 8] = value
 
 
 def fields_kernel(
-    level_count, place, probes, spread, wind, mass, heat, totals, fields, strips, top, bottom
+    level_count, probes, spread, wind, mass, heat, totals, fields, strips, top, bottom
 ):
-    level = place[0]
+    level, tile_row = lax.axis_index("face"), lax.axis_index("tx")
     planes = {}
     for pp in range(3):
         east = pair(wind, (0, 0), pp)
@@ -222,7 +243,7 @@
     ordered = [planes[n, pr, pp] for n in FORWARD for pr in range(PROBES) for pp in range(3)]
     for a, plane in enumerate(ordered):
         fields[a] = plane
-    put_strips(ordered, strips, place[1])
+    put_strips(ordered, strips, tile_row)
     put_outer_rows(
         [planes[n, pr, pp] for n in FORWARD_X for pr in range(PROBES) for pp in range(3)],
         top,
@@ -230,18 +251,17 @@
     )
 
 
-def route_kernel(
-    nt, nq, place, links, gathered, top, bottom, codes, picks, slots, swap_a, swap_b, local, halos
-):
-    tile_row, tile_column = place[1], place[2]
+def route_kernel(nt, nq, links, gathered, top, bottom, codes, picks, slots, local, halos):
+    tile_row, tile_column = lax.axis_index("tx"), lax.axis_index("ty")
     is_first, is_last = tile_row == 0, tile_row == nt - 1
-    line = jnp.where(is_first, 0, 1)
-    line_f = line.astype(jnp.float32)
+    line_f = jnp.where(is_first, 0.0, 1.0)
     column_edge = jnp.where(tile_column == 0, 2, 3)
     panel = codes[4]
     c0 = coefficients(links, 0, codes[0], codes[1], panel)
     c1 = coefficients(links, 1, codes[0], codes[1], panel)
     cc = coefficients(links, column_edge, codes[2], codes[3], panel)
+    ends = joined(c0, c1).astype(jnp.bfloat16)
+    cc = cc.astype(jnp.bfloat16)
 
     def masks(edge, source):
         far = link_lanes(links, edge, 1)
@@ -257,66 +277,64 @@
 
     def segment(q):
         packed = gathered[q, 16:STRIP]
-        return jnp.concatenate([packed[:, 0:64], empty, packed[:, 64:128], empty], axis=0)
+        return parts(
+            jnp.concatenate([packed[:, 0:64], empty, packed[:, 64:128], empty], axis=0)
+        )
 
     on_boundary = jnp.where(is_first | is_last, 1.0, 0.0)
     plain_c, turned_c = masks(column_edge, line_f)
-    across = [dot(segment(q), cc, (0, 0)) for q in range(nq)]
-    pieces = []
-    for q in range(nq):
-        pieces.append(
-            on_boundary
-            * (across[q] * plain_c + dot(back64, across[nq - 1 - q] * turned_c))
-        )
-    low_column, high_column = gathered[0, 0:8], gathered[nq - 1, 8:16]
+    across = [moved(segment(q), cc, (0, 0)) * on_boundary for q in range(nq)]
+    turned = joined_all([a * turned_c for a in across])
+    turned = chosen(back64, parts(turned))
+    pieces = [
+        across[q] * plain_c + turned[:, 64 * (nq - 1 - q) : 64 * (nq - q)] for q in range(nq)
+    ]
+    columns = parts(jnp.concatenate([gathered[0, 0:8], gathered[nq - 1, 8:16]], axis=0))
     low_plain, low_turned = masks(column_edge, 2.0)
     high_plain, high_turned = masks(column_edge, 3.0)
-    low_c, high_c = dot(low_column, cc), dot(high_column, cc)
+    to_columns = moved(columns, cc)
+    low_c, high_c = to_columns[0:8], to_columns[8:16]
     straight = low_c * low_plain + high_c * high_plain
-    flipped = dot(reversal(8), low_c * low_turned + high_c * high_turned)
-    to_rows = []
-    for edge, c in ((0, c0), (1, c1)):
-        far = link_lanes(links, edge, 1)
-        to_rows.append(
-            dot(low_column, c) * jnp.where(far == 2.0, 1.0, 0.0)
-            + dot(high_column, c) * jnp.where(far == 3.0, 1.0, 0.0)
-        )
+    flipped = chosen(reversal(8), parts(low_c * low_turned + high_c * high_turned))
+    to_rows = moved(columns, ends)
+    far = joined(link_lanes(links, 0, 1), link_lanes(links, 1, 1))
+    to_rows = to_rows[0:8] * jnp.where(far == 2.0, 1.0, 0.0) + to_rows[8:16] * jnp.where(
+        far == 3.0, 1.0, 0.0
+    )
+    to_rows = [to_rows[:, 0:64], to_rows[:, 64:128]]
     for t in range(nt):
         q, at = t // 8, (t % 8) * 8
         left = pieces[q][at : at + 8]
         left = left + jnp.where(tile_row == t, straight, 0.0)
         left = left + jnp.where(tile_row == nt - 1 - t, flipped, 0.0)
-        slots[t] = joined(left, to_rows[1] if t == nt - 1 else to_rows[0])
-
-    mine, mirrored = gathered[tile_column, 16:STRIP], gathered[nq - 1 - tile_column, 16:STRIP]
-    mine = jnp.concatenate([mine[:, 0:64], empty, mine[:, 64:128], empty], axis=0)
-    mirrored = jnp.concatenate([mirrored[:, 0:64], empty, mirrored[:, 64:128], empty], axis=0)
-    by_row = []
-    for edge, c in ((0, c0), (1, c1)):
-        plain, turned = masks(edge, line_f)
-        by_row.append(
-            dot(c * plain, mine, (0, 0)) + dot(dot(c * turned, mirrored, (0, 0)), back64)
-        )
-    by_row = [joined(z[0:32], z[32:64]) for z in by_row]
+        slots[t, 0:8] = joined(left, to_rows[1] if t == nt - 1 else to_rows[0])
+
+    plain0, turned0 = masks(0, line_f)
+    plain1, turned1 = masks(1, line_f)
+    plain = (joined(c0, c1) * joined(plain0, plain1)).astype(jnp.bfloat16)
+    mirror = (joined(c0, c1) * joined(turned0, turned1)).astype(jnp.bfloat16)
+    by_row = chosen(plain, segment(tile_column), (0, 0))
+    by_row = by_row + moved(
+        parts(chosen(mirror, segment(nq - 1 - tile_column), (0, 0))), back64
+    )
+    by_row = [joined(by_row[k : k + 32], by_row[k + 32 : k + 64]) for k in (0, 64)]
     local[...] = jnp.where(is_first, by_row[0], by_row[1])
-    to_lower = jnp.where(is_first, by_row[1], top[...])
-    to_upper = jnp.where(is_last, by_row[0], bottom[...])
-    even = lax.rem(tile_row, 2) == 0
-    swap_a[...] = jnp.where(even, to_upper, to_lower)
-    swap_b[...] = jnp.where(even, to_lower, to_upper)
+    slots[lax.rem(tile_row + nt - 1, nt), 8:40] = jnp.where(is_first, by_row[1], top[...])
+    slots[lax.rem(tile_row + 1, nt), 8:40] = jnp.where(is_last, by_row[0], bottom[...])
 
     below = gathered[jnp.maximum(tile_column - 1, 0), 8:16]
     above = gathered[jnp.minimum(tile_column + 1, nq - 1), 0:8]
-    halos[0:8] = jnp.where(tile_column > 0, dot(below, picks[...]), 0.0)
-    halos[8:16] = jnp.where(tile_column < nq - 1, dot(above, picks[...]), 0.0)
-
-
-def outer_values(nt, nq, place, links, arrived, swapped_a, swapped_b, local, halos):
-    tile_row, tile_column = place[1], place[2]
+    near = moved(parts(jnp.concatenate([below, above], axis=0)), picks[...].astype(jnp.bfloat16))
+    halos[0:8] = jnp.where(tile_column > 0, near[0:8], 0.0)
+    halos[8:16] = jnp.where(tile_column < nq - 1, near[8:16], 0.0)
+
+
+def outer_values(nt, nq, links, arrived, local, halos):
+    tile_row, tile_column = lax.axis_index("tx"), lax.axis_index("ty")
     is_first, is_last = tile_row == 0, tile_row == nt - 1
-    column = arrived[0]
+    column = arrived[0, 0:8]
     for t in range(1, nt):
-        column = column + arrived[t]
+        column = column + arrived[t, 0:8]
     column = column[:, 0:64]
     south = halos[0:8] + jnp.where(tile_column == 0, column, 0.0)
     north = halos[8:16] + jnp.where(tile_column == nq - 1, column, 0.0)
@@ -326,27 +344,23 @@
         wide = joined(narrow, narrow)
         return jnp.where(lane < 32, wide, pltpu.roll(wide, 32, 1))
 
-    mine = arrived[pl.ds(tile_column * 8, 8)].reshape(64, 128)[:, 64:128]
-    mirrored = arrived[pl.ds((nq - 1 - tile_column) * 8, 8)].reshape(64, 128)[:, 64:128]
+    mine = arrived[pl.ds(tile_column * 8, 8), 0:8].reshape(64, 128)[:, 64:128]
+    mirrored = arrived[pl.ds((nq - 1 - tile_column) * 8, 8), 0:8].reshape(64, 128)[:, 64:128]
     flip = link_lanes(links, jnp.where(is_first, 0, 1), 2)
-    row = dot(jnp.where(flip != 1.0, mine, 0.0), identity(64), (0, 0)) + dot(
-        jnp.where(flip == 1.0, mirrored, 0.0), reversal(64), (0, 0)
+    row = moved(parts(jnp.where(flip != 1.0, mine, 0.0)), identity(64), (0, 0)) + moved(
+        parts(jnp.where(flip == 1.0, mirrored, 0.0)), reversal(64), (0, 0)
     )
     row = joined(row[0:32], row[32:64]) + local[...]
-    even = lax.rem(tile_row, 2) == 0
-    west = jnp.where(even, swapped_b[...], swapped_a[...]) + jnp.where(is_first, row, 0.0)
-    east = jnp.where(even, swapped_a[...], swapped_b[...]) + jnp.where(is_last, row, 0.0)
+    west = arrived[lax.rem(tile_row + nt - 1, nt), 8:40] + jnp.where(is_first, row, 0.0)
+    east = arrived[lax.rem(tile_row + 1, nt), 8:40] + jnp.where(is_last, row, 0.0)
     return west, east, spread_out(south), spread_out(north)
 
 
 def image_kernel(
     nt,
     nq,
-    place,
     links,
     arrived,
-    swapped_a,
-    swapped_b,
     local,
     halos,
     fields,
@@ -359,9 +373,7 @@
     top,
     bottom,
 ):
-    west, east, south, north = outer_values(
-        nt, nq, place, links, arrived, swapped_a, swapped_b, local, halos
-    )
+    west, east, south, north = outer_values(nt, nq, links, arrived, local, halos)
     planes = {}
     for pp in range(3):
         u = pair(wind, (0, 0), pp)
@@ -387,7 +399,7 @@
     put_strips(
         [planes[n, pr, pp] for n in ADJOINT for pr in range(PROBES) for pp in range(3)],
         strips,
-        place[1],
+        lax.axis_index("tx"),
     )
     put_outer_rows(
         [planes[n, pr, pp] for n in ADJOINT_X for pr in range(PROBES) for pp in range(3)],
@@ -400,11 +412,8 @@
     nt,
     nq,
     levels,
-    place,
     links,
     arrived,
-    swapped_a,
-    swapped_b,
     local,
     halos,
     costs,
@@ -414,9 +423,7 @@
     backs,
     loads,
 ):
-    west, east, south, north = outer_values(
-        nt, nq, place, links, arrived, swapped_a, swapped_b, local, halos
-    )
+    west, east, south, north = outer_values(nt, nq, links, arrived, local, halos)
     for pp in range(3):
         u = pair(wind, (0, 0), pp)
         v = pair(wind, (1, 0), pp)
@@ -446,8 +453,8 @@
                 loads[k, (probe * 3 + pp) * 8 : (probe * 3 + pp) * 8 + 8] = load
 
 
-def final_kernel(level_count, place, probes, spread, backs, loads, out):
-    level = place[0]
+def final_kernel(level_count, probes, spread, backs, loads, out):
+    level = lax.axis_index("face")
     for probe in range(PROBES):
         for pp in range(3):
             at = (probe * 3 + pp) * 8
@@ -470,10 +477,11 @@
 GRANT = 8 << 20
 
 
-def call(kernel, small, operands, shapes):
+def call(kernel, name, small, operands, shapes):
     shapes = [jax.ShapeDtypeStruct(s, jnp.float32) for s in shapes]
     return pl.pallas_call(
         kernel,
+        name=name,
         out_shape=shapes,
         in_specs=[SMEM] * len(small) + [VMEM] * len(operands),
         out_specs=[VMEM] * len(shapes),
@@ -482,60 +490,69 @@
     )(*small, *operands)
 
 
-def exchange(kind, nt, nq, place, links, strips, top, bottom):
+def thickness_copies(slots, probes, spread):
+    return pl.pallas_call(
+        functools.partial(thickness_kernel, slots),
+        name="thickness",
+        grid=(1,),
+        out_shape=jax.ShapeDtypeStruct((slots, 48, 128), jnp.float32),
+        in_specs=[
+            pl.BlockSpec((PROBES, 1, 1, 6, 8, 64), lambda i: (0, 2, 0, 0, 0, 0)),
+            pl.BlockSpec((1, 1, 6, 8, 64), lambda i: (2, 0, 0, 0, 0)),
+        ],
+        out_specs=pl.BlockSpec((slots, 48, 128), lambda i: (0, 0, 0)),
+        interpret=INTERPRET,
+    )(probes, spread)
+
+
+def exchange(kind, nt, nq, links, strips, top, bottom):
     sources, x_targets, y_targets = TABLES[kind]
     codes = jnp.asarray(codes_of(sources, x_targets, y_targets))
     picks = jnp.asarray(picks_of(sources, y_targets))
     gathered = lax.all_gather(strips, "ty", axis=0)
-    slots, swap_a, swap_b, local, halos = call(
+    slots, local, halos = call(
         functools.partial(route_kernel, nt, nq),
-        (place, links),
+        "route_" + kind,
+        (links,),
         (gathered, top, bottom, codes, picks),
-        ((nt, 8, 128), (32, 128), (32, 128), (32, 128), (16, 64)),
-    )
-    near = [(i, i ^ 1) for i in range(nt)]
-    wrapped = [(i, (i + 1 if i % 2 else i - 1) % nt) for i in range(nt)]
-    swapped_a = lax.ppermute(swap_a, "tx", near)
-    swapped_b = lax.ppermute(swap_b, "tx", wrapped)
+        ((nt, 40, 128), (32, 128), (16, 64)),
+    )
     arrived = lax.all_to_all(slots, "tx", 0, 0, tiled=True)
-    return arrived, swapped_a, swapped_b, local, halos
-
-
-def body(probes, wind, mass, heat, spread, misfit, face_links):
+    return arrived, local, halos
+
+
+def body(probes, wind, mass, heat, spread, misfit, links):
     nf, nt, nq = (lax.axis_size(a) for a in ("face", "tx", "ty"))
-    links = face_links.reshape(-1)
-    index = lax.broadcasted_iota(jnp.int32, (3,), 0)
-    place = jnp.where(
-        index == 0,
-        lax.axis_index("face"),
-        jnp.where(index == 1, lax.axis_index("tx"), lax.axis_index("ty")),
-    )
-    (sent,) = call(functools.partial(thickness_kernel, nf), (), (probes, spread), ((nf, 48, 128),))
+    sent = thickness_copies(nf, probes, spread)
     totals = lax.all_to_all(sent, "face", 0, 0, tiled=True)
     fields, strips, top, bottom = call(
         functools.partial(fields_kernel, nf),
-        (place,),
+        "fields",
+        (),
         (probes, spread, wind, mass, heat, totals),
         ((36, 8, 128), (STRIP, 128), (32, 128), (32, 128)),
     )
-    outer = exchange("forward", nt, nq, place, links, strips, top, bottom)
+    outer = exchange("forward", nt, nq, links, strips, top, bottom)
     costs, strips, top, bottom = call(
         functools.partial(image_kernel, nt, nq),
-        (place, links),
+        "image",
+        (links,),
         (*outer, fields, probes, spread, wind, misfit),
         ((24, 8, 128), (STRIP, 128), (32, 128), (32, 128)),
     )
-    outer = exchange("adjoint", nt, nq, place, links, strips, top, bottom)
+    outer = exchange("adjoint", nt, nq, links, strips, top, bottom)
     backs, loads = call(
         functools.partial(adjoint_kernel, nt, nq, nf),
-        (place, links),
+        "adjoint",
+        (links,),
         (*outer, costs, wind, mass, heat),
         ((24, 8, 128), (nf, 48, 128)),
     )
     loads = lax.all_to_all(loads, "face", 0, 0, tiled=True)
     (applied,) = call(
         functools.partial(final_kernel, nf),
-        (place,),
+        "final",
+        (),
         (probes, spread, backs, loads),
         (probes.shape,),
     )

time: 114 us -> 126 us (1.11)
  the two profiles are of different devices: /device:TPU:2 before, /device:TPU:4 now
where the time goes in v2:
time: 126 us; the launch traced here: 125 us
  blocking collectives  116 us (92%)
  Pallas kernels  8.57 us (7%)
    all_to_all x2, blocking collectives, exchange(): arrived = lax.all_to_all(slots, 'tx', 0, 0, tiled=True)  74.5 us
    all_to_all x1, blocking collectives, body(): totals = lax.all_to_all(sent, 'face', 0, 0, tiled=True)  18.2 us
    all_to_all x1, blocking collectives, body(): loads = lax.all_to_all(loads, 'face', 0, 0, tiled=True)  12.6 us
    all_gather x2, blocking collectives, exchange(): gathered = lax.all_gather(strips, 'ty', axis=0)  11.2 us
    pallas_call x6, Pallas kernels, call(): pl.pallas_call(kernel, name=name, out_shape=shapes, in_specs=[SMEM] * len...  7.01 us

profile of v2, /device:TPU:4, one launch (start us, length us, event | category | flops | bytes accessed | tf_op | source)
XLA Modules:
  0.0 125.2 jit_solution(10091015359408617076)
XLA Ops:
  0.0 1.6 %thickness.1 = f32[8,48,128]{2,1,0:T(8,128)} custom-call(f32[2,4,1,6,8,64]{5,4,3,2,1,0:T(8,128)} %probes.7, f32[4,1,6,8,64]{4,3,2,1,0:T(8,128)} %spread.7), custom_call_target="tpu_custom_call" | custom-call | tf_op jit(solution)/shard_map/thickness/pallas_call | solution.py:494
  1.6 0.0 copy-start
  1.6 0.0 copy-start.1
  1.6 0.0 copy-start.2
  1.6 0.0 copy-start.6
  1.6 0.0 copy-start.7
  1.6 18.2 %all_to_all.20.totals = f32[8,48,128]{2,1,0:T(8,128)S(1)} all-to-all(f32[8,48,128]{2,1,0:T(8,128)} %thickness.1), channel_id=1, replica_groups=mesh['face'=8,'tx'=32,'ty'=4] {'face'}, dimensions={0} | all-to-all | bytes 393216 | tf_op jit(solution)/shard_map/all_to_all | solution.py:527
  19.8 0.0 copy-done
  19.8 0.0 copy-done.1
  19.8 0.0 copy-done.2
  19.8 0.0 copy-done.6
  19.8 0.0 copy-done.7
  19.8 0.0 copy-start.4
  19.8 0.2 fields.1
  20.1 0.0 copy-start.5
  20.1 0.0 copy-start.10
  20.1 5.6 %all-gather = f32[288,128]{1,0:T(8,128)S(1)} all-gather(f32[72,128]{1,0:T(8,128)S(1)} %get-tuple-element.21), channel_id=2, replica_groups=mesh['face'=8,'tx'=32,'ty'=4] {'ty'}, dimensions={0}, use_global_device_ids=true | all-gather | bytes 184320 | tf_op jit(solution)/shard_map/all_gather | solution.py:512
  25.7 0.0 copy-done.4
  25.7 0.0 copy-done.5
  25.7 0.0 copy-done.10
  25.7 1.7 %route_forward.1 = (f32[32,40,128]{2,1,0:T(8,128)S(1)}, f32[32,128]{1,0:T(8,128)S(1)}, f32[16,64]{1,0:T(8,128)S(1)}) custom-call(s32[6,4,7]{2,1,0:T(4,128)S(1)} %copy-done.5, f32[4,72,128]{2,1,0:T(8,128)S(1)} %bitcast.2, f32[32,128]{1,0:T(8,128)S(1)} %get-tuple-element.22.top, f32[32,128]{1,0:T(8,128)S(1)} %get-tuple-element.23.bottom, ...), custom_call_target="tpu_custom_call" | custom-call | tf_op jit(solution)/shard_map/route_forward/pallas_call | solution.py:482
  27.3 0.0 copy-start.8
  27.4 45.1 %all_to_all.21.arrived = f32[32,40,128]{2,1,0:T(8,128)S(1)} all-to-all(f32[32,40,128]{2,1,0:T(8,128)S(1)} %get-tuple-element.24), channel_id=1, replica_groups=mesh['face'=8,'tx'=32,'ty'=4] {'tx'}, dimensions={0} | all-to-all | bytes 1310720 | tf_op jit(solution)/shard_map/all_to_all | solution.py:520
  72.5 0.0 copy-done.8
  72.5 0.0 copy-start.3
  72.5 1.3 %image.1 = (f32[24,8,128]{2,1,0:T(8,128)S(1)}, f32[72,128]{1,0:T(8,128)S(1)}, f32[32,128]{1,0:T(8,128)S(1)}, f32[32,128]{1,0:T(8,128)S(1)}) custom-call(s32[6,4,7]{2,1,0:T(4,128)S(1)} %copy-done.5, f32[32,40,128]{2,1,0:T(8,128)S(1)} %all_to_all.21.arrived, f32[32,128]{1,0:T(8,128)S(1)} %get-tuple-element.25.local, f32[16,64]{1,0:T(8,128)S(1)} %get-tuple-element.26.halos, ...), custom_call_target="tpu_custom_call" | custom-call | tf_op jit(solution)/shard_map/image/pallas_call | solution.py:482
  73.8 0.0 copy-start.9
  73.8 5.6 %all-gather.1 = f32[288,128]{1,0:T(8,128)S(1)} all-gather(f32[72,128]{1,0:T(8,128)S(1)} %get-tuple-element.28), channel_id=3, replica_groups=mesh['face'=8,'tx'=32,'ty'=4] {'ty'}, dimensions={0}, use_global_device_ids=true | all-gather | bytes 184320 | tf_op jit(solution)/shard_map/all_gather | solution.py:512
  79.4 0.0 copy-done.3
  79.4 0.0 copy-done.9
  79.4 1.7 %route_adjoint.1 = (f32[32,40,128]{2,1,0:T(8,128)S(1)}, f32[32,128]{1,0:T(8,128)S(1)}, f32[16,64]{1,0:T(8,128)S(1)}) custom-call(s32[6,4,7]{2,1,0:T(4,128)S(1)} %copy-done.5, f32[4,72,128]{2,1,0:T(8,128)S(1)} %bitcast.3, f32[32,128]{1,0:T(8,128)S(1)} %get-tuple-element.29.top, f32[32,128]{1,0:T(8,128)S(1)} %get-tuple-element.30.bottom, ...), custom_call_target="tpu_custom_call" | custom-call | tf_op jit(solution)/shard_map/route_adjoint/pallas_call | solution.py:482
  81.1 29.4 %all_to_all.22.arrived = f32[32,40,128]{2,1,0:T(8,128)S(1)} all-to-all(f32[32,40,128]{2,1,0:T(8,128)S(1)} %get-tuple-element.31), channel_id=1, replica_groups=mesh['face'=8,'tx'=32,'ty'=4] {'tx'}, dimensions={0} | all-to-all | bytes 1310720 | tf_op jit(solution)/shard_map/all_to_all | solution.py:520
  110.5 1.3 %adjoint.1 = (f32[24,8,128]{2,1,0:T(8,128)S(1)}, f32[8,48,128]{2,1,0:T(8,128)S(1)}) custom-call(s32[6,4,7]{2,1,0:T(4,128)S(1)} %copy-done.5, f32[32,40,128]{2,1,0:T(8,128)S(1)} %all_to_all.22.arrived, f32[32,128]{1,0:T(8,128)S(1)} %get-tuple-element.32.local, f32[16,64]{1,0:T(8,128)S(1)} %get-tuple-element.33.halos, ...), custom_call_target="tpu_custom_call" | custom-call | tf_op jit(solution)/shard_map/adjoint/pallas_call | solution.py:482
  111.8 12.6 %all_to_all.23.loads = f32[8,48,128]{2,1,0:T(8,128)S(1)} all-to-all(f32[8,48,128]{2,1,0:T(8,128)S(1)} %get-tuple-element.36), channel_id=1, replica_groups=mesh['face'=8,'tx'=32,'ty'=4] {'face'}, dimensions={0} | all-to-all | bytes 393216 | tf_op jit(solution)/shard_map/all_to_all | solution.py:551
  124.4 0.8 final.1
Async XLA Ops:
  1.6 18.2 %copy-start = (f32[2,4,1,6,8,64]{5,4,3,2,1,0:T(8,128)S(1)}, f32[2,4,1,6,8,64]{5,4,3,2,1,0:T(8,128)}, u32[]{:S(2)}) copy-start(f32[2,4,1,6,8,64]{5,4,3,2,1,0:T(8,128)} %probes.7) | copy-start | bytes 294916
  1.6 18.2 %copy-start.1 = (f32[4,1,6,8,64]{4,3,2,1,0:T(8,128)S(1)}, f32[4,1,6,8,64]{4,3,2,1,0:T(8,128)}, u32[]{:S(2)}) copy-start(f32[4,1,6,8,64]{4,3,2,1,0:T(8,128)} %spread.7) | copy-start | bytes 147460
  1.6 18.2 %copy-start.2 = (f32[2,1,6,8,64]{4,3,2,1,0:T(8,128)S(1)}, f32[2,1,6,8,64]{4,3,2,1,0:T(8,128)}, u32[]{:S(2)}) copy-start(f32[2,1,6,8,64]{4,3,2,1,0:T(8,128)} %wind.5) | copy-start | bytes 73732
  1.6 18.2 %copy-start.6 = (f32[1,6,8,64]{3,2,1,0:T(8,128)S(1)}, f32[1,6,8,64]{3,2,1,0:T(8,128)}, u32[]{:S(2)}) copy-start(f32[1,6,8,64]{3,2,1,0:T(8,128)} %mass.3) | copy-start | bytes 36868
  1.6 18.2 %copy-start.7 = (f32[1,6,8,64]{3,2,1,0:T(8,128)S(1)}, f32[1,6,8,64]{3,2,1,0:T(8,128)}, u32[]{:S(2)}) copy-start(f32[1,6,8,64]{3,2,1,0:T(8,128)} %heat.3) | copy-start | bytes 36868
  19.8 5.9 %copy-start.4 = (f32[5,128,64]{2,1,0:T(8,128)S(1)}, f32[5,128,64]{2,1,0:T(8,128)}, u32[]{:S(2)}) copy-start(f32[5,128,64]{2,1,0:T(8,128)} %constant.8.clone.codes) | copy-start | bytes 491524
  20.1 5.6 %copy-start.5 = (s32[6,4,7]{2,1,0:T(4,128)S(1)}, s32[6,4,7]{2,1,0:T(4,128)}, u32[]{:S(2)}) copy-start(s32[6,4,7]{2,1,0:T(4,128)} %links.7) | copy-start | bytes 2020
  20.1 5.6 %copy-start.10 = (f32[128,64]{1,0:T(8,128)S(1)}, f32[128,64]{1,0:T(8,128)}, u32[]{:S(2)}) copy-start(f32[128,64]{1,0:T(8,128)} %constant.9.clone.picks) | copy-start | bytes 98308
  27.3 45.1 %copy-start.8 = (f32[4,1,6,8,64]{4,3,2,1,0:T(8,128)S(1)}, f32[4,1,6,8,64]{4,3,2,1,0:T(8,128)}, u32[]{:S(2)}) copy-start(f32[4,1,6,8,64]{4,3,2,1,0:T(8,128)} %misfit.1) | copy-start | bytes 147460
  72.5 7.0 %copy-start.3 = (f32[5,128,64]{2,1,0:T(8,128)S(1)}, f32[5,128,64]{2,1,0:T(8,128)}, u32[]{:S(2)}) copy-start(f32[5,128,64]{2,1,0:T(8,128)} %constant.10.clone.codes) | copy-start | bytes 491524
  73.8 5.6 %copy-start.9 = (f32[128,64]{1,0:T(8,128)S(1)}, f32[128,64]{1,0:T(8,128)}, u32[]{:S(2)}) copy-start(f32[128,64]{1,0:T(8,128)} %constant.11.clone.picks) | copy-start | bytes 98308

commit v3 on v2

--- a/solution.py
+++ b/solution.py
@@ -251,7 +251,9 @@
     )
 
 
-def route_kernel(nt, nq, links, gathered, top, bottom, codes, picks, slots, local, halos):
+def route_kernel(
+    nt, nq, links, gathered, top, bottom, codes, picks, slots, swap_a, swap_b, local, halos
+):
     tile_row, tile_column = lax.axis_index("tx"), lax.axis_index("ty")
     is_first, is_last = tile_row == 0, tile_row == nt - 1
     line_f = jnp.where(is_first, 0.0, 1.0)
@@ -307,7 +309,7 @@
         left = pieces[q][at : at + 8]
         left = left + jnp.where(tile_row == t, straight, 0.0)
         left = left + jnp.where(tile_row == nt - 1 - t, flipped, 0.0)
-        slots[t, 0:8] = joined(left, to_rows[1] if t == nt - 1 else to_rows[0])
+        slots[t] = joined(left, to_rows[1] if t == nt - 1 else to_rows[0])
 
     plain0, turned0 = masks(0, line_f)
     plain1, turned1 = masks(1, line_f)
@@ -319,8 +321,11 @@
     )
     by_row = [joined(by_row[k : k + 32], by_row[k + 32 : k + 64]) for k in (0, 64)]
     local[...] = jnp.where(is_first, by_row[0], by_row[1])
-    slots[lax.rem(tile_row + nt - 1, nt), 8:40] = jnp.where(is_first, by_row[1], top[...])
-    slots[lax.rem(tile_row + 1, nt), 8:40] = jnp.where(is_last, by_row[0], bottom[...])
+    to_lower = jnp.where(is_first, by_row[1], top[...])
+    to_upper = jnp.where(is_last, by_row[0], bottom[...])
+    even = lax.rem(tile_row, 2) == 0
+    swap_a[...] = jnp.where(even, to_upper, to_lower)
+    swap_b[...] = jnp.where(even, to_lower, to_upper)
 
     below = gathered[jnp.maximum(tile_column - 1, 0), 8:16]
     above = gathered[jnp.minimum(tile_column + 1, nq - 1), 0:8]
@@ -329,40 +334,46 @@
     halos[8:16] = jnp.where(tile_column < nq - 1, near[8:16], 0.0)
 
 
-def outer_values(nt, nq, links, arrived, local, halos):
+def collect_kernel(nt, nq, links, arrived, local, halos, sides, row_out):
     tile_row, tile_column = lax.axis_index("tx"), lax.axis_index("ty")
     is_first, is_last = tile_row == 0, tile_row == nt - 1
-    column = arrived[0, 0:8]
+    column = arrived[0]
     for t in range(1, nt):
-        column = column + arrived[t, 0:8]
+        column = column + arrived[t]
     column = column[:, 0:64]
-    south = halos[0:8] + jnp.where(tile_column == 0, column, 0.0)
-    north = halos[8:16] + jnp.where(tile_column == nq - 1, column, 0.0)
     lane = lanes((8, 128))
 
     def spread_out(narrow):
         wide = joined(narrow, narrow)
         return jnp.where(lane < 32, wide, pltpu.roll(wide, 32, 1))
 
-    mine = arrived[pl.ds(tile_column * 8, 8), 0:8].reshape(64, 128)[:, 64:128]
-    mirrored = arrived[pl.ds((nq - 1 - tile_column) * 8, 8), 0:8].reshape(64, 128)[:, 64:128]
+    sides[0:8] = spread_out(halos[0:8] + jnp.where(tile_column == 0, column, 0.0))
+    sides[8:16] = spread_out(halos[8:16] + jnp.where(tile_column == nq - 1, column, 0.0))
+    mine = arrived[pl.ds(tile_column * 8, 8)].reshape(64, 128)[:, 64:128]
+    mirrored = arrived[pl.ds((nq - 1 - tile_column) * 8, 8)].reshape(64, 128)[:, 64:128]
     flip = link_lanes(links, jnp.where(is_first, 0, 1), 2)
     row = moved(parts(jnp.where(flip != 1.0, mine, 0.0)), identity(64), (0, 0)) + moved(
         parts(jnp.where(flip == 1.0, mirrored, 0.0)), reversal(64), (0, 0)
     )
-    row = joined(row[0:32], row[32:64]) + local[...]
-    west = arrived[lax.rem(tile_row + nt - 1, nt), 8:40] + jnp.where(is_first, row, 0.0)
-    east = arrived[lax.rem(tile_row + 1, nt), 8:40] + jnp.where(is_last, row, 0.0)
-    return west, east, spread_out(south), spread_out(north)
+    row_out[...] = joined(row[0:32], row[32:64]) + local[...]
+
+
+def outer_values(nt, sides, row, swapped_a, swapped_b):
+    tile_row = lax.axis_index("tx")
+    even = lax.rem(tile_row, 2) == 0
+    west = jnp.where(even, swapped_b[...], swapped_a[...])
+    east = jnp.where(even, swapped_a[...], swapped_b[...])
+    west = west + jnp.where(tile_row == 0, row[...], 0.0)
+    east = east + jnp.where(tile_row == nt - 1, row[...], 0.0)
+    return west, east, sides[0:8], sides[8:16]
 
 
 def image_kernel(
     nt,
-    nq,
-    links,
-    arrived,
-    local,
-    halos,
+    sides,
+    row,
+    swapped_a,
+    swapped_b,
     fields,
     probes,
     spread,
@@ -373,7 +384,7 @@
     top,
     bottom,
 ):
-    west, east, south, north = outer_values(nt, nq, links, arrived, local, halos)
+    west, east, south, north = outer_values(nt, sides, row, swapped_a, swapped_b)
     planes = {}
     for pp in range(3):
         u = pair(wind, (0, 0), pp)
@@ -410,12 +421,11 @@
 
 def adjoint_kernel(
     nt,
-    nq,
     levels,
-    links,
-    arrived,
-    local,
-    halos,
+    sides,
+    row,
+    swapped_a,
+    swapped_b,
     costs,
     wind,
     mass,
@@ -423,7 +433,7 @@
     backs,
     loads,
 ):
-    west, east, south, north = outer_values(nt, nq, links, arrived, local, halos)
+    west, east, south, north = outer_values(nt, sides, row, swapped_a, swapped_b)
     for pp in range(3):
         u = pair(wind, (0, 0), pp)
         v = pair(wind, (1, 0), pp)
@@ -477,11 +487,10 @@
 GRANT = 8 << 20
 
 
-def call(kernel, name, small, operands, shapes):
+def call(kernel, small, operands, shapes):
     shapes = [jax.ShapeDtypeStruct(s, jnp.float32) for s in shapes]
     return pl.pallas_call(
         kernel,
-        name=name,
         out_shape=shapes,
         in_specs=[SMEM] * len(small) + [VMEM] * len(operands),
         out_specs=[VMEM] * len(shapes),
@@ -510,15 +519,24 @@
     codes = jnp.asarray(codes_of(sources, x_targets, y_targets))
     picks = jnp.asarray(picks_of(sources, y_targets))
     gathered = lax.all_gather(strips, "ty", axis=0)
-    slots, local, halos = call(
+    slots, swap_a, swap_b, local, halos = call(
         functools.partial(route_kernel, nt, nq),
-        "route_" + kind,
         (links,),
         (gathered, top, bottom, codes, picks),
-        ((nt, 40, 128), (32, 128), (16, 64)),
-    )
+        ((nt, 8, 128), (32, 128), (32, 128), (32, 128), (16, 64)),
+    )
+    near = [(i, i ^ 1) for i in range(nt)]
+    wrapped = [(i, (i + 1 if i % 2 else i - 1) % nt) for i in range(nt)]
+    swapped_a = lax.ppermute(swap_a, "tx", near)
+    swapped_b = lax.ppermute(swap_b, "tx", wrapped)
     arrived = lax.all_to_all(slots, "tx", 0, 0, tiled=True)
-    return arrived, local, halos
+    sides, row = call(
+        functools.partial(collect_kernel, nt, nq),
+        (links,),
+        (arrived, local, halos),
+        ((16, 128), (32, 128)),
+    )
+    return sides, row, swapped_a, swapped_b
 
 
 def body(probes, wind, mass, heat, spread, misfit, links):
@@ -527,34 +545,27 @@
     totals = lax.all_to_all(sent, "face", 0, 0, tiled=True)
     fields, strips, top, bottom = call(
         functools.partial(fields_kernel, nf),
-        "fields",
         (),
         (probes, spread, wind, mass, heat, totals),
         ((36, 8, 128), (STRIP, 128), (32, 128), (32, 128)),
     )
     outer = exchange("forward", nt, nq, links, strips, top, bottom)
     costs, strips, top, bottom = call(
-        functools.partial(image_kernel, nt, nq),
-        "image",
-        (links,),
+        functools.partial(image_kernel, nt),
+        (),
         (*outer, fields, probes, spread, wind, misfit),
         ((24, 8, 128), (STRIP, 128), (32, 128), (32, 128)),
     )
     outer = exchange("adjoint", nt, nq, links, strips, top, bottom)
     backs, loads = call(
-        functools.partial(adjoint_kernel, nt, nq, nf),
-        "adjoint",
-        (links,),
+        functools.partial(adjoint_kernel, nt, nf),
+        (),
         (*outer, costs, wind, mass, heat),
         ((24, 8, 128), (nf, 48, 128)),
     )
     loads = lax.all_to_all(loads, "face", 0, 0, tiled=True)
     (applied,) = call(
-        functools.partial(final_kernel, nf),
-        "final",
-        (),
-        (probes, spread, backs, loads),
-        (probes.shape,),
+        functools.partial(final_kernel, nf), (), (probes, spread, backs, loads), (probes.shape,)
     )
     return applied
 

time: 126 us -> 109 us (0.87)
  the two profiles are of different devices: /device:TPU:4 before, /device:TPU:2 now
where the time goes in v3:
time: 109 us
  starting transfers between devices  48.3 us (44%)
  blocking collectives  47.9 us (44%)
  Pallas kernels  10.1 us (9%)
  waiting for transfers between devices  2.13 us (2%)
    all_to_all x2, starting transfers between devices, exchange(): arrived = lax.all_to_all(slots, 'tx', 0, 0, tiled=True)  23.7 us
    all_to_all x1, blocking collectives, body(): totals = lax.all_to_all(sent, 'face', 0, 0, tiled=True)  18.2 us
    all_gather x2, blocking collectives, exchange(): gathered = lax.all_gather(strips, 'ty', axis=0)  17.6 us
    ppermute x2, starting transfers between devices, exchange(): swapped_b = lax.ppermute(swap_b, 'tx', wrapped)  15.4 us
    all_to_all x1, blocking collectives, body(): loads = lax.all_to_all(loads, 'face', 0, 0, tiled=True)  12.2 us
    ppermute x2, starting transfers between devices, exchange(): swapped_a = lax.ppermute(swap_a, 'tx', near)  9.33 us
    pallas_call x8, Pallas kernels, call(): pl.pallas_call(kernel, out_shape=shapes, in_specs=[SMEM] * len(small) + [...  8.54 us
  transfers between devices with their start and end apart: 6, of which 4 were waited for; matrix products, arithmetic and copies ran while one was open for 0% of the time, Pallas kernels for 2%

profile of v3, /device:TPU:2, one launch (start us, length us, event | category | flops | bytes accessed | tf_op | source)
XLA Modules:
  0.0 108.7 jit_solution(9704911185820839026)
XLA Ops:
  0.0 1.6 %thickness.1 = f32[8,48,128]{2,1,0:T(8,128)} custom-call(f32[2,4,1,6,8,64]{5,4,3,2,1,0:T(8,128)} %probes.7, f32[4,1,6,8,64]{4,3,2,1,0:T(8,128)} %spread.7), custom_call_target="tpu_custom_call" | custom-call | tf_op jit(solution)/shard_map/thickness/pallas_call | solution.py:503
  1.6 0.0 copy-start
  1.6 0.0 copy-start.1
  1.6 0.0 copy-start.2
  1.6 0.0 copy-start.7
  1.6 0.0 copy-start.8
  1.6 18.2 %all_to_all.20.totals = f32[8,48,128]{2,1,0:T(8,128)S(1)} all-to-all(f32[8,48,128]{2,1,0:T(8,128)} %thickness.1), channel_id=1, replica_groups=mesh['face'=8,'tx'=32,'ty'=4] {'face'}, dimensions={0} | all-to-all | bytes 393216 | tf_op jit(solution)/shard_map/all_to_all | solution.py:545
  19.8 0.0 copy-done
  19.8 0.0 copy-done.1
  19.8 0.0 copy-done.2
  19.8 0.0 copy-done.7
  19.8 0.0 copy-done.8
  19.8 0.0 copy-start.4
  19.8 0.2 shard_map.109
  20.1 0.0 copy-start.5
  20.1 0.0 copy-start.10
  20.1 12.0 %all-gather = f32[288,128]{1,0:T(8,128)S(1)} all-gather(f32[72,128]{1,0:T(8,128)S(1)} %get-tuple-element.29), channel_id=2, replica_groups=mesh['face'=8,'tx'=32,'ty'=4] {'ty'}, dimensions={0}, use_global_device_ids=true | all-gather | bytes 184320 | tf_op jit(solution)/shard_map/all_gather | solution.py:521
  32.0 0.0 copy-done.4
  32.0 0.0 copy-done.5
  32.0 0.0 copy-done.10
  32.1 2.3 %shard_map.110 = (f32[32,8,128]{2,1,0:T(8,128)}, f32[32,128]{1,0:T(8,128)S(1)}, f32[32,128]{1,0:T(8,128)S(1)}, f32[32,128]{1,0:T(8,128)S(1)}, f32[16,64]{1,0:T(8,128)S(1)}) custom-call(s32[6,4,7]{2,1,0:T(4,128)S(1)} %copy-done.5, f32[4,72,128]{2,1,0:T(8,128)S(1)} %bitcast.2, f32[32,128]{1,0:T(8,128)S(1)} %get-tuple-element.30.top, ...), custom_call_target="tpu_custom_call" | custom-call | tf_op jit(solution)/shard_map/pallas_call | solution.py:492
  34.4 14.7 %all-to-all-start.1 = ((f32[32,8,128]{2,1,0:T(8,128)}), f32[32,8,128]{2,1,0:T(8,128)S(1)}, u32[]{:S(2)}, u32[]{:S(2)}) async-start(f32[32,8,128]{2,1,0:T(8,128)} %get-tuple-element.32), calls=%async_computation.1 | async-start | bytes 262144 | tf_op jit(solution)/shard_map/all_to_all | solution.py:532
  49.1 0.0 copy-start.6
  49.1 4.7 %collective-permute-start = (f32[32,128]{1,0:T(8,128)S(1)}, f32[32,128]{1,0:T(8,128)S(1)}, u32[]{:S(2)}, u32[]{:S(2)}) collective-permute-start(f32[32,128]{1,0:T(8,128)S(1)} %get-tuple-element.37), channel_id=1, source_target_pairs={{0,4},{4,0},{8,12},{12,8},{16,20},{20,16},{24,28},{28,24},{32,36},... | collective-permute-start | bytes 49160 | tf_op jit(solution)/shard_map/ppermute | solution.py:530
  53.9 7.7 %collective-permute-start.1 = (f32[32,128]{1,0:T(8,128)S(1)}, f32[32,128]{1,0:T(8,128)S(1)}, u32[]{:S(2)}, u32[]{:S(2)}) collective-permute-start(f32[32,128]{1,0:T(8,128)S(1)} %get-tuple-element.38), channel_id=1, source_target_pairs={{0,124},{4,8},{8,4},{12,16},{16,12},{20,24},{24,20},{28,32},{32,28... | collective-permute-start | bytes 49160 | tf_op jit(solution)/shard_map/ppermute | solution.py:531
  61.5 0.3 all-to-all-done.1.arrived
  61.9 1.1 %shard_map.111 = (f32[16,128]{1,0:T(8,128)S(1)}, f32[32,128]{1,0:T(8,128)S(1)}) custom-call(s32[6,4,7]{2,1,0:T(4,128)S(1)} %copy-done.5, f32[32,8,128]{2,1,0:T(8,128)S(1)} %all-to-all-done.1.arrived, f32[32,128]{1,0:T(8,128)S(1)} %get-tuple-element.33.local, f32[16,64]{1,0:T(8,128)S(1)} %get-tuple-element.34.halos), custom_call_target="tpu_custom_call" | custom-call | tf_op jit(solution)/shard_map/pallas_call | solution.py:492
  63.0 0.0 collective-permute-done.swapped_a
  63.0 0.7 collective-permute-done.1.swapped_b
  63.7 0.0 copy-done.6
  63.7 0.0 copy-start.3
  63.7 0.4 shard_map.112
  64.1 0.0 copy-start.9
  64.1 5.6 %all-gather.1 = f32[288,128]{1,0:T(8,128)S(1)} all-gather(f32[72,128]{1,0:T(8,128)S(1)} %get-tuple-element.40), channel_id=3, replica_groups=mesh['face'=8,'tx'=32,'ty'=4] {'ty'}, dimensions={0}, use_global_device_ids=true | all-gather | bytes 184320 | tf_op jit(solution)/shard_map/all_gather | solution.py:521
  69.7 0.0 copy-done.3
  69.7 0.0 copy-done.9
  69.7 2.3 %shard_map.113 = (f32[32,8,128]{2,1,0:T(8,128)}, f32[32,128]{1,0:T(8,128)S(1)}, f32[32,128]{1,0:T(8,128)S(1)}, f32[32,128]{1,0:T(8,128)S(1)}, f32[16,64]{1,0:T(8,128)S(1)}) custom-call(s32[6,4,7]{2,1,0:T(4,128)S(1)} %copy-done.5, f32[4,72,128]{2,1,0:T(8,128)S(1)} %bitcast.3, f32[32,128]{1,0:T(8,128)S(1)} %get-tuple-element.41.top, ...), custom_call_target="tpu_custom_call" | custom-call | tf_op jit(solution)/shard_map/pallas_call | solution.py:492
  72.1 8.9 %all-to-all-start.2 = ((f32[32,8,128]{2,1,0:T(8,128)}), f32[32,8,128]{2,1,0:T(8,128)S(1)}, u32[]{:S(2)}, u32[]{:S(2)}) async-start(f32[32,8,128]{2,1,0:T(8,128)} %get-tuple-element.43), calls=%async_computation.2 | async-start | bytes 262144 | tf_op jit(solution)/shard_map/all_to_all | solution.py:532
  81.0 4.6 %collective-permute-start.2 = (f32[32,128]{1,0:T(8,128)S(1)}, f32[32,128]{1,0:T(8,128)S(1)}, u32[]{:S(2)}, u32[]{:S(2)}) collective-permute-start(f32[32,128]{1,0:T(8,128)S(1)} %get-tuple-element.48), channel_id=1, source_target_pairs={{0,4},{4,0},{8,12},{12,8},{16,20},{20,16},{24,28},{28,24},{32,36},... | collective-permute-start | bytes 49160 | tf_op jit(solution)/shard_map/ppermute | solution.py:530
  85.6 7.7 %collective-permute-start.3 = (f32[32,128]{1,0:T(8,128)S(1)}, f32[32,128]{1,0:T(8,128)S(1)}, u32[]{:S(2)}, u32[]{:S(2)}) collective-permute-start(f32[32,128]{1,0:T(8,128)S(1)} %get-tuple-element.49), channel_id=1, source_target_pairs={{0,124},{4,8},{8,4},{12,16},{16,12},{20,24},{24,20},{28,32},{32,28... | collective-permute-start | bytes 49160 | tf_op jit(solution)/shard_map/ppermute | solution.py:531
  93.3 0.5 all-to-all-done.2.arrived
  93.8 1.1 %shard_map.114 = (f32[16,128]{1,0:T(8,128)S(1)}, f32[32,128]{1,0:T(8,128)S(1)}) custom-call(s32[6,4,7]{2,1,0:T(4,128)S(1)} %copy-done.5, f32[32,8,128]{2,1,0:T(8,128)S(1)} %all-to-all-done.2.arrived, f32[32,128]{1,0:T(8,128)S(1)} %get-tuple-element.44.local, f32[16,64]{1,0:T(8,128)S(1)} %get-tuple-element.45.halos), custom_call_target="tpu_custom_call" | custom-call | tf_op jit(solution)/shard_map/pallas_call | solution.py:492
  94.9 0.0 collective-permute-done.2.swapped_a
  94.9 0.6 collective-permute-done.3.swapped_b
  95.5 0.2 shard_map.115
  95.7 12.2 %all_to_all.21.loads = f32[8,48,128]{2,1,0:T(8,128)S(1)} all-to-all(f32[8,48,128]{2,1,0:T(8,128)S(1)} %get-tuple-element.52), channel_id=1, replica_groups=mesh['face'=8,'tx'=32,'ty'=4] {'face'}, dimensions={0} | all-to-all | bytes 393216 | tf_op jit(solution)/shard_map/all_to_all | solution.py:566
  107.9 0.8 shard_map.116
Async XLA Ops:
  1.6 18.2 %copy-start = (f32[2,4,1,6,8,64]{5,4,3,2,1,0:T(8,128)S(1)}, f32[2,4,1,6,8,64]{5,4,3,2,1,0:T(8,128)}, u32[]{:S(2)}) copy-start(f32[2,4,1,6,8,64]{5,4,3,2,1,0:T(8,128)} %probes.7) | copy-start | bytes 294916
  1.6 18.2 %copy-start.1 = (f32[4,1,6,8,64]{4,3,2,1,0:T(8,128)S(1)}, f32[4,1,6,8,64]{4,3,2,1,0:T(8,128)}, u32[]{:S(2)}) copy-start(f32[4,1,6,8,64]{4,3,2,1,0:T(8,128)} %spread.7) | copy-start | bytes 147460
  1.6 18.2 %copy-start.2 = (f32[2,1,6,8,64]{4,3,2,1,0:T(8,128)S(1)}, f32[2,1,6,8,64]{4,3,2,1,0:T(8,128)}, u32[]{:S(2)}) copy-start(f32[2,1,6,8,64]{4,3,2,1,0:T(8,128)} %wind.5) | copy-start | bytes 73732
  1.6 18.2 %copy-start.7 = (f32[1,6,8,64]{3,2,1,0:T(8,128)S(1)}, f32[1,6,8,64]{3,2,1,0:T(8,128)}, u32[]{:S(2)}) copy-start(f32[1,6,8,64]{3,2,1,0:T(8,128)} %mass.3) | copy-start | bytes 36868
  1.6 18.2 %copy-start.8 = (f32[1,6,8,64]{3,2,1,0:T(8,128)S(1)}, f32[1,6,8,64]{3,2,1,0:T(8,128)}, u32[]{:S(2)}) copy-start(f32[1,6,8,64]{3,2,1,0:T(8,128)} %heat.3) | copy-start | bytes 36868
  19.8 12.3 %copy-start.4 = (f32[5,128,64]{2,1,0:T(8,128)S(1)}, f32[5,128,64]{2,1,0:T(8,128)}, u32[]{:S(2)}) copy-start(f32[5,128,64]{2,1,0:T(8,128)} %constant.8.clone.codes) | copy-start | bytes 491524
  20.1 12.0 %copy-start.5 = (s32[6,4,7]{2,1,0:T(4,128)S(1)}, s32[6,4,7]{2,1,0:T(4,128)}, u32[]{:S(2)}) copy-start(s32[6,4,7]{2,1,0:T(4,128)} %links.7) | copy-start | bytes 2020
  20.1 12.0 %copy-start.10 = (f32[128,64]{1,0:T(8,128)S(1)}, f32[128,64]{1,0:T(8,128)}, u32[]{:S(2)}) copy-start(f32[128,64]{1,0:T(8,128)} %constant.9.clone.picks) | copy-start | bytes 98308
  34.4 27.5 %all-to-all-start.1 = ((f32[32,8,128]{2,1,0:T(8,128)}), f32[32,8,128]{2,1,0:T(8,128)S(1)}, u32[]{:S(2)}, u32[]{:S(2)}) async-start(f32[32,8,128]{2,1,0:T(8,128)} %get-tuple-element.32), calls=%async_computation.1 | async-start | bytes 262144 | tf_op jit(solution)/shard_map/all_to_all | solution.py:532
  49.1 14.6 %copy-start.6 = (f32[4,1,6,8,64]{4,3,2,1,0:T(8,128)S(1)}, f32[4,1,6,8,64]{4,3,2,1,0:T(8,128)}, u32[]{:S(2)}) copy-start(f32[4,1,6,8,64]{4,3,2,1,0:T(8,128)} %misfit.1) | copy-start | bytes 147460
  49.1 13.8 %collective-permute-start = (f32[32,128]{1,0:T(8,128)S(1)}, f32[32,128]{1,0:T(8,128)S(1)}, u32[]{:S(2)}, u32[]{:S(2)}) collective-permute-start(f32[32,128]{1,0:T(8,128)S(1)} %get-tuple-element.37), channel_id=1, source_target_pairs={{0,4},{4,0},{8,12},{12,8},{16,20},{20,16},{24,28},{28,24},{32,36},... | collective-permute-start | bytes 49160 | tf_op jit(solution)/shard_map/ppermute | solution.py:530
  53.9 9.9 %collective-permute-start.1 = (f32[32,128]{1,0:T(8,128)S(1)}, f32[32,128]{1,0:T(8,128)S(1)}, u32[]{:S(2)}, u32[]{:S(2)}) collective-permute-start(f32[32,128]{1,0:T(8,128)S(1)} %get-tuple-element.38), channel_id=1, source_target_pairs={{0,124},{4,8},{8,4},{12,16},{16,12},{20,24},{24,20},{28,32},{32,28... | collective-permute-start | bytes 49160 | tf_op jit(solution)/shard_map/ppermute | solution.py:531
  63.7 6.0 %copy-start.3 = (f32[5,128,64]{2,1,0:T(8,128)S(1)}, f32[5,128,64]{2,1,0:T(8,128)}, u32[]{:S(2)}) copy-start(f32[5,128,64]{2,1,0:T(8,128)} %constant.10.clone.codes) | copy-start | bytes 491524
  64.1 5.6 %copy-start.9 = (f32[128,64]{1,0:T(8,128)S(1)}, f32[128,64]{1,0:T(8,128)}, u32[]{:S(2)}) copy-start(f32[128,64]{1,0:T(8,128)} %constant.11.clone.picks) | copy-start | bytes 98308
  72.1 21.7 %all-to-all-start.2 = ((f32[32,8,128]{2,1,0:T(8,128)}), f32[32,8,128]{2,1,0:T(8,128)S(1)}, u32[]{:S(2)}, u32[]{:S(2)}) async-start(f32[32,8,128]{2,1,0:T(8,128)} %get-tuple-element.43), calls=%async_computation.2 | async-start | bytes 262144 | tf_op jit(solution)/shard_map/all_to_all | solution.py:532
  81.0 13.9 %collective-permute-start.2 = (f32[32,128]{1,0:T(8,128)S(1)}, f32[32,128]{1,0:T(8,128)S(1)}, u32[]{:S(2)}, u32[]{:S(2)}) collective-permute-start(f32[32,128]{1,0:T(8,128)S(1)} %get-tuple-element.48), channel_id=1, source_target_pairs={{0,4},{4,0},{8,12},{12,8},{16,20},{20,16},{24,28},{28,24},{32,36},... | collective-permute-start | bytes 49160 | tf_op jit(solution)/shard_map/ppermute | solution.py:530
  85.6 9.9 %collective-permute-start.3 = (f32[32,128]{1,0:T(8,128)S(1)}, f32[32,128]{1,0:T(8,128)S(1)}, u32[]{:S(2)}, u32[]{:S(2)}) collective-permute-start(f32[32,128]{1,0:T(8,128)S(1)} %get-tuple-element.49), channel_id=1, source_target_pairs={{0,124},{4,8},{8,4},{12,16},{16,12},{20,24},{24,20},{28,32},{32,28... | collective-permute-start | bytes 49160 | tf_op jit(solution)/shard_map/ppermute | solution.py:531

commit v4 on v3

--- a/solution.py
+++ b/solution.py
@@ -144,16 +144,22 @@
     return joined(ref[(*index, 2 * pp)], ref[(*index, 2 * pp + 1)])
 
 
-def link_lanes(links, edge, item):
+def put_table(links, table):
     lane = lanes((1, 64))
     within = jnp.where(lane >= 32, lane - 32, lane)
     third = within - 3 * ((within * 43) // 128)
-    out = jnp.zeros((1, 64), jnp.float32)
-    for f in range(6):
-        value = links[f, edge, item].astype(jnp.float32)
-        here = (third == f // 2) & ((lane >= 32) == (f % 2 == 1))
-        out = jnp.where(here, value, out)
-    return out
+    here = [(third == f // 2) & ((lane >= 32) == (f % 2 == 1)) for f in range(6)]
+    for edge in range(4):
+        for item in range(7):
+            out = jnp.zeros((1, 64), jnp.float32)
+            for f in range(6):
+                out = jnp.where(here[f], links[f, edge, item].astype(jnp.float32), out)
+            table[edge, item : item + 1] = out
+        table[edge, 7:8] = jnp.zeros((1, 64), jnp.float32)
+
+
+def link_lanes(table, edge, item):
+    return table[edge, item : item + 1]
 
 
 def coefficients(links, edge, code_a, code_b, panel):
@@ -184,10 +190,13 @@
     out_ref[16:STRIP] = jnp.concatenate(rows, axis=0)
 
 
-def put_outer_rows(planes, top_ref, bottom_ref):
+def put_outer_rows(planes, near_ref, far_ref):
     spare = [jnp.zeros((32 - len(planes), 128), jnp.float32)]
-    top_ref[...] = jnp.concatenate([p[0:1] for p in planes] + spare, axis=0)
-    bottom_ref[...] = jnp.concatenate([p[7:8] for p in planes] + spare, axis=0)
+    top = jnp.concatenate([p[0:1] for p in planes] + spare, axis=0)
+    bottom = jnp.concatenate([p[7:8] for p in planes] + spare, axis=0)
+    even = lax.rem(lax.axis_index("tx"), 2) == 0
+    near_ref[...] = jnp.where(even, bottom, top)
+    far_ref[...] = jnp.where(even, top, bottom)
 
 
 def slopes_x(plane, b, west, east):
@@ -207,7 +216,8 @@
     return 0.5 * (after - before)
 
 
-def thickness_kernel(slots, probes, spread, out):
+def thickness_kernel(slots, links, probes, spread, out, table):
+    put_table(links, table)
     for probe in range(PROBES):
         for pp in range(3):
             value = pair(spread, (0, 0), pp) * pair(probes, (probe, 0, 0), pp)
@@ -216,7 +226,7 @@
 
 
 def fields_kernel(
-    level_count, probes, spread, wind, mass, heat, totals, fields, strips, top, bottom
+    level_count, probes, spread, wind, mass, heat, totals, fields, strips, near_row, far_row
 ):
     level, tile_row = lax.axis_index("face"), lax.axis_index("tx")
     planes = {}
@@ -246,13 +256,13 @@
     put_strips(ordered, strips, tile_row)
     put_outer_rows(
         [planes[n, pr, pp] for n in FORWARD_X for pr in range(PROBES) for pp in range(3)],
-        top,
-        bottom,
+        near_row,
+        far_row,
     )
 
 
 def route_kernel(
-    nt, nq, links, gathered, top, bottom, codes, picks, slots, swap_a, swap_b, local, halos
+    nt, nq, links, gathered, far_row, codes, picks, slots, swap_b, local, halos
 ):
     tile_row, tile_column = lax.axis_index("tx"), lax.axis_index("ty")
     is_first, is_last = tile_row == 0, tile_row == nt - 1
@@ -321,11 +331,8 @@
     )
     by_row = [joined(by_row[k : k + 32], by_row[k + 32 : k + 64]) for k in (0, 64)]
     local[...] = jnp.where(is_first, by_row[0], by_row[1])
-    to_lower = jnp.where(is_first, by_row[1], top[...])
-    to_upper = jnp.where(is_last, by_row[0], bottom[...])
-    even = lax.rem(tile_row, 2) == 0
-    swap_a[...] = jnp.where(even, to_upper, to_lower)
-    swap_b[...] = jnp.where(even, to_lower, to_upper)
+    sent = jnp.where(is_first, by_row[1], far_row[...])
+    swap_b[...] = jnp.where(is_last, by_row[0], sent)
 
     below = gathered[jnp.maximum(tile_column - 1, 0), 8:16]
     above = gathered[jnp.minimum(tile_column + 1, nq - 1), 0:8]
@@ -381,8 +388,8 @@
     misfit,
     costs,
     strips,
-    top,
-    bottom,
+    near_row,
+    far_row,
 ):
     west, east, south, north = outer_values(nt, sides, row, swapped_a, swapped_b)
     planes = {}
@@ -414,8 +421,8 @@
     )
     put_outer_rows(
         [planes[n, pr, pp] for n in ADJOINT_X for pr in range(PROBES) for pp in range(3)],
-        top,
-        bottom,
+        near_row,
+        far_row,
     )
 
 
@@ -487,53 +494,58 @@
 GRANT = 8 << 20
 
 
-def call(kernel, small, operands, shapes):
+def call(kernel, operands, shapes):
     shapes = [jax.ShapeDtypeStruct(s, jnp.float32) for s in shapes]
     return pl.pallas_call(
         kernel,
         out_shape=shapes,
-        in_specs=[SMEM] * len(small) + [VMEM] * len(operands),
+        in_specs=[VMEM] * len(operands),
         out_specs=[VMEM] * len(shapes),
         compiler_params=pltpu.CompilerParams(vmem_limit_bytes=GRANT),
         interpret=INTERPRET,
-    )(*small, *operands)
-
-
-def thickness_copies(slots, probes, spread):
+    )(*operands)
+
+
+def thickness_copies(slots, links, probes, spread):
     return pl.pallas_call(
         functools.partial(thickness_kernel, slots),
         name="thickness",
         grid=(1,),
-        out_shape=jax.ShapeDtypeStruct((slots, 48, 128), jnp.float32),
+        out_shape=[
+            jax.ShapeDtypeStruct((slots, 48, 128), jnp.float32),
+            jax.ShapeDtypeStruct((4, 8, 64), jnp.float32),
+        ],
         in_specs=[
+            SMEM,
             pl.BlockSpec((PROBES, 1, 1, 6, 8, 64), lambda i: (0, 2, 0, 0, 0, 0)),
             pl.BlockSpec((1, 1, 6, 8, 64), lambda i: (2, 0, 0, 0, 0)),
         ],
-        out_specs=pl.BlockSpec((slots, 48, 128), lambda i: (0, 0, 0)),
+        out_specs=[
+            pl.BlockSpec((slots, 48, 128), lambda i: (0, 0, 0)),
+            pl.BlockSpec((4, 8, 64), lambda i: (0, 0, 0)),
+        ],
         interpret=INTERPRET,
-    )(probes, spread)
-
-
-def exchange(kind, nt, nq, links, strips, top, bottom):
+    )(links, probes, spread)
+
+
+def exchange(kind, nt, nq, table, strips, near_row, far_row):
     sources, x_targets, y_targets = TABLES[kind]
     codes = jnp.asarray(codes_of(sources, x_targets, y_targets))
     picks = jnp.asarray(picks_of(sources, y_targets))
-    gathered = lax.all_gather(strips, "ty", axis=0)
-    slots, swap_a, swap_b, local, halos = call(
-        functools.partial(route_kernel, nt, nq),
-        (links,),
-        (gathered, top, bottom, codes, picks),
-        ((nt, 8, 128), (32, 128), (32, 128), (32, 128), (16, 64)),
-    )
     near = [(i, i ^ 1) for i in range(nt)]
     wrapped = [(i, (i + 1 if i % 2 else i - 1) % nt) for i in range(nt)]
-    swapped_a = lax.ppermute(swap_a, "tx", near)
+    swapped_a = lax.ppermute(near_row, "tx", near)
+    gathered = lax.all_gather(strips, "ty", axis=0)
+    slots, swap_b, local, halos = call(
+        functools.partial(route_kernel, nt, nq),
+        (table, gathered, far_row, codes, picks),
+        ((nt, 8, 128), (32, 128), (32, 128), (16, 64)),
+    )
     swapped_b = lax.ppermute(swap_b, "tx", wrapped)
     arrived = lax.all_to_all(slots, "tx", 0, 0, tiled=True)
     sides, row = call(
         functools.partial(collect_kernel, nt, nq),
-        (links,),
-        (arrived, local, halos),
+        (table, arrived, local, halos),
         ((16, 128), (32, 128)),
     )
     return sides, row, swapped_a, swapped_b
@@ -541,31 +553,28 @@
 
 def body(probes, wind, mass, heat, spread, misfit, links):
     nf, nt, nq = (lax.axis_size(a) for a in ("face", "tx", "ty"))
-    sent = thickness_copies(nf, probes, spread)
+    sent, table = thickness_copies(nf, links, probes, spread)
     totals = lax.all_to_all(sent, "face", 0, 0, tiled=True)
-    fields, strips, top, bottom = call(
+    fields, strips, *rows = call(
         functools.partial(fields_kernel, nf),
-        (),
         (probes, spread, wind, mass, heat, totals),
         ((36, 8, 128), (STRIP, 128), (32, 128), (32, 128)),
     )
-    outer = exchange("forward", nt, nq, links, strips, top, bottom)
-    costs, strips, top, bottom = call(
+    outer = exchange("forward", nt, nq, table, strips, *rows)
+    costs, strips, *rows = call(
         functools.partial(image_kernel, nt),
-        (),
         (*outer, fields, probes, spread, wind, misfit),
         ((24, 8, 128), (STRIP, 128), (32, 128), (32, 128)),
     )
-    outer = exchange("adjoint", nt, nq, links, strips, top, bottom)
+    outer = exchange("adjoint", nt, nq, table, strips, *rows)
     backs, loads = call(
         functools.partial(adjoint_kernel, nt, nf),
-        (),
         (*outer, costs, wind, mass, heat),
         ((24, 8, 128), (nf, 48, 128)),
     )
     loads = lax.all_to_all(loads, "face", 0, 0, tiled=True)
     (applied,) = call(
-        functools.partial(final_kernel, nf), (), (probes, spread, backs, loads), (probes.shape,)
+        functools.partial(final_kernel, nf), (probes, spread, backs, loads), (probes.shape,)
     )
     return applied
 

time: 109 us -> 107 us (0.982)
  Pallas kernels: 10.1 us -> 6.79 us
  waiting for transfers between devices: 2.13 us -> 3.6 us
    pallas_call x8, Pallas kernels: 8.54 us -> 5.16 us  [call(): pl.pallas_call(kernel, out_shape=shapes, in_specs=[VMEM] * len(operands),...]
    ppermute x2, waiting for transfers between devices: 1.3 us -> 2.78 us  [exchange(): swapped_b = lax.ppermute(swap_b, 'tx', wrapped)]
  transfers between devices with their start and end apart: 6 -> 6, of which waited for: 4 -> 4; matrix products, arithmetic and copies ran while one was open for 0% -> 0% of each run, Pallas kernels for 2% -> 1%
where the time goes in v4:
time: 107 us
  starting transfers between devices  48.3 us (45%)
  blocking collectives  47.9 us (45%)
  Pallas kernels  6.79 us (6%)
  waiting for transfers between devices  3.6 us (3%)
    all_to_all x2, starting transfers between devices, exchange(): arrived = lax.all_to_all(slots, 'tx', 0, 0, tiled=True)  23.7 us
    all_to_all x1, blocking collectives, body(): totals = lax.all_to_all(sent, 'face', 0, 0, tiled=True)  18.2 us
    all_gather x2, blocking collectives, exchange(): gathered = lax.all_gather(strips, 'ty', axis=0)  17.6 us
    ppermute x2, starting transfers between devices, exchange(): swapped_b = lax.ppermute(swap_b, 'tx', wrapped)  15.4 us
    all_to_all x1, blocking collectives, body(): loads = lax.all_to_all(loads, 'face', 0, 0, tiled=True)  12.2 us
    ppermute x2, starting transfers between devices, exchange(): swapped_a = lax.ppermute(near_row, 'tx', near)  9.33 us
    pallas_call x8, Pallas kernels, call(): pl.pallas_call(kernel, out_shape=shapes, in_specs=[VMEM] * len(operands),...  5.16 us
    ppermute x2, waiting for transfers between devices, exchange(): swapped_b = lax.ppermute(swap_b, 'tx', wrapped)  2.78 us
  transfers between devices with their start and end apart: 6, of which 4 were waited for; matrix products, arithmetic and copies ran while one was open for 0% of the time, Pallas kernels for 1%

profile of v4, /device:TPU:2, one launch (start us, length us, event | category | flops | bytes accessed | tf_op | source)
XLA Modules:
  0.0 106.9 jit_solution(18195834918758808645)
XLA Ops:
  0.0 1.6 %thickness.1 = (f32[8,48,128]{2,1,0:T(8,128)}, f32[4,8,64]{2,1,0:T(8,128)}) custom-call(s32[6,4,7]{2,1,0:T(4,128)} %links.1, f32[2,4,1,6,8,64]{5,4,3,2,1,0:T(8,128)} %probes.7, f32[4,1,6,8,64]{4,3,2,1,0:T(8,128)} %spread.7), custom_call_target="tpu_custom_call" | custom-call | tf_op jit(solution)/shard_map/thickness/pallas_call | solution.py:510
  1.6 0.0 copy-start
  1.6 0.0 copy-start.1
  1.6 0.0 copy-start.2
  1.6 0.0 copy-start.7
  1.6 0.0 copy-start.8
  1.7 18.2 %all_to_all.20.totals = f32[8,48,128]{2,1,0:T(8,128)S(1)} all-to-all(f32[8,48,128]{2,1,0:T(8,128)} %get-tuple-element.30), channel_id=1, replica_groups=mesh['face'=8,'tx'=32,'ty'=4] {'face'}, dimensions={0} | all-to-all | bytes 393216 | tf_op jit(solution)/shard_map/all_to_all | solution.py:557
  19.8 0.0 copy-done
  19.8 0.0 copy-done.1
  19.8 0.0 copy-done.2
  19.8 0.0 copy-done.7
  19.8 0.0 copy-done.8
  19.9 0.0 copy-start.4
  19.9 0.2 shard_map.109
  20.1 0.0 copy-start.5
  20.1 0.0 copy-start.10
  20.1 12.0 %all-gather = f32[288,128]{1,0:T(8,128)S(1)} all-gather(f32[72,128]{1,0:T(8,128)S(1)} %get-tuple-element.31), channel_id=2, replica_groups=mesh['face'=8,'tx'=32,'ty'=4] {'ty'}, dimensions={0}, use_global_device_ids=true | all-gather | bytes 184320 | tf_op jit(solution)/shard_map/all_gather | solution.py:538
  32.1 0.0 copy-done.4
  32.1 0.0 copy-done.5
  32.1 0.0 copy-done.10
  32.1 1.4 %shard_map.110 = (f32[32,8,128]{2,1,0:T(8,128)}, f32[32,128]{1,0:T(8,128)S(1)}, f32[32,128]{1,0:T(8,128)S(1)}, f32[16,64]{1,0:T(8,128)S(1)}) custom-call(f32[4,8,64]{2,1,0:T(8,128)S(1)} %copy-done.5, f32[4,72,128]{2,1,0:T(8,128)S(1)} %bitcast.2, f32[32,128]{1,0:T(8,128)S(1)} %get-tuple-element.32.far_row, f32[5,128,64]{2,1,0:T(8,128)S(1)} %copy-done.4, ...), custom_call_target="tpu_custom_call" | custom-call | tf_op jit(solution)/shard_map/pallas_call | solution.py:499
  33.5 14.7 %all-to-all-start.1 = ((f32[32,8,128]{2,1,0:T(8,128)}), f32[32,8,128]{2,1,0:T(8,128)S(1)}, u32[]{:S(2)}, u32[]{:S(2)}) async-start(f32[32,8,128]{2,1,0:T(8,128)} %get-tuple-element.33), calls=%async_computation.1 | async-start | bytes 262144 | tf_op jit(solution)/shard_map/all_to_all | solution.py:545
  48.2 0.0 copy-start.6
  48.2 4.7 %collective-permute-start = (f32[32,128]{1,0:T(8,128)S(1)}, f32[32,128]{1,0:T(8,128)S(1)}, u32[]{:S(2)}, u32[]{:S(2)}) collective-permute-start(f32[32,128]{1,0:T(8,128)S(1)} %get-tuple-element.38), channel_id=1, source_target_pairs={{0,4},{4,0},{8,12},{12,8},{16,20},{20,16},{24,28},{28,24},{32,36},... | collective-permute-start | bytes 49160 | tf_op jit(solution)/shard_map/ppermute | solution.py:537
  53.0 7.7 %collective-permute-start.1 = (f32[32,128]{1,0:T(8,128)S(1)}, f32[32,128]{1,0:T(8,128)S(1)}, u32[]{:S(2)}, u32[]{:S(2)}) collective-permute-start(f32[32,128]{1,0:T(8,128)S(1)} %get-tuple-element.39), channel_id=1, source_target_pairs={{0,124},{4,8},{8,4},{12,16},{16,12},{20,24},{24,20},{28,32},{32,28... | collective-permute-start | bytes 49160 | tf_op jit(solution)/shard_map/ppermute | solution.py:544
  60.7 0.3 all-to-all-done.1.arrived
  61.0 0.4 shard_map.111
  61.4 0.0 collective-permute-done.swapped_a
  61.4 1.5 %collective-permute-done.1.swapped_b = f32[32,128]{1,0:T(8,128)S(1)} collective-permute-done((f32[32,128]{1,0:T(8,128)S(1)}, f32[32,128]{1,0:T(8,128)S(1)}, u32[]{:S(2)}, u32[]{:S(2)}) %collective-permute-start.1) | collective-permute-done | bytes 16416 | tf_op jit(solution)/shard_map/ppermute | solution.py:544
  62.8 0.0 copy-done.6
  62.8 0.0 copy-start.3
  62.8 0.4 shard_map.112
  63.3 0.0 copy-start.9
  63.3 5.6 %all-gather.1 = f32[288,128]{1,0:T(8,128)S(1)} all-gather(f32[72,128]{1,0:T(8,128)S(1)} %get-tuple-element.41), channel_id=3, replica_groups=mesh['face'=8,'tx'=32,'ty'=4] {'ty'}, dimensions={0}, use_global_device_ids=true | all-gather | bytes 184320 | tf_op jit(solution)/shard_map/all_gather | solution.py:538
  68.9 0.0 copy-done.3
  68.9 0.0 copy-done.9
  68.9 1.4 %shard_map.113 = (f32[32,8,128]{2,1,0:T(8,128)}, f32[32,128]{1,0:T(8,128)S(1)}, f32[32,128]{1,0:T(8,128)S(1)}, f32[16,64]{1,0:T(8,128)S(1)}) custom-call(f32[4,8,64]{2,1,0:T(8,128)S(1)} %copy-done.5, f32[4,72,128]{2,1,0:T(8,128)S(1)} %bitcast.3, f32[32,128]{1,0:T(8,128)S(1)} %get-tuple-element.42.far_row, f32[5,128,64]{2,1,0:T(8,128)S(1)} %copy-done.3, ...), custom_call_target="tpu_custom_call" | custom-call | tf_op jit(solution)/shard_map/pallas_call | solution.py:499
  70.2 8.9 %all-to-all-start.2 = ((f32[32,8,128]{2,1,0:T(8,128)}), f32[32,8,128]{2,1,0:T(8,128)S(1)}, u32[]{:S(2)}, u32[]{:S(2)}) async-start(f32[32,8,128]{2,1,0:T(8,128)} %get-tuple-element.43), calls=%async_computation.2 | async-start | bytes 262144 | tf_op jit(solution)/shard_map/all_to_all | solution.py:545
  79.2 4.6 %collective-permute-start.2 = (f32[32,128]{1,0:T(8,128)S(1)}, f32[32,128]{1,0:T(8,128)S(1)}, u32[]{:S(2)}, u32[]{:S(2)}) collective-permute-start(f32[32,128]{1,0:T(8,128)S(1)} %get-tuple-element.48), channel_id=1, source_target_pairs={{0,4},{4,0},{8,12},{12,8},{16,20},{20,16},{24,28},{28,24},{32,36},... | collective-permute-start | bytes 49160 | tf_op jit(solution)/shard_map/ppermute | solution.py:537
  83.8 7.7 %collective-permute-start.3 = (f32[32,128]{1,0:T(8,128)S(1)}, f32[32,128]{1,0:T(8,128)S(1)}, u32[]{:S(2)}, u32[]{:S(2)}) collective-permute-start(f32[32,128]{1,0:T(8,128)S(1)} %get-tuple-element.49), channel_id=1, source_target_pairs={{0,124},{4,8},{8,4},{12,16},{16,12},{20,24},{24,20},{28,32},{32,28... | collective-permute-start | bytes 49160 | tf_op jit(solution)/shard_map/ppermute | solution.py:544
  91.5 0.5 all-to-all-done.2.arrived
  92.0 0.4 shard_map.114
  92.3 0.0 collective-permute-done.2.swapped_a
  92.3 1.3 %collective-permute-done.3.swapped_b = f32[32,128]{1,0:T(8,128)S(1)} collective-permute-done((f32[32,128]{1,0:T(8,128)S(1)}, f32[32,128]{1,0:T(8,128)S(1)}, u32[]{:S(2)}, u32[]{:S(2)}) %collective-permute-start.3) | collective-permute-done | bytes 16416 | tf_op jit(solution)/shard_map/ppermute | solution.py:544
  93.7 0.2 shard_map.115
  93.9 12.2 %all_to_all.21.loads = f32[8,48,128]{2,1,0:T(8,128)S(1)} all-to-all(f32[8,48,128]{2,1,0:T(8,128)S(1)} %get-tuple-element.52), channel_id=1, replica_groups=mesh['face'=8,'tx'=32,'ty'=4] {'face'}, dimensions={0} | all-to-all | bytes 393216 | tf_op jit(solution)/shard_map/all_to_all | solution.py:575
  106.1 0.8 shard_map.116
Async XLA Ops:
  1.6 18.2 %copy-start = (f32[2,4,1,6,8,64]{5,4,3,2,1,0:T(8,128)S(1)}, f32[2,4,1,6,8,64]{5,4,3,2,1,0:T(8,128)}, u32[]{:S(2)}) copy-start(f32[2,4,1,6,8,64]{5,4,3,2,1,0:T(8,128)} %probes.7) | copy-start | bytes 294916
  1.6 18.2 %copy-start.1 = (f32[4,1,6,8,64]{4,3,2,1,0:T(8,128)S(1)}, f32[4,1,6,8,64]{4,3,2,1,0:T(8,128)}, u32[]{:S(2)}) copy-start(f32[4,1,6,8,64]{4,3,2,1,0:T(8,128)} %spread.7) | copy-start | bytes 147460
  1.6 18.2 %copy-start.2 = (f32[2,1,6,8,64]{4,3,2,1,0:T(8,128)S(1)}, f32[2,1,6,8,64]{4,3,2,1,0:T(8,128)}, u32[]{:S(2)}) copy-start(f32[2,1,6,8,64]{4,3,2,1,0:T(8,128)} %wind.5) | copy-start | bytes 73732
  1.6 18.2 %copy-start.7 = (f32[1,6,8,64]{3,2,1,0:T(8,128)S(1)}, f32[1,6,8,64]{3,2,1,0:T(8,128)}, u32[]{:S(2)}) copy-start(f32[1,6,8,64]{3,2,1,0:T(8,128)} %mass.3) | copy-start | bytes 36868
  1.6 18.2 %copy-start.8 = (f32[1,6,8,64]{3,2,1,0:T(8,128)S(1)}, f32[1,6,8,64]{3,2,1,0:T(8,128)}, u32[]{:S(2)}) copy-start(f32[1,6,8,64]{3,2,1,0:T(8,128)} %heat.3) | copy-start | bytes 36868
  19.9 12.3 %copy-start.4 = (f32[5,128,64]{2,1,0:T(8,128)S(1)}, f32[5,128,64]{2,1,0:T(8,128)}, u32[]{:S(2)}) copy-start(f32[5,128,64]{2,1,0:T(8,128)} %constant.8.clone.codes) | copy-start | bytes 491524
  20.1 12.0 %copy-start.5 = (f32[4,8,64]{2,1,0:T(8,128)S(1)}, f32[4,8,64]{2,1,0:T(8,128)}, u32[]{:S(2)}) copy-start(f32[4,8,64]{2,1,0:T(8,128)} %get-tuple-element.29.links) | copy-start | bytes 24580
  20.1 12.0 %copy-start.10 = (f32[128,64]{1,0:T(8,128)S(1)}, f32[128,64]{1,0:T(8,128)}, u32[]{:S(2)}) copy-start(f32[128,64]{1,0:T(8,128)} %constant.9.clone.picks) | copy-start | bytes 98308
  33.5 27.5 %all-to-all-start.1 = ((f32[32,8,128]{2,1,0:T(8,128)}), f32[32,8,128]{2,1,0:T(8,128)S(1)}, u32[]{:S(2)}, u32[]{:S(2)}) async-start(f32[32,8,128]{2,1,0:T(8,128)} %get-tuple-element.33), calls=%async_computation.1 | async-start | bytes 262144 | tf_op jit(solution)/shard_map/all_to_all | solution.py:545
  48.2 14.6 %copy-start.6 = (f32[4,1,6,8,64]{4,3,2,1,0:T(8,128)S(1)}, f32[4,1,6,8,64]{4,3,2,1,0:T(8,128)}, u32[]{:S(2)}) copy-start(f32[4,1,6,8,64]{4,3,2,1,0:T(8,128)} %misfit.1) | copy-start | bytes 147460
  48.2 13.1 %collective-permute-start = (f32[32,128]{1,0:T(8,128)S(1)}, f32[32,128]{1,0:T(8,128)S(1)}, u32[]{:S(2)}, u32[]{:S(2)}) collective-permute-start(f32[32,128]{1,0:T(8,128)S(1)} %get-tuple-element.38), channel_id=1, source_target_pairs={{0,4},{4,0},{8,12},{12,8},{16,20},{20,16},{24,28},{28,24},{32,36},... | collective-permute-start | bytes 49160 | tf_op jit(solution)/shard_map/ppermute | solution.py:537
  53.0 9.9 %collective-permute-start.1 = (f32[32,128]{1,0:T(8,128)S(1)}, f32[32,128]{1,0:T(8,128)S(1)}, u32[]{:S(2)}, u32[]{:S(2)}) collective-permute-start(f32[32,128]{1,0:T(8,128)S(1)} %get-tuple-element.39), channel_id=1, source_target_pairs={{0,124},{4,8},{8,4},{12,16},{16,12},{20,24},{24,20},{28,32},{32,28... | collective-permute-start | bytes 49160 | tf_op jit(solution)/shard_map/ppermute | solution.py:544
  62.8 6.0 %copy-start.3 = (f32[5,128,64]{2,1,0:T(8,128)S(1)}, f32[5,128,64]{2,1,0:T(8,128)}, u32[]{:S(2)}) copy-start(f32[5,128,64]{2,1,0:T(8,128)} %constant.10.clone.codes) | copy-start | bytes 491524
  63.3 5.6 %copy-start.9 = (f32[128,64]{1,0:T(8,128)S(1)}, f32[128,64]{1,0:T(8,128)}, u32[]{:S(2)}) copy-start(f32[128,64]{1,0:T(8,128)} %constant.11.clone.picks) | copy-start | bytes 98308
  70.2 21.7 %all-to-all-start.2 = ((f32[32,8,128]{2,1,0:T(8,128)}), f32[32,8,128]{2,1,0:T(8,128)S(1)}, u32[]{:S(2)}, u32[]{:S(2)}) async-start(f32[32,8,128]{2,1,0:T(8,128)} %get-tuple-element.43), calls=%async_computation.2 | async-start | bytes 262144 | tf_op jit(solution)/shard_map/all_to_all | solution.py:545
  79.2 13.1 %collective-permute-start.2 = (f32[32,128]{1,0:T(8,128)S(1)}, f32[32,128]{1,0:T(8,128)S(1)}, u32[]{:S(2)}, u32[]{:S(2)}) collective-permute-start(f32[32,128]{1,0:T(8,128)S(1)} %get-tuple-element.48), channel_id=1, source_target_pairs={{0,4},{4,0},{8,12},{12,8},{16,20},{20,16},{24,28},{28,24},{32,36},... | collective-permute-start | bytes 49160 | tf_op jit(solution)/shard_map/ppermute | solution.py:537
  83.8 9.9 %collective-permute-start.3 = (f32[32,128]{1,0:T(8,128)S(1)}, f32[32,128]{1,0:T(8,128)S(1)}, u32[]{:S(2)}, u32[]{:S(2)}) collective-permute-start(f32[32,128]{1,0:T(8,128)S(1)} %get-tuple-element.49), channel_id=1, source_target_pairs={{0,124},{4,8},{8,4},{12,16},{16,12},{20,24},{24,20},{28,32},{32,28... | collective-permute-start | bytes 49160 | tf_op jit(solution)/shard_map/ppermute | solution.py:544

commit v5 on v4

--- a/solution.py
+++ b/solution.py
@@ -226,7 +226,19 @@
 
 
 def fields_kernel(
-    level_count, probes, spread, wind, mass, heat, totals, fields, strips, near_row, far_row
+    level_count,
+    probes,
+    spread,
+    wind,
+    mass,
+    heat,
+    misfit,
+    totals,
+    fields,
+    strips,
+    near_row,
+    far_row,
+    weights,
 ):
     level, tile_row = lax.axis_index("face"), lax.axis_index("tx")
     planes = {}
@@ -235,6 +247,8 @@
         north = pair(wind, (1, 0), pp)
         mass_here = pair(mass, (0,), pp)
         heat_here = pair(heat, (0,), pp)
+        for c in range(4):
+            weights[c * 3 + pp] = pair(misfit, (c, 0), pp)
         for probe in range(PROBES):
             scaled = [
                 pair(spread, (c, 0), pp) * pair(probes, (probe, c, 0), pp) for c in range(4)
@@ -385,7 +399,7 @@
     probes,
     spread,
     wind,
-    misfit,
+    weights,
     costs,
     strips,
     near_row,
@@ -408,7 +422,7 @@
             )
             t = thickness - dt * (dx["flux_x"] + dy["flux_y"])
             h = field("temp") - dt * (u * dx["temp"] + v * dy["temp"])
-            z, m, t, h = (pair(misfit, (c, 0), pp) * w for c, w in enumerate((z, m, t, h)))
+            z, m, t, h = (weights[c * 3 + pp] * w for c, w in enumerate((z, m, t, h)))
             for c, w in enumerate((z, m, t, h)):
                 costs[(c * PROBES + probe) * 3 + pp] = w
             made = (u * z, u * m, v * z, v * m, z, m, t, u * h, v * h)
@@ -555,15 +569,15 @@
     nf, nt, nq = (lax.axis_size(a) for a in ("face", "tx", "ty"))
     sent, table = thickness_copies(nf, links, probes, spread)
     totals = lax.all_to_all(sent, "face", 0, 0, tiled=True)
-    fields, strips, *rows = call(
+    fields, strips, *rows, weights = call(
         functools.partial(fields_kernel, nf),
-        (probes, spread, wind, mass, heat, totals),
-        ((36, 8, 128), (STRIP, 128), (32, 128), (32, 128)),
+        (probes, spread, wind, mass, heat, misfit, totals),
+        ((36, 8, 128), (STRIP, 128), (32, 128), (32, 128), (12, 8, 128)),
     )
     outer = exchange("forward", nt, nq, table, strips, *rows)
     costs, strips, *rows = call(
         functools.partial(image_kernel, nt),
-        (*outer, fields, probes, spread, wind, misfit),
+        (*outer, fields, probes, spread, wind, weights),
         ((24, 8, 128), (STRIP, 128), (32, 128), (32, 128)),
     )
     outer = exchange("adjoint", nt, nq, table, strips, *rows)

time: 107 us -> 107 us (level)
  no operation moved by 1% of the time
where the time goes in v5:
time: 107 us
  starting transfers between devices  48.2 us (45%)
  blocking collectives  47.9 us (45%)
  Pallas kernels  6.9 us (6%)
  waiting for transfers between devices  3.6 us (3%)
    all_to_all x2, starting transfers between devices, exchange(): arrived = lax.all_to_all(slots, 'tx', 0, 0, tiled=True)  23.7 us
    all_to_all x1, blocking collectives, body(): totals = lax.all_to_all(sent, 'face', 0, 0, tiled=True)  18.2 us
    all_gather x2, blocking collectives, exchange(): gathered = lax.all_gather(strips, 'ty', axis=0)  17.6 us
    ppermute x2, starting transfers between devices, exchange(): swapped_b = lax.ppermute(swap_b, 'tx', wrapped)  15.4 us
    all_to_all x1, blocking collectives, body(): loads = lax.all_to_all(loads, 'face', 0, 0, tiled=True)  12.2 us
    ppermute x2, starting transfers between devices, exchange(): swapped_a = lax.ppermute(near_row, 'tx', near)  9.19 us
    pallas_call x8, Pallas kernels, call(): pl.pallas_call(kernel, out_shape=shapes, in_specs=[VMEM] * len(operands),...  5.15 us
    ppermute x2, waiting for transfers between devices, exchange(): swapped_b = lax.ppermute(swap_b, 'tx', wrapped)  2.63 us
  transfers between devices with their start and end apart: 6, of which 4 were waited for; matrix products, arithmetic and copies ran while one was open for 0% of the time, Pallas kernels for 1%

profile of v5, /device:TPU:2, one launch (start us, length us, event | category | flops | bytes accessed | tf_op | source)
XLA Modules:
  0.0 106.9 jit_solution(16664850196883258829)
XLA Ops:
  0.0 0.0 copy-start.8
  0.0 1.8 %thickness.1 = (f32[8,48,128]{2,1,0:T(8,128)}, f32[4,8,64]{2,1,0:T(8,128)}) custom-call(s32[6,4,7]{2,1,0:T(4,128)} %links.1, f32[2,4,1,6,8,64]{5,4,3,2,1,0:T(8,128)} %probes.7, f32[4,1,6,8,64]{4,3,2,1,0:T(8,128)} %spread.7), custom_call_target="tpu_custom_call" | custom-call | tf_op jit(solution)/shard_map/thickness/pallas_call | solution.py:524
  1.8 0.0 copy-start
  1.8 0.0 copy-start.1
  1.8 0.0 copy-start.2
  1.8 0.0 copy-start.6
  1.8 0.0 copy-start.7
  1.8 18.2 %all_to_all.20.totals = f32[8,48,128]{2,1,0:T(8,128)S(1)} all-to-all(f32[8,48,128]{2,1,0:T(8,128)} %get-tuple-element.31), channel_id=1, replica_groups=mesh['face'=8,'tx'=32,'ty'=4] {'face'}, dimensions={0} | all-to-all | bytes 393216 | tf_op jit(solution)/shard_map/all_to_all | solution.py:571
  20.0 0.0 copy-done.8
  20.0 0.0 copy-done
  20.0 0.0 copy-done.1
  20.0 0.0 copy-done.2
  20.0 0.0 copy-done.6
  20.0 0.0 copy-done.7
  20.0 0.0 copy-start.4
  20.0 0.3 shard_map.109
  20.3 0.0 copy-start.5
  20.3 0.0 copy-start.10
  20.3 12.0 %all-gather = f32[288,128]{1,0:T(8,128)S(1)} all-gather(f32[72,128]{1,0:T(8,128)S(1)} %get-tuple-element.32), channel_id=2, replica_groups=mesh['face'=8,'tx'=32,'ty'=4] {'ty'}, dimensions={0}, use_global_device_ids=true | all-gather | bytes 184320 | tf_op jit(solution)/shard_map/all_gather | solution.py:552
  32.3 0.0 copy-done.4
  32.3 0.0 copy-done.5
  32.3 0.0 copy-done.10
  32.3 1.4 %shard_map.110 = (f32[32,8,128]{2,1,0:T(8,128)}, f32[32,128]{1,0:T(8,128)S(1)}, f32[32,128]{1,0:T(8,128)S(1)}, f32[16,64]{1,0:T(8,128)S(1)}) custom-call(f32[4,8,64]{2,1,0:T(8,128)S(1)} %copy-done.5, f32[4,72,128]{2,1,0:T(8,128)S(1)} %bitcast.2, f32[32,128]{1,0:T(8,128)S(1)} %get-tuple-element.33.far_row, f32[5,128,64]{2,1,0:T(8,128)S(1)} %copy-done.4, ...), custom_call_target="tpu_custom_call" | custom-call | tf_op jit(solution)/shard_map/pallas_call | solution.py:513
  33.7 14.7 %all-to-all-start.1 = ((f32[32,8,128]{2,1,0:T(8,128)}), f32[32,8,128]{2,1,0:T(8,128)S(1)}, u32[]{:S(2)}, u32[]{:S(2)}) async-start(f32[32,8,128]{2,1,0:T(8,128)} %get-tuple-element.34), calls=%async_computation.1 | async-start | bytes 262144 | tf_op jit(solution)/shard_map/all_to_all | solution.py:559
  48.4 4.6 %collective-permute-start = (f32[32,128]{1,0:T(8,128)S(1)}, f32[32,128]{1,0:T(8,128)S(1)}, u32[]{:S(2)}, u32[]{:S(2)}) collective-permute-start(f32[32,128]{1,0:T(8,128)S(1)} %get-tuple-element.39), channel_id=1, source_target_pairs={{0,4},{4,0},{8,12},{12,8},{16,20},{20,16},{24,28},{28,24},{32,36},... | collective-permute-start | bytes 49160 | tf_op jit(solution)/shard_map/ppermute | solution.py:551
  53.0 7.7 %collective-permute-start.1 = (f32[32,128]{1,0:T(8,128)S(1)}, f32[32,128]{1,0:T(8,128)S(1)}, u32[]{:S(2)}, u32[]{:S(2)}) collective-permute-start(f32[32,128]{1,0:T(8,128)S(1)} %get-tuple-element.40), channel_id=1, source_target_pairs={{0,124},{4,8},{8,4},{12,16},{16,12},{20,24},{24,20},{28,32},{32,28... | collective-permute-start | bytes 49160 | tf_op jit(solution)/shard_map/ppermute | solution.py:558
  60.7 0.5 all-to-all-done.1.arrived
  61.2 0.4 shard_map.111
  61.5 0.0 collective-permute-done.swapped_a
  61.5 1.3 %collective-permute-done.1.swapped_b = f32[32,128]{1,0:T(8,128)S(1)} collective-permute-done((f32[32,128]{1,0:T(8,128)S(1)}, f32[32,128]{1,0:T(8,128)S(1)}, u32[]{:S(2)}, u32[]{:S(2)}) %collective-permute-start.1) | collective-permute-done | bytes 16416 | tf_op jit(solution)/shard_map/ppermute | solution.py:558
  62.9 0.0 copy-start.3
  62.9 0.4 shard_map.112
  63.2 0.0 copy-start.9
  63.2 5.6 %all-gather.1 = f32[288,128]{1,0:T(8,128)S(1)} all-gather(f32[72,128]{1,0:T(8,128)S(1)} %get-tuple-element.43), channel_id=3, replica_groups=mesh['face'=8,'tx'=32,'ty'=4] {'ty'}, dimensions={0}, use_global_device_ids=true | all-gather | bytes 184320 | tf_op jit(solution)/shard_map/all_gather | solution.py:552
  68.8 0.0 copy-done.3
  68.8 0.0 copy-done.9
  68.8 1.4 %shard_map.113 = (f32[32,8,128]{2,1,0:T(8,128)}, f32[32,128]{1,0:T(8,128)S(1)}, f32[32,128]{1,0:T(8,128)S(1)}, f32[16,64]{1,0:T(8,128)S(1)}) custom-call(f32[4,8,64]{2,1,0:T(8,128)S(1)} %copy-done.5, f32[4,72,128]{2,1,0:T(8,128)S(1)} %bitcast.3, f32[32,128]{1,0:T(8,128)S(1)} %get-tuple-element.44.far_row, f32[5,128,64]{2,1,0:T(8,128)S(1)} %copy-done.3, ...), custom_call_target="tpu_custom_call" | custom-call | tf_op jit(solution)/shard_map/pallas_call | solution.py:513
  70.2 8.9 %all-to-all-start.2 = ((f32[32,8,128]{2,1,0:T(8,128)}), f32[32,8,128]{2,1,0:T(8,128)S(1)}, u32[]{:S(2)}, u32[]{:S(2)}) async-start(f32[32,8,128]{2,1,0:T(8,128)} %get-tuple-element.45), calls=%async_computation.2 | async-start | bytes 262144 | tf_op jit(solution)/shard_map/all_to_all | solution.py:559
  79.2 4.6 %collective-permute-start.2 = (f32[32,128]{1,0:T(8,128)S(1)}, f32[32,128]{1,0:T(8,128)S(1)}, u32[]{:S(2)}, u32[]{:S(2)}) collective-permute-start(f32[32,128]{1,0:T(8,128)S(1)} %get-tuple-element.50), channel_id=1, source_target_pairs={{0,4},{4,0},{8,12},{12,8},{16,20},{20,16},{24,28},{28,24},{32,36},... | collective-permute-start | bytes 49160 | tf_op jit(solution)/shard_map/ppermute | solution.py:551
  83.8 7.7 %collective-permute-start.3 = (f32[32,128]{1,0:T(8,128)S(1)}, f32[32,128]{1,0:T(8,128)S(1)}, u32[]{:S(2)}, u32[]{:S(2)}) collective-permute-start(f32[32,128]{1,0:T(8,128)S(1)} %get-tuple-element.51), channel_id=1, source_target_pairs={{0,124},{4,8},{8,4},{12,16},{16,12},{20,24},{24,20},{28,32},{32,28... | collective-permute-start | bytes 49160 | tf_op jit(solution)/shard_map/ppermute | solution.py:558
  91.5 0.5 all-to-all-done.2.arrived
  92.0 0.4 shard_map.114
  92.3 0.0 collective-permute-done.2.swapped_a
  92.3 1.3 %collective-permute-done.3.swapped_b = f32[32,128]{1,0:T(8,128)S(1)} collective-permute-done((f32[32,128]{1,0:T(8,128)S(1)}, f32[32,128]{1,0:T(8,128)S(1)}, u32[]{:S(2)}, u32[]{:S(2)}) %collective-permute-start.3) | collective-permute-done | bytes 16416 | tf_op jit(solution)/shard_map/ppermute | solution.py:558
  93.6 0.2 shard_map.115
  93.9 12.2 %all_to_all.21.loads = f32[8,48,128]{2,1,0:T(8,128)S(1)} all-to-all(f32[8,48,128]{2,1,0:T(8,128)S(1)} %get-tuple-element.54), channel_id=1, replica_groups=mesh['face'=8,'tx'=32,'ty'=4] {'face'}, dimensions={0} | all-to-all | bytes 393216 | tf_op jit(solution)/shard_map/all_to_all | solution.py:589
  106.1 0.8 shard_map.116
Async XLA Ops:
  0.0 20.0 %copy-start.8 = (f32[4,1,6,8,64]{4,3,2,1,0:T(8,128)S(1)}, f32[4,1,6,8,64]{4,3,2,1,0:T(8,128)}, u32[]{:S(2)}) copy-start(f32[4,1,6,8,64]{4,3,2,1,0:T(8,128)} %misfit.1) | copy-start | bytes 147460
  1.8 18.2 %copy-start = (f32[2,4,1,6,8,64]{5,4,3,2,1,0:T(8,128)S(1)}, f32[2,4,1,6,8,64]{5,4,3,2,1,0:T(8,128)}, u32[]{:S(2)}) copy-start(f32[2,4,1,6,8,64]{5,4,3,2,1,0:T(8,128)} %probes.7) | copy-start | bytes 294916
  1.8 18.2 %copy-start.1 = (f32[4,1,6,8,64]{4,3,2,1,0:T(8,128)S(1)}, f32[4,1,6,8,64]{4,3,2,1,0:T(8,128)}, u32[]{:S(2)}) copy-start(f32[4,1,6,8,64]{4,3,2,1,0:T(8,128)} %spread.7) | copy-start | bytes 147460
  1.8 18.2 %copy-start.2 = (f32[2,1,6,8,64]{4,3,2,1,0:T(8,128)S(1)}, f32[2,1,6,8,64]{4,3,2,1,0:T(8,128)}, u32[]{:S(2)}) copy-start(f32[2,1,6,8,64]{4,3,2,1,0:T(8,128)} %wind.5) | copy-start | bytes 73732
  1.8 18.2 %copy-start.6 = (f32[1,6,8,64]{3,2,1,0:T(8,128)S(1)}, f32[1,6,8,64]{3,2,1,0:T(8,128)}, u32[]{:S(2)}) copy-start(f32[1,6,8,64]{3,2,1,0:T(8,128)} %mass.3) | copy-start | bytes 36868
  1.8 18.2 %copy-start.7 = (f32[1,6,8,64]{3,2,1,0:T(8,128)S(1)}, f32[1,6,8,64]{3,2,1,0:T(8,128)}, u32[]{:S(2)}) copy-start(f32[1,6,8,64]{3,2,1,0:T(8,128)} %heat.3) | copy-start | bytes 36868
  20.0 12.3 %copy-start.4 = (f32[5,128,64]{2,1,0:T(8,128)S(1)}, f32[5,128,64]{2,1,0:T(8,128)}, u32[]{:S(2)}) copy-start(f32[5,128,64]{2,1,0:T(8,128)} %constant.8.clone.codes) | copy-start | bytes 491524
  20.3 12.0 %copy-start.5 = (f32[4,8,64]{2,1,0:T(8,128)S(1)}, f32[4,8,64]{2,1,0:T(8,128)}, u32[]{:S(2)}) copy-start(f32[4,8,64]{2,1,0:T(8,128)} %get-tuple-element.30.links) | copy-start | bytes 24580
  20.3 12.0 %copy-start.10 = (f32[128,64]{1,0:T(8,128)S(1)}, f32[128,64]{1,0:T(8,128)}, u32[]{:S(2)}) copy-start(f32[128,64]{1,0:T(8,128)} %constant.9.clone.picks) | copy-start | bytes 98308
  33.7 27.5 %all-to-all-start.1 = ((f32[32,8,128]{2,1,0:T(8,128)}), f32[32,8,128]{2,1,0:T(8,128)S(1)}, u32[]{:S(2)}, u32[]{:S(2)}) async-start(f32[32,8,128]{2,1,0:T(8,128)} %get-tuple-element.34), calls=%async_computation.1 | async-start | bytes 262144 | tf_op jit(solution)/shard_map/all_to_all | solution.py:559
  48.4 13.1 %collective-permute-start = (f32[32,128]{1,0:T(8,128)S(1)}, f32[32,128]{1,0:T(8,128)S(1)}, u32[]{:S(2)}, u32[]{:S(2)}) collective-permute-start(f32[32,128]{1,0:T(8,128)S(1)} %get-tuple-element.39), channel_id=1, source_target_pairs={{0,4},{4,0},{8,12},{12,8},{16,20},{20,16},{24,28},{28,24},{32,36},... | collective-permute-start | bytes 49160 | tf_op jit(solution)/shard_map/ppermute | solution.py:551
  53.0 9.9 %collective-permute-start.1 = (f32[32,128]{1,0:T(8,128)S(1)}, f32[32,128]{1,0:T(8,128)S(1)}, u32[]{:S(2)}, u32[]{:S(2)}) collective-permute-start(f32[32,128]{1,0:T(8,128)S(1)} %get-tuple-element.40), channel_id=1, source_target_pairs={{0,124},{4,8},{8,4},{12,16},{16,12},{20,24},{24,20},{28,32},{32,28... | collective-permute-start | bytes 49160 | tf_op jit(solution)/shard_map/ppermute | solution.py:558
  62.9 6.0 %copy-start.3 = (f32[5,128,64]{2,1,0:T(8,128)S(1)}, f32[5,128,64]{2,1,0:T(8,128)}, u32[]{:S(2)}) copy-start(f32[5,128,64]{2,1,0:T(8,128)} %constant.10.clone.codes) | copy-start | bytes 491524
  63.2 5.6 %copy-start.9 = (f32[128,64]{1,0:T(8,128)S(1)}, f32[128,64]{1,0:T(8,128)}, u32[]{:S(2)}) copy-start(f32[128,64]{1,0:T(8,128)} %constant.11.clone.picks) | copy-start | bytes 98308
  70.2 21.7 %all-to-all-start.2 = ((f32[32,8,128]{2,1,0:T(8,128)}), f32[32,8,128]{2,1,0:T(8,128)S(1)}, u32[]{:S(2)}, u32[]{:S(2)}) async-start(f32[32,8,128]{2,1,0:T(8,128)} %get-tuple-element.45), calls=%async_computation.2 | async-start | bytes 262144 | tf_op jit(solution)/shard_map/all_to_all | solution.py:559
  79.2 13.1 %collective-permute-start.2 = (f32[32,128]{1,0:T(8,128)S(1)}, f32[32,128]{1,0:T(8,128)S(1)}, u32[]{:S(2)}, u32[]{:S(2)}) collective-permute-start(f32[32,128]{1,0:T(8,128)S(1)} %get-tuple-element.50), channel_id=1, source_target_pairs={{0,4},{4,0},{8,12},{12,8},{16,20},{20,16},{24,28},{28,24},{32,36},... | collective-permute-start | bytes 49160 | tf_op jit(solution)/shard_map/ppermute | solution.py:551
  83.8 9.9 %collective-permute-start.3 = (f32[32,128]{1,0:T(8,128)S(1)}, f32[32,128]{1,0:T(8,128)S(1)}, u32[]{:S(2)}, u32[]{:S(2)}) collective-permute-start(f32[32,128]{1,0:T(8,128)S(1)} %get-tuple-element.51), channel_id=1, source_target_pairs={{0,124},{4,8},{8,4},{12,16},{16,12},{20,24},{24,20},{28,32},{32,28... | collective-permute-start | bytes 49160 | tf_op jit(solution)/shard_map/ppermute | solution.py:558

commit v6 on v5

--- a/solution.py
+++ b/solution.py
@@ -275,55 +275,49 @@
     )
 
 
-def route_kernel(
-    nt, nq, links, gathered, far_row, codes, picks, slots, swap_b, local, halos
-):
+def edge_masks(table, edge, source):
+    flip = link_lanes(table, edge, 2)
+    here = link_lanes(table, edge, 1) == source
+    return (
+        jnp.where(here & (flip != 1.0), 1.0, 0.0),
+        jnp.where(here & (flip == 1.0), 1.0, 0.0),
+    )
+
+
+def segment(gathered, q):
+    packed = gathered[q, 16:STRIP]
+    empty = jnp.zeros((64 - ROWS, 64), jnp.float32)
+    return parts(jnp.concatenate([packed[:, 0:64], empty, packed[:, 64:128], empty], axis=0))
+
+
+def slots_kernel(nt, nq, table, gathered, codes, slots):
     tile_row, tile_column = lax.axis_index("tx"), lax.axis_index("ty")
     is_first, is_last = tile_row == 0, tile_row == nt - 1
     line_f = jnp.where(is_first, 0.0, 1.0)
     column_edge = jnp.where(tile_column == 0, 2, 3)
     panel = codes[4]
-    c0 = coefficients(links, 0, codes[0], codes[1], panel)
-    c1 = coefficients(links, 1, codes[0], codes[1], panel)
-    cc = coefficients(links, column_edge, codes[2], codes[3], panel)
+    c0 = coefficients(table, 0, codes[0], codes[1], panel)
+    c1 = coefficients(table, 1, codes[0], codes[1], panel)
+    cc = coefficients(table, column_edge, codes[2], codes[3], panel)
     ends = joined(c0, c1).astype(jnp.bfloat16)
     cc = cc.astype(jnp.bfloat16)
-
-    def masks(edge, source):
-        far = link_lanes(links, edge, 1)
-        flip = link_lanes(links, edge, 2)
-        here = far == source
-        return (
-            jnp.where(here & (flip != 1.0), 1.0, 0.0),
-            jnp.where(here & (flip == 1.0), 1.0, 0.0),
-        )
-
-    back64 = reversal(64)
-    empty = jnp.zeros((64 - ROWS, 64), jnp.float32)
-
-    def segment(q):
-        packed = gathered[q, 16:STRIP]
-        return parts(
-            jnp.concatenate([packed[:, 0:64], empty, packed[:, 64:128], empty], axis=0)
-        )
-
     on_boundary = jnp.where(is_first | is_last, 1.0, 0.0)
-    plain_c, turned_c = masks(column_edge, line_f)
-    across = [moved(segment(q), cc, (0, 0)) * on_boundary for q in range(nq)]
+    plain_c, turned_c = edge_masks(table, column_edge, line_f)
+    across = [moved(segment(gathered, q), cc, (0, 0)) * on_boundary for q in range(nq)]
     turned = joined_all([a * turned_c for a in across])
-    turned = chosen(back64, parts(turned))
+    turned = chosen(reversal(64), parts(turned))
     pieces = [
         across[q] * plain_c + turned[:, 64 * (nq - 1 - q) : 64 * (nq - q)] for q in range(nq)
     ]
     columns = parts(jnp.concatenate([gathered[0, 0:8], gathered[nq - 1, 8:16]], axis=0))
-    low_plain, low_turned = masks(column_edge, 2.0)
-    high_plain, high_turned = masks(column_edge, 3.0)
+    low_plain, low_turned = edge_masks(table, column_edge, 2.0)
+    high_plain, high_turned = edge_masks(table, column_edge, 3.0)
     to_columns = moved(columns, cc)
     low_c, high_c = to_columns[0:8], to_columns[8:16]
     straight = low_c * low_plain + high_c * high_plain
     flipped = chosen(reversal(8), parts(low_c * low_turned + high_c * high_turned))
     to_rows = moved(columns, ends)
-    far = joined(link_lanes(links, 0, 1), link_lanes(links, 1, 1))
+    far = joined(link_lanes(table, 0, 1), link_lanes(table, 1, 1))
     to_rows = to_rows[0:8] * jnp.where(far == 2.0, 1.0, 0.0) + to_rows[8:16] * jnp.where(
         far == 3.0, 1.0, 0.0
     )
@@ -335,19 +329,25 @@
         left = left + jnp.where(tile_row == nt - 1 - t, flipped, 0.0)
         slots[t] = joined(left, to_rows[1] if t == nt - 1 else to_rows[0])
 
-    plain0, turned0 = masks(0, line_f)
-    plain1, turned1 = masks(1, line_f)
+
+def rows_kernel(nt, nq, table, gathered, far_row, codes, picks, swap_b, local, halos):
+    tile_row, tile_column = lax.axis_index("tx"), lax.axis_index("ty")
+    is_first, is_last = tile_row == 0, tile_row == nt - 1
+    line_f = jnp.where(is_first, 0.0, 1.0)
+    panel = codes[4]
+    c0 = coefficients(table, 0, codes[0], codes[1], panel)
+    c1 = coefficients(table, 1, codes[0], codes[1], panel)
+    plain0, turned0 = edge_masks(table, 0, line_f)
+    plain1, turned1 = edge_masks(table, 1, line_f)
     plain = (joined(c0, c1) * joined(plain0, plain1)).astype(jnp.bfloat16)
     mirror = (joined(c0, c1) * joined(turned0, turned1)).astype(jnp.bfloat16)
-    by_row = chosen(plain, segment(tile_column), (0, 0))
-    by_row = by_row + moved(
-        parts(chosen(mirror, segment(nq - 1 - tile_column), (0, 0))), back64
-    )
+    by_row = chosen(plain, segment(gathered, tile_column), (0, 0))
+    mirrored = chosen(mirror, segment(gathered, nq - 1 - tile_column), (0, 0))
+    by_row = by_row + moved(parts(mirrored), reversal(64))
     by_row = [joined(by_row[k : k + 32], by_row[k + 32 : k + 64]) for k in (0, 64)]
     local[...] = jnp.where(is_first, by_row[0], by_row[1])
     sent = jnp.where(is_first, by_row[1], far_row[...])
     swap_b[...] = jnp.where(is_last, by_row[0], sent)
-
     below = gathered[jnp.maximum(tile_column - 1, 0), 8:16]
     above = gathered[jnp.minimum(tile_column + 1, nq - 1), 0:8]
     near = moved(parts(jnp.concatenate([below, above], axis=0)), picks[...].astype(jnp.bfloat16))
@@ -548,15 +548,18 @@
     picks = jnp.asarray(picks_of(sources, y_targets))
     near = [(i, i ^ 1) for i in range(nt)]
     wrapped = [(i, (i + 1 if i % 2 else i - 1) % nt) for i in range(nt)]
+    gathered = lax.all_gather(strips, "ty", axis=0)
+    (slots,) = call(
+        functools.partial(slots_kernel, nt, nq), (table, gathered, codes), ((nt, 8, 128),)
+    )
+    arrived = lax.all_to_all(slots, "tx", 0, 0, tiled=True)
+    swap_b, local, halos = call(
+        functools.partial(rows_kernel, nt, nq),
+        (table, gathered, far_row, codes, picks),
+        ((32, 128), (32, 128), (16, 64)),
+    )
+    swapped_b = lax.ppermute(swap_b, "tx", wrapped)
     swapped_a = lax.ppermute(near_row, "tx", near)
-    gathered = lax.all_gather(strips, "ty", axis=0)
-    slots, swap_b, local, halos = call(
-        functools.partial(route_kernel, nt, nq),
-        (table, gathered, far_row, codes, picks),
-        ((nt, 8, 128), (32, 128), (32, 128), (16, 64)),
-    )
-    swapped_b = lax.ppermute(swap_b, "tx", wrapped)
-    arrived = lax.all_to_all(slots, "tx", 0, 0, tiled=True)
     sides, row = call(
         functools.partial(collect_kernel, nt, nq),
         (table, arrived, local, halos),

time: 107 us -> 109 us (1.019)
  Pallas kernels: 6.9 us -> 8.1 us
    pallas_call x8 -> x10, Pallas kernels: 5.15 us -> 6.35 us  [call(): pl.pallas_call(kernel, out_shape=shapes, in_specs=[VMEM] * len(operands),...]
  transfers between devices with their start and end apart: 6 -> 6, of which waited for: 4 -> 2; matrix products, arithmetic and copies ran while one was open for 0% -> 0% of each run, Pallas kernels for 1% -> 2%
where the time goes in v6:
time: 109 us; the launch traced here: 108 us
  starting transfers between devices  48.5 us (44%)
  blocking collectives  47.6 us (44%)
  Pallas kernels  8.1 us (7%)
  waiting for transfers between devices  3.58 us (3%)
    all_to_all x2, starting transfers between devices, exchange(): arrived = lax.all_to_all(slots, 'tx', 0, 0, tiled=True)  23.9 us
    all_to_all x1, blocking collectives, body(): totals = lax.all_to_all(sent, 'face', 0, 0, tiled=True)  18.2 us
    all_gather x2, blocking collectives, exchange(): gathered = lax.all_gather(strips, 'ty', axis=0)  17.3 us
    ppermute x2, starting transfers between devices, exchange(): swapped_b = lax.ppermute(swap_b, 'tx', wrapped)  15.4 us
    all_to_all x1, blocking collectives, body(): loads = lax.all_to_all(loads, 'face', 0, 0, tiled=True)  12.2 us
    ppermute x2, starting transfers between devices, exchange(): swapped_a = lax.ppermute(near_row, 'tx', near)  9.19 us
    pallas_call x10, Pallas kernels, call(): pl.pallas_call(kernel, out_shape=shapes, in_specs=[VMEM] * len(operands),...  6.35 us
    ppermute x2, waiting for transfers between devices, exchange(): swapped_b = lax.ppermute(swap_b, 'tx', wrapped)  3.57 us
  transfers between devices with their start and end apart: 6, of which 2 were waited for; matrix products, arithmetic and copies ran while one was open for 0% of the time, Pallas kernels for 2%

profile of v6, /device:TPU:2, one launch (start us, length us, event | category | flops | bytes accessed | tf_op | source)
XLA Modules:
  0.0 108.1 jit_solution(6055143929757063179)
XLA Ops:
  0.0 0.0 copy-start.8
  0.0 1.8 %thickness.1 = (f32[8,48,128]{2,1,0:T(8,128)}, f32[4,8,64]{2,1,0:T(8,128)}) custom-call(s32[6,4,7]{2,1,0:T(4,128)} %links.1, f32[2,4,1,6,8,64]{5,4,3,2,1,0:T(8,128)} %probes.7, f32[4,1,6,8,64]{4,3,2,1,0:T(8,128)} %spread.7), custom_call_target="tpu_custom_call" | custom-call | tf_op jit(solution)/shard_map/thickness/pallas_call | solution.py:524
  1.8 0.0 copy-start
  1.8 0.0 copy-start.1
  1.8 0.0 copy-start.5
  1.8 0.0 copy-start.6
  1.8 0.0 copy-start.7
  1.8 18.2 %all_to_all.20.totals = f32[8,48,128]{2,1,0:T(8,128)S(1)} all-to-all(f32[8,48,128]{2,1,0:T(8,128)} %get-tuple-element.29), channel_id=1, replica_groups=mesh['face'=8,'tx'=32,'ty'=4] {'face'}, dimensions={0} | all-to-all | bytes 393216 | tf_op jit(solution)/shard_map/all_to_all | solution.py:574
  20.0 0.0 copy-done.8
  20.0 0.0 copy-done
  20.0 0.0 copy-done.1
  20.0 0.0 copy-done.5
  20.0 0.0 copy-done.6
  20.0 0.0 copy-done.7
  20.0 0.0 copy-start.3
  20.0 0.3 shard_map.109
  20.3 0.0 copy-start.4
  20.3 11.8 %all-gather = f32[288,128]{1,0:T(8,128)S(1)} all-gather(f32[72,128]{1,0:T(8,128)S(1)} %get-tuple-element.30), channel_id=2, replica_groups=mesh['face'=8,'tx'=32,'ty'=4] {'ty'}, dimensions={0}, use_global_device_ids=true | all-gather | bytes 184320 | tf_op jit(solution)/shard_map/all_gather | solution.py:551
  32.1 0.0 copy-done.3
  32.1 0.0 copy-done.4
  32.1 1.4 %shard_map.110 = f32[32,8,128]{2,1,0:T(8,128)} custom-call(f32[4,8,64]{2,1,0:T(8,128)S(1)} %copy-done.4, f32[4,72,128]{2,1,0:T(8,128)S(1)} %bitcast.2, f32[5,128,64]{2,1,0:T(8,128)S(1)} %copy-done.3), custom_call_target="tpu_custom_call" | custom-call | tf_op jit(solution)/shard_map/pallas_call | solution.py:513
  33.6 0.0 copy-start.10
  33.6 14.9 %all-to-all-start.1 = ((f32[32,8,128]{2,1,0:T(8,128)}), f32[32,8,128]{2,1,0:T(8,128)S(1)}, u32[]{:S(2)}, u32[]{:S(2)}) async-start(f32[32,8,128]{2,1,0:T(8,128)} %shard_map.110), calls=%async_computation.1 | async-start | bytes 262144 | tf_op jit(solution)/shard_map/all_to_all | solution.py:555
  48.4 4.6 %collective-permute-start = (f32[32,128]{1,0:T(8,128)S(1)}, f32[32,128]{1,0:T(8,128)S(1)}, u32[]{:S(2)}, u32[]{:S(2)}) collective-permute-start(f32[32,128]{1,0:T(8,128)S(1)} %get-tuple-element.36), channel_id=1, source_target_pairs={{0,4},{4,0},{8,12},{12,8},{16,20},{20,16},{24,28},{28,24},{32,36},... | collective-permute-start | bytes 49160 | tf_op jit(solution)/shard_map/ppermute | solution.py:562
  53.0 0.0 copy-done.10
  53.0 0.6 shard_map.111
  53.6 7.7 %collective-permute-start.1 = (f32[32,128]{1,0:T(8,128)S(1)}, f32[32,128]{1,0:T(8,128)S(1)}, u32[]{:S(2)}, u32[]{:S(2)}) collective-permute-start(f32[32,128]{1,0:T(8,128)S(1)} %get-tuple-element.37), channel_id=1, source_target_pairs={{0,124},{4,8},{8,4},{12,16},{16,12},{20,24},{24,20},{28,32},{32,28... | collective-permute-start | bytes 49160 | tf_op jit(solution)/shard_map/ppermute | solution.py:561
  61.3 0.0 all-to-all-done.1.arrived
  61.3 0.4 shard_map.112
  61.7 0.0 collective-permute-done.swapped_a
  61.7 1.8 %collective-permute-done.1.swapped_b = f32[32,128]{1,0:T(8,128)S(1)} collective-permute-done((f32[32,128]{1,0:T(8,128)S(1)}, f32[32,128]{1,0:T(8,128)S(1)}, u32[]{:S(2)}, u32[]{:S(2)}) %collective-permute-start.1) | collective-permute-done | bytes 16416 | tf_op jit(solution)/shard_map/ppermute | solution.py:561
  63.5 0.0 copy-start.2
  63.5 0.4 shard_map.113
  63.8 5.5 %all-gather.1 = f32[288,128]{1,0:T(8,128)S(1)} all-gather(f32[72,128]{1,0:T(8,128)S(1)} %get-tuple-element.40), channel_id=3, replica_groups=mesh['face'=8,'tx'=32,'ty'=4] {'ty'}, dimensions={0}, use_global_device_ids=true | all-gather | bytes 184320 | tf_op jit(solution)/shard_map/all_gather | solution.py:551
  69.3 0.0 copy-done.2
  69.3 1.4 %shard_map.114 = f32[32,8,128]{2,1,0:T(8,128)} custom-call(f32[4,8,64]{2,1,0:T(8,128)S(1)} %copy-done.4, f32[4,72,128]{2,1,0:T(8,128)S(1)} %bitcast.4, f32[5,128,64]{2,1,0:T(8,128)S(1)} %copy-done.2), custom_call_target="tpu_custom_call" | custom-call | tf_op jit(solution)/shard_map/pallas_call | solution.py:513
  70.7 0.0 copy-start.9
  70.7 9.1 %all-to-all-start.2 = ((f32[32,8,128]{2,1,0:T(8,128)}), f32[32,8,128]{2,1,0:T(8,128)S(1)}, u32[]{:S(2)}, u32[]{:S(2)}) async-start(f32[32,8,128]{2,1,0:T(8,128)} %shard_map.114), calls=%async_computation.2 | async-start | bytes 262144 | tf_op jit(solution)/shard_map/all_to_all | solution.py:555
  79.8 4.6 %collective-permute-start.2 = (f32[32,128]{1,0:T(8,128)S(1)}, f32[32,128]{1,0:T(8,128)S(1)}, u32[]{:S(2)}, u32[]{:S(2)}) collective-permute-start(f32[32,128]{1,0:T(8,128)S(1)} %get-tuple-element.46), channel_id=1, source_target_pairs={{0,4},{4,0},{8,12},{12,8},{16,20},{20,16},{24,28},{28,24},{32,36},... | collective-permute-start | bytes 49160 | tf_op jit(solution)/shard_map/ppermute | solution.py:562
  84.4 0.0 copy-done.9
  84.4 0.6 shard_map.115
  85.0 7.7 %collective-permute-start.3 = (f32[32,128]{1,0:T(8,128)S(1)}, f32[32,128]{1,0:T(8,128)S(1)}, u32[]{:S(2)}, u32[]{:S(2)}) collective-permute-start(f32[32,128]{1,0:T(8,128)S(1)} %get-tuple-element.47), channel_id=1, source_target_pairs={{0,124},{4,8},{8,4},{12,16},{16,12},{20,24},{24,20},{28,32},{32,28... | collective-permute-start | bytes 49160 | tf_op jit(solution)/shard_map/ppermute | solution.py:561
  92.7 0.0 all-to-all-done.2.arrived
  92.7 0.4 shard_map.116
  93.1 0.0 collective-permute-done.2.swapped_a
  93.1 1.8 %collective-permute-done.3.swapped_b = f32[32,128]{1,0:T(8,128)S(1)} collective-permute-done((f32[32,128]{1,0:T(8,128)S(1)}, f32[32,128]{1,0:T(8,128)S(1)}, u32[]{:S(2)}, u32[]{:S(2)}) %collective-permute-start.3) | collective-permute-done | bytes 16416 | tf_op jit(solution)/shard_map/ppermute | solution.py:561
  94.9 0.2 shard_map.117
  95.1 12.2 %all_to_all.21.loads = f32[8,48,128]{2,1,0:T(8,128)S(1)} all-to-all(f32[8,48,128]{2,1,0:T(8,128)S(1)} %get-tuple-element.50), channel_id=1, replica_groups=mesh['face'=8,'tx'=32,'ty'=4] {'face'}, dimensions={0} | all-to-all | bytes 393216 | tf_op jit(solution)/shard_map/all_to_all | solution.py:592
  107.3 0.8 shard_map.118
Async XLA Ops:
  0.0 20.0 %copy-start.8 = (f32[4,1,6,8,64]{4,3,2,1,0:T(8,128)S(1)}, f32[4,1,6,8,64]{4,3,2,1,0:T(8,128)}, u32[]{:S(2)}) copy-start(f32[4,1,6,8,64]{4,3,2,1,0:T(8,128)} %misfit.1) | copy-start | bytes 147460
  1.8 18.2 %copy-start = (f32[2,4,1,6,8,64]{5,4,3,2,1,0:T(8,128)S(1)}, f32[2,4,1,6,8,64]{5,4,3,2,1,0:T(8,128)}, u32[]{:S(2)}) copy-start(f32[2,4,1,6,8,64]{5,4,3,2,1,0:T(8,128)} %probes.7) | copy-start | bytes 294916
  1.8 18.2 %copy-start.1 = (f32[4,1,6,8,64]{4,3,2,1,0:T(8,128)S(1)}, f32[4,1,6,8,64]{4,3,2,1,0:T(8,128)}, u32[]{:S(2)}) copy-start(f32[4,1,6,8,64]{4,3,2,1,0:T(8,128)} %spread.7) | copy-start | bytes 147460
  1.8 18.2 %copy-start.5 = (f32[2,1,6,8,64]{4,3,2,1,0:T(8,128)S(1)}, f32[2,1,6,8,64]{4,3,2,1,0:T(8,128)}, u32[]{:S(2)}) copy-start(f32[2,1,6,8,64]{4,3,2,1,0:T(8,128)} %wind.5) | copy-start | bytes 73732
  1.8 18.2 %copy-start.6 = (f32[1,6,8,64]{3,2,1,0:T(8,128)S(1)}, f32[1,6,8,64]{3,2,1,0:T(8,128)}, u32[]{:S(2)}) copy-start(f32[1,6,8,64]{3,2,1,0:T(8,128)} %mass.3) | copy-start | bytes 36868
  1.8 18.2 %copy-start.7 = (f32[1,6,8,64]{3,2,1,0:T(8,128)S(1)}, f32[1,6,8,64]{3,2,1,0:T(8,128)}, u32[]{:S(2)}) copy-start(f32[1,6,8,64]{3,2,1,0:T(8,128)} %heat.3) | copy-start | bytes 36868
  20.0 12.1 %copy-start.3 = (f32[5,128,64]{2,1,0:T(8,128)S(1)}, f32[5,128,64]{2,1,0:T(8,128)}, u32[]{:S(2)}) copy-start(f32[5,128,64]{2,1,0:T(8,128)} %constant.8.clone.codes) | copy-start | bytes 491524
  20.3 11.9 %copy-start.4 = (f32[4,8,64]{2,1,0:T(8,128)S(1)}, f32[4,8,64]{2,1,0:T(8,128)}, u32[]{:S(2)}) copy-start(f32[4,8,64]{2,1,0:T(8,128)} %get-tuple-element.28.table.links) | copy-start | bytes 24580
  33.6 19.5 %copy-start.10 = (f32[128,64]{1,0:T(8,128)S(1)}, f32[128,64]{1,0:T(8,128)}, u32[]{:S(2)}) copy-start(f32[128,64]{1,0:T(8,128)} %constant.9.clone.picks) | copy-start | bytes 98308
  33.6 27.7 %all-to-all-start.1 = ((f32[32,8,128]{2,1,0:T(8,128)}), f32[32,8,128]{2,1,0:T(8,128)S(1)}, u32[]{:S(2)}, u32[]{:S(2)}) async-start(f32[32,8,128]{2,1,0:T(8,128)} %shard_map.110), calls=%async_computation.1 | async-start | bytes 262144 | tf_op jit(solution)/shard_map/all_to_all | solution.py:555
  48.4 13.2 %collective-permute-start = (f32[32,128]{1,0:T(8,128)S(1)}, f32[32,128]{1,0:T(8,128)S(1)}, u32[]{:S(2)}, u32[]{:S(2)}) collective-permute-start(f32[32,128]{1,0:T(8,128)S(1)} %get-tuple-element.36), channel_id=1, source_target_pairs={{0,4},{4,0},{8,12},{12,8},{16,20},{20,16},{24,28},{28,24},{32,36},... | collective-permute-start | bytes 49160 | tf_op jit(solution)/shard_map/ppermute | solution.py:562
  53.6 9.9 %collective-permute-start.1 = (f32[32,128]{1,0:T(8,128)S(1)}, f32[32,128]{1,0:T(8,128)S(1)}, u32[]{:S(2)}, u32[]{:S(2)}) collective-permute-start(f32[32,128]{1,0:T(8,128)S(1)} %get-tuple-element.37), channel_id=1, source_target_pairs={{0,124},{4,8},{8,4},{12,16},{16,12},{20,24},{24,20},{28,32},{32,28... | collective-permute-start | bytes 49160 | tf_op jit(solution)/shard_map/ppermute | solution.py:561
  63.5 5.8 %copy-start.2 = (f32[5,128,64]{2,1,0:T(8,128)S(1)}, f32[5,128,64]{2,1,0:T(8,128)}, u32[]{:S(2)}) copy-start(f32[5,128,64]{2,1,0:T(8,128)} %constant.10.clone.codes) | copy-start | bytes 491524
  70.7 13.7 %copy-start.9 = (f32[128,64]{1,0:T(8,128)S(1)}, f32[128,64]{1,0:T(8,128)}, u32[]{:S(2)}) copy-start(f32[128,64]{1,0:T(8,128)} %constant.11.clone.picks) | copy-start | bytes 98308
  70.7 22.0 %all-to-all-start.2 = ((f32[32,8,128]{2,1,0:T(8,128)}), f32[32,8,128]{2,1,0:T(8,128)S(1)}, u32[]{:S(2)}, u32[]{:S(2)}) async-start(f32[32,8,128]{2,1,0:T(8,128)} %shard_map.114), calls=%async_computation.2 | async-start | bytes 262144 | tf_op jit(solution)/shard_map/all_to_all | solution.py:555
  79.8 13.2 %collective-permute-start.2 = (f32[32,128]{1,0:T(8,128)S(1)}, f32[32,128]{1,0:T(8,128)S(1)}, u32[]{:S(2)}, u32[]{:S(2)}) collective-permute-start(f32[32,128]{1,0:T(8,128)S(1)} %get-tuple-element.46), channel_id=1, source_target_pairs={{0,4},{4,0},{8,12},{12,8},{16,20},{20,16},{24,28},{28,24},{32,36},... | collective-permute-start | bytes 49160 | tf_op jit(solution)/shard_map/ppermute | solution.py:562
  85.0 9.9 %collective-permute-start.3 = (f32[32,128]{1,0:T(8,128)S(1)}, f32[32,128]{1,0:T(8,128)S(1)}, u32[]{:S(2)}, u32[]{:S(2)}) collective-permute-start(f32[32,128]{1,0:T(8,128)S(1)} %get-tuple-element.47), channel_id=1, source_target_pairs={{0,124},{4,8},{8,4},{12,16},{16,12},{20,24},{24,20},{28,32},{32,28... | collective-permute-start | bytes 49160 | tf_op jit(solution)/shard_map/ppermute | solution.py:561
